TPU v7x, 8 devices: a whole 2x2x1 slice. The times are simulated.
8 devices in a mesh: fsdp: 8 (over z, y, x, core).
Axes of the slice: x: 2, y: 2, z: 1, core: 2. Of those that a mesh axis runs over, the one named last changes fastest.
Arguments:
- act_in: bfloat16 [192, 196, 768], P('fsdp')
- labels: int32 [192], P('fsdp')
- layer_p: float32 [2, 4877312], P(None, 'fsdp')
- head_w: float32 [768, 1000], P('fsdp')
- small_p: float32 [3072], P('fsdp')
- layer_m: float32 [2, 4877312], P(None, 'fsdp')
- head_m: float32 [768, 1000], P('fsdp')
- small_m: float32 [3072], P('fsdp')
- layer_v: float32 [2, 4877312], P(None, 'fsdp')
- head_v: float32 [768, 1000], P('fsdp')
- small_v: float32 [3072], P('fsdp')
Outputs:
- output 1: float32 [], replicated
- output 2: float32 [2, 4877312], P(None, 'fsdp')
- output 3: float32 [768, 1000], P('fsdp')
- output 4: float32 [3072], P('fsdp')
- output 5: float32 [2, 4877312], P(None, 'fsdp')
- output 6: float32 [768, 1000], P('fsdp')
- output 7: float32 [3072], P('fsdp')
- output 8: float32 [2, 4877312], P(None, 'fsdp')
- output 9: float32 [768, 1000], P('fsdp')
- output 10: float32 [3072], P('fsdp')
All inputs are finite; a program needn't handle non-finite values.
Results may differ from a plain program's by a relative error of at most 0.001.
Values are sent between devices in bfloat16 or wider.
A program may use at most 1 GiB of HBM per device.

v0:
```python
import math
import jax
import jax.numpy as jnp
from jax import lax
from jax.sharding import PartitionSpec as P

LN_EPS = 1e-6
LEARN_RATE = 0.003
BETA_ONE = 0.9
BETA_TWO = 0.999
ADAM_EPS = 1e-8
WEIGHT_DECAY = 0.03
ADAM_STEP = 10


def piece_shapes(num_tokens, num_chans):
    tok_hid = num_chans // 2
    ch_hid = 4 * num_chans
    return [(num_tokens, tok_hid), (tok_hid, num_tokens), (num_chans, ch_hid), (ch_hid, num_chans), (num_chans,), (num_chans,), (tok_hid,), (num_tokens,), (num_chans,), (num_chans,), (ch_hid,), (num_chans,)]


def layer_length(num_tokens, num_chans):
    return sum(math.prod(shape_one) for shape_one in piece_shapes(num_tokens, num_chans))


def unpack_layer(flat, num_tokens, num_chans):
    pieces = []
    piece_start = 0
    for shape_one in piece_shapes(num_tokens, num_chans):
        piece_len = math.prod(shape_one)
        pieces.append(flat[piece_start:piece_start + piece_len].reshape(shape_one))
        piece_start = piece_start + piece_len
    return pieces


def layer_norm(x_in, ln_gain, ln_shift):
    x_f = x_in.astype(jnp.float32)
    mean_val = jnp.mean(x_f, axis=-1, keepdims=True)
    var_val = jnp.mean(jnp.square(x_f - mean_val), axis=-1, keepdims=True)
    normed = (x_f - mean_val) * lax.rsqrt(var_val + LN_EPS)
    return (normed * ln_gain.astype(jnp.float32) + ln_shift.astype(jnp.float32)).astype(jnp.bfloat16)


def gelu_bf16(hidden):
    return jax.nn.gelu(hidden).astype(jnp.bfloat16)


def gelu_grad(hidden, d_act):
    _, pullback = jax.vjp(gelu_bf16, hidden)
    return pullback(d_act.astype(jnp.bfloat16))[0]


def norm_grad(x_in, ln_gain, ln_shift, d_normed):
    _, pullback = jax.vjp(layer_norm, x_in, ln_gain.astype(jnp.float32), ln_shift.astype(jnp.float32))
    d_x, d_gain, d_shift = pullback(d_normed.astype(jnp.bfloat16))
    return d_x.astype(jnp.float32), d_gain, d_shift


def layer_forward(x_in, flat, num_tokens, num_chans):
    w_tok1, w_tok2, w_ch1, w_ch2, ln1_g, ln1_b, b_tok1, b_tok2, ln2_g, ln2_b, b_ch1, b_ch2 = unpack_layer(flat, num_tokens, num_chans)
    normed = layer_norm(x_in, ln1_g, ln1_b)
    hid_tok = jnp.einsum('bsc,sj->bcj', normed, w_tok1, preferred_element_type=jnp.float32) + b_tok1.astype(jnp.float32)
    act_tok = gelu_bf16(hid_tok)
    tok_out = jnp.einsum('bcj,js->bsc', act_tok, w_tok2, preferred_element_type=jnp.float32) + b_tok2.astype(jnp.float32)[:, None]
    after_tok = (x_in.astype(jnp.float32) + tok_out).astype(jnp.bfloat16)
    normed2 = layer_norm(after_tok, ln2_g, ln2_b)
    hid_ch = jnp.einsum('bsc,cd->bsd', normed2, w_ch1, preferred_element_type=jnp.float32) + b_ch1.astype(jnp.float32)
    act_ch = gelu_bf16(hid_ch)
    ch_out = jnp.einsum('bsd,dc->bsc', act_ch, w_ch2, preferred_element_type=jnp.float32) + b_ch2.astype(jnp.float32)
    layer_out = (after_tok.astype(jnp.float32) + ch_out).astype(jnp.bfloat16)
    return layer_out, (x_in, normed, hid_tok, act_tok, after_tok, normed2, hid_ch, act_ch)


def layer_backward(d_out, flat, cache, num_tokens, num_chans):
    w_tok1, w_tok2, w_ch1, w_ch2, ln1_g, ln1_b, b_tok1, b_tok2, ln2_g, ln2_b, b_ch1, b_ch2 = unpack_layer(flat, num_tokens, num_chans)
    x_in, normed, hid_tok, act_tok, after_tok, normed2, hid_ch, act_ch = cache
    d_out_bf = d_out.astype(jnp.bfloat16)
    g_b_ch2 = jnp.sum(d_out, axis=(0, 1))
    g_w_ch2 = jnp.einsum('bsd,bsc->dc', act_ch, d_out_bf, preferred_element_type=jnp.float32)
    d_act_ch = jnp.einsum('bsc,dc->bsd', d_out_bf, w_ch2, preferred_element_type=jnp.float32)
    d_hid_ch = gelu_grad(hid_ch, d_act_ch)
    d_hid_ch_bf = d_hid_ch.astype(jnp.bfloat16)
    g_b_ch1 = jnp.sum(d_hid_ch, axis=(0, 1))
    g_w_ch1 = jnp.einsum('bsc,bsd->cd', normed2, d_hid_ch_bf, preferred_element_type=jnp.float32)
    d_normed2 = jnp.einsum('bsd,cd->bsc', d_hid_ch_bf, w_ch1, preferred_element_type=jnp.float32)
    d_after_ln, g_ln2_g, g_ln2_b = norm_grad(after_tok, ln2_g, ln2_b, d_normed2)
    d_after = d_after_ln + d_out
    d_after_bf = d_after.astype(jnp.bfloat16)
    g_b_tok2 = jnp.sum(d_after, axis=(0, 2))
    g_w_tok2 = jnp.einsum('bcj,bsc->js', act_tok, d_after_bf, preferred_element_type=jnp.float32)
    d_act_tok = jnp.einsum('bsc,js->bcj', d_after_bf, w_tok2, preferred_element_type=jnp.float32)
    d_hid_tok = gelu_grad(hid_tok, d_act_tok)
    d_hid_tok_bf = d_hid_tok.astype(jnp.bfloat16)
    g_b_tok1 = jnp.sum(d_hid_tok, axis=(0, 1))
    g_w_tok1 = jnp.einsum('bsc,bcj->sj', normed, d_hid_tok_bf, preferred_element_type=jnp.float32)
    d_normed = jnp.einsum('bcj,sj->bsc', d_hid_tok_bf, w_tok1, preferred_element_type=jnp.float32)
    d_in_ln, g_ln1_g, g_ln1_b = norm_grad(x_in, ln1_g, ln1_b, d_normed)
    d_in = d_in_ln + d_after
    pad_len = flat.shape[0] - layer_length(num_tokens, num_chans)
    flat_grad = jnp.concatenate([g_w_tok1.reshape(-1), g_w_tok2.reshape(-1), g_w_ch1.reshape(-1), g_w_ch2.reshape(-1), g_ln1_g, g_ln1_b, g_b_tok1, g_b_tok2, g_ln2_g, g_ln2_b, g_b_ch1, g_b_ch2, jnp.zeros((pad_len,), jnp.float32)])
    return d_in, flat_grad


def head_step(hidden, labels, small_full, head_full, global_b):
    num_tokens = hidden.shape[1]
    num_chans = hidden.shape[2]
    num_classes = head_full.shape[1]
    lnf_g = small_full[:num_chans]
    lnf_b = small_full[num_chans:2 * num_chans]
    head_b = small_full[2 * num_chans:2 * num_chans + num_classes]
    normed = layer_norm(hidden, lnf_g, lnf_b)
    pooled = (jnp.sum(normed, axis=1, dtype=jnp.float32) / num_tokens).astype(jnp.bfloat16)
    logits = jnp.dot(pooled, head_full, preferred_element_type=jnp.float32) + head_b.astype(jnp.float32)
    log_norm = jax.nn.logsumexp(logits, axis=-1)
    is_label = jnp.arange(num_classes)[None, :] == labels[:, None]
    picked = jnp.sum(jnp.where(is_label, logits, 0.0), axis=-1)
    loss_sum = jnp.sum(log_norm - picked)
    d_logits = (jnp.exp(logits - log_norm[:, None]) - is_label.astype(jnp.float32)) / global_b
    d_logits_bf = d_logits.astype(jnp.bfloat16)
    g_head_b = jnp.sum(d_logits, axis=0)
    g_head_w = jnp.einsum('bc,bk->ck', pooled, d_logits_bf, preferred_element_type=jnp.float32)
    d_pooled = jnp.einsum('bk,ck->bc', d_logits_bf, head_full, preferred_element_type=jnp.float32)
    d_normed = jnp.broadcast_to((d_pooled / num_tokens)[:, None, :], normed.shape)
    d_hidden, g_lnf_g, g_lnf_b = norm_grad(hidden, lnf_g, lnf_b, d_normed)
    g_small = jnp.concatenate([g_lnf_g, g_lnf_b, g_head_b])
    return loss_sum, d_hidden, g_head_w, g_small


def adam_update(master, gradient, moment, second, decay_rate):
    moment_new = BETA_ONE * moment + (1.0 - BETA_ONE) * gradient
    second_new = BETA_TWO * second + (1.0 - BETA_TWO) * gradient * gradient
    m_hat = moment_new / (1.0 - BETA_ONE ** ADAM_STEP)
    v_hat = second_new / (1.0 - BETA_TWO ** ADAM_STEP)
    master_new = master - LEARN_RATE * (m_hat / (jnp.sqrt(v_hat) + ADAM_EPS) + decay_rate * master)
    return master_new, moment_new, second_new


def solution(mesh):
    group = mesh.shape['fsdp']
    row_spec = P('fsdp')
    layer_spec = P(None, 'fsdp')
    in_specs = (row_spec, row_spec, layer_spec, row_spec, row_spec, layer_spec, row_spec, row_spec, layer_spec, row_spec, row_spec)
    out_specs = (P(),) + in_specs[2:]

    def device_step(act_in, labels, layer_p, head_w, small_p, layer_m, head_m, small_m, layer_v, head_v, small_v):
        local_b, num_tokens, num_chans = act_in.shape
        global_b = local_b * group
        num_layers = layer_p.shape[0]
        mat_len = 2 * num_tokens * (num_chans // 2) + 8 * num_chans * num_chans
        caches = []
        hidden = act_in
        for layer_idx in range(num_layers):
            flat_full = lax.all_gather(layer_p[layer_idx].astype(jnp.bfloat16), 'fsdp', tiled=True)
            hidden, cache = layer_forward(hidden, flat_full, num_tokens, num_chans)
            caches.append(cache)
        small_full = lax.all_gather(small_p.astype(jnp.bfloat16), 'fsdp', tiled=True)
        head_full = lax.all_gather(head_w.astype(jnp.bfloat16), 'fsdp', tiled=True)
        loss_sum, d_hidden, g_head_w, g_small = head_step(hidden, labels, small_full, head_full, global_b)
        layer_shards = [None] * num_layers
        for layer_idx in reversed(range(num_layers)):
            flat_full = lax.all_gather(layer_p[layer_idx].astype(jnp.bfloat16), 'fsdp', tiled=True)
            d_hidden, flat_grad = layer_backward(d_hidden, flat_full, caches[layer_idx], num_tokens, num_chans)
            layer_shards[layer_idx] = lax.psum_scatter(flat_grad, 'fsdp', scatter_dimension=0, tiled=True)
        layer_g = jnp.stack(layer_shards)
        head_g = lax.psum_scatter(g_head_w, 'fsdp', scatter_dimension=0, tiled=True)
        small_flat = jnp.concatenate([g_small, jnp.zeros((small_full.shape[0] - g_small.shape[0],), jnp.float32)])
        small_g = lax.psum_scatter(small_flat, 'fsdp', scatter_dimension=0, tiled=True)
        loss_value = lax.psum(loss_sum, 'fsdp') / global_b
        sq_local = jnp.sum(jnp.square(layer_g)) + jnp.sum(jnp.square(head_g)) + jnp.sum(jnp.square(small_g))
        grad_norm = jnp.sqrt(lax.psum(sq_local, 'fsdp'))
        clip_scale = 1.0 / jnp.maximum(1.0, grad_norm)
        shard_len = layer_p.shape[1]
        flat_pos = lax.axis_index('fsdp') * shard_len + jnp.arange(shard_len)
        layer_decay = jnp.where(flat_pos < mat_len, WEIGHT_DECAY, 0.0)[None, :]
        new_lp, new_lm, new_lv = adam_update(layer_p, layer_g * clip_scale, layer_m, layer_v, layer_decay)
        new_hw, new_hm, new_hv = adam_update(head_w, head_g * clip_scale, head_m, head_v, WEIGHT_DECAY)
        new_sp, new_sm, new_sv = adam_update(small_p, small_g * clip_scale, small_m, small_v, 0.0)
        return (loss_value, new_lp, new_hw, new_sp, new_lm, new_hm, new_sm, new_lv, new_hv, new_sv)

    return jax.shard_map(device_step, mesh=mesh, in_specs=in_specs, out_specs=out_specs, check_vma=False)
```

profile of v0, /device:TPU:0, one launch (start us, length us, event | category | flops | bytes accessed | tf_op | source)
XLA Modules:
  0.0 2088.1 jit_solution(299793039340765531)
XLA Ops:
  45.9 69.8 %all-gather.9.cloned.1.call-done = bf16[1,4877312]{1,0:T(2,128)(2,1)} async-done(((bf16[1,609664]{1,0:T(2,128)(2,1)}), bf16[1,4877312]{1,0:T(2,128)(2,1)}) %all-gather.9.cloned.1.call-update) | async-done | bytes 9754640 | tf_op jit(solution)/shard_map/all_gather | solution.py:153
  120.8 23.1 %multiply_convert_fusion.3 = (bf16[24,768,384]{2,1,0:T(8,128)(2,1)}, f32[24,768,384]{2,1,0:T(8,128)}) fusion(f32[384]{0:T(512)S(1)} %fusion.215, bf16[196,384,1]{1,0,2:T(8,128)(2,1)S(1)} %reshape.338, f32[768]{0:T(1024)S(1)} %get-tuple-element.22, f32[768]{0:T(1024)S(1)} %get-tuple-element.23, f32[24,196]{1,0:T(8,128)S(1)} %add_rsqrt_fusion, ...), kind=kOutput, calls=%fused_computation.55 | convolution fusion | flops 2866987008 | bytes 49888512 | tf_op jit(solution)/shard_map/bsc,sj->bcj/dot_general | solution.py:62
  163.6 105.0 %slice_reduce_fusion.2 = (bf16[2359296]{0:T(1024)(128)(2,1)}, bf16[2359296]{0:T(1024)(128)(2,1)}) fusion(bf16[1,4877312]{1,0:T(2,128)(2,1)} %all-gather.9.cloned.1.call-done), kind=kLoop, calls=%fused_computation.178 | loop fusion | bytes 18874368 | tf_op jit(solution)/shard_map/slice | solution.py:31
  287.1 46.0 %multiply_convert_fusion.1 = (bf16[24,196,3072]{2,1,0:T(8,128)(2,1)}, f32[24,196,3072]{2,1,0:T(8,128)}) fusion(f32[3072]{0:T(1024)S(1)} %bitcast.125, bf16[768,3072,1]{1,0,2:T(8,128)(2,1)} %reshape.340, bf16[24,196,768]{2,1,0:T(8,128)(2,1)} %get-tuple-element.71, f32[768]{0:T(1024)S(1)} %get-tuple-element.20, f32[768]{0:T(1024)S(1)} %get-tuple-element.21, ...), kind=kOutput, calls=%fused_computation.27 | convolution fusion | flops 22362439680 | bytes 98704128 | tf_op jit(solution)/shard_map/bsc,cd->bsd/dot_general | solution.py:67
  333.2 29.5 %convert_reduce_fusion.3 = (f32[24,196]{1,0:T(8,128)S(1)}, bf16[24,196,768]{2,1,0:T(8,128)(2,1)S(1)}) fusion(f32[768]{0:T(1024)S(1)} %get-tuple-element.19, bf16[24,196,3072]{2,1,0:T(8,128)(2,1)} %get-tuple-element.72, bf16[3072,768,1]{1,0,2:T(8,128)(2,1)} %reshape.341, bf16[24,196,768]{2,1,0:T(8,128)(2,1)S(1)} %bitcast.116), kind=kOutput, calls=%fused_computation.71 | convolution fusion | flops 22217928704 | bytes 48092544 | tf_op jit(solution)/shard_map/bsd,dc->bsc/dot_general | solution.py:69
  415.3 104.5 %slice_reduce_fusion = (bf16[2359296]{0:T(1024)(128)(2,1)}, bf16[2359296]{0:T(1024)(128)(2,1)}) fusion(bf16[1,4877312]{1,0:T(2,128)(2,1)} %all-gather.11.cloned.1.call-done), kind=kLoop, calls=%fused_computation.176 | loop fusion | bytes 18874368 | tf_op jit(solution)/shard_map/slice | solution.py:31
  538.2 46.1 %multiply_convert_fusion = (bf16[24,196,3072]{2,1,0:T(8,128)(2,1)}, f32[24,196,3072]{2,1,0:T(8,128)}) fusion(f32[3072]{0:T(1024)S(1)} %bitcast.127, bf16[768,3072,1]{1,0,2:T(8,128)(2,1)} %reshape.344, bf16[24,196,768]{2,1,0:T(8,128)(2,1)} %get-tuple-element.79, f32[768]{0:T(1024)S(1)} %get-tuple-element.11, f32[768]{0:T(1024)S(1)} %get-tuple-element.12, ...), kind=kOutput, calls=%fused_computation.26 | convolution fusion | flops 22362439680 | bytes 98704128 | tf_op jit(solution)/shard_map/bsc,cd->bsd/dot_general | solution.py:67
  584.4 29.5 %convert_reduce_fusion.9 = (f32[24,196]{1,0:T(8,128)S(1)}, bf16[24,196,768]{2,1,0:T(8,128)(2,1)S(1)}) fusion(f32[768]{0:T(1024)S(1)} %get-tuple-element.10, bf16[24,196,3072]{2,1,0:T(8,128)(2,1)} %get-tuple-element.80, bf16[3072,768,1]{1,0,2:T(8,128)(2,1)} %reshape.345, bf16[24,196,768]{2,1,0:T(8,128)(2,1)S(1)} %bitcast.120), kind=kOutput, calls=%fused_computation.99 | convolution fusion | flops 22217928704 | bytes 48092544 | tf_op jit(solution)/shard_map/bsd,dc->bsc/dot_general | solution.py:69
  639.1 65.7 %fusion.235 = (f32[3072]{0:T(1024)}, bf16[24,196,3072]{2,1,0:T(8,128)(2,1)}) fusion(f32[24,196,3072]{2,1,0:T(8,128)} %get-tuple-element.81, f32[3072]{0:T(1024)S(1)} %bitcast.128, bf16[3072,768,1]{1,0,2:T(8,128)(2,1)} %reshape.345, bf16[24,196,768]{2,1,0:T(8,128)(2,1)S(1)} %bitcast.112, f32[24,196]{1,0:T(8,128)S(1)} %add_multiply_fusion.3, ...), kind=kOutput, calls=%fused_computation.310 | convolution fusion | flops 22571970560 | bytes 98824704 | tf_op jit(solution)/shard_map/bsc,dc->bsd/dot_general | solution.py:80
  704.8 35.5 %fusion.111 = (f32[768]{0:T(1024)}, f32[24,196]{1,0:T(8,128)S(1)}, f32[24,196]{1,0:T(8,128)S(1)}, f32[768]{0:T(1024)}, bf16[24,196,768]{2,1,0:T(8,128)(2,1)}) fusion(bf16[24,196,768]{2,1,0:T(8,128)(2,1)} %get-tuple-element.79, f32[24,196]{1,0:T(8,128)S(1)} %copy-done.54, f32[24,196]{1,0:T(8,128)S(1)} %copy-done.28, f32[768]{0:T(1024)S(1)} %copy-done.69, ...), kind=kOutput, calls=%fused_computation.159 | convolution fusion | flops 22243213312 | bytes 48155136 | tf_op jit(solution)/shard_map/bsd,cd->bsc/dot_general | solution.py:85
  762.0 35.7 %fusion.234 = (f32[384]{0:T(512)}, bf16[24,768,384]{2,1,0:T(8,128)(2,1)}) fusion(f32[24,768,384]{2,1,0:T(8,128)} %get-tuple-element.77, f32[384]{0:T(512)S(1)} %copy-done.105, bf16[384,196]{1,0:T(8,128)(2,1)S(1)} %copy-done.39, bf16[24,196,768]{2,1,0:T(8,128)(2,1)S(1)} %get-tuple-element.65, f32[24,196]{1,0:T(8,128)S(1)} %add_multiply_fusion.3, ...), kind=kOutput, calls=%fused_computation.309 | convolution fusion | flops 2987752960 | bytes 57223680 | tf_op jit(solution)/shard_map/bsc,js->bcj/dot_general | solution.py:91
  833.2 33.1 %convolution_bitcast_fusion.1 = f32[3072,768]{1,0:T(8,128)} fusion(bf16[24,196,3072]{2,1,0:T(8,128)(2,1)} %get-tuple-element.72, f32[24,196,768]{2,1,0:T(8,128)} %convert_add_fusion.6), kind=kOutput, calls=%fused_computation.195 | convolution fusion | flops 22199869440 | bytes 52789248 | tf_op jit(solution)/shard_map/bsd,bsc->dc/dot_general | solution.py:79
  866.3 65.1 %fusion.237 = (f32[3072]{0:T(1024)}, bf16[24,196,3072]{2,1,0:T(8,128)(2,1)}) fusion(f32[24,196,3072]{2,1,0:T(8,128)} %get-tuple-element.73, f32[3072]{0:T(1024)S(1)} %bitcast.126, bf16[3072,768,1]{1,0,2:T(8,128)(2,1)} %reshape.341, f32[24,196,768]{2,1,0:T(8,128)} %convert_add_fusion.6), kind=kOutput, calls=%fused_computation.312 | convolution fusion | flops 22546681856 | bytes 105897984 | tf_op jit(solution)/shard_map/bsc,dc->bsd/dot_general | solution.py:80
  931.5 34.1 %fusion.162 = f32[96,24,8,128]{3,2,1,0:T(8,128)} fusion(bf16[24,196,3072]{2,1,0:T(8,128)(2,1)} %get-tuple-element.98, bf16[24,196,768]{2,1,0:T(8,128)(2,1)} %get-tuple-element.71, f32[768]{0:T(1024)S(1)} %copy-done.95, f32[768]{0:T(1024)S(1)} %copy-done.63, f32[24,196]{1,0:T(8,128)S(1)} %copy-done.52, f32[24,196]{1,0:T(8,128)S(1)} %copy-done.26), kind=kOutput, calls=%fused_computation.207 | convolution fusion | flops 22217932800 | bytes 45607680 | tf_op jit(solution)/shard_map/bsc,bsd->cd/dot_general | solution.py:84
  965.6 35.4 %fusion.112 = (f32[768]{0:T(1024)}, f32[24,196]{1,0:T(8,128)S(1)}, f32[24,196]{1,0:T(8,128)S(1)}, f32[768]{0:T(1024)}, bf16[24,196,768]{2,1,0:T(8,128)(2,1)}) fusion(bf16[24,196,768]{2,1,0:T(8,128)(2,1)} %get-tuple-element.71, f32[24,196]{1,0:T(8,128)S(1)} %copy-done.52, f32[24,196]{1,0:T(8,128)S(1)} %copy-done.26, f32[768]{0:T(1024)S(1)} %copy-done.63, ...), kind=kOutput, calls=%fused_computation.160 | convolution fusion | flops 22243213312 | bytes 48155136 | tf_op jit(solution)/shard_map/bsd,cd->bsc/dot_general | solution.py:85
  1001.1 36.9 %convolution_bitcast_fusion = f32[3072,768]{1,0:T(8,128)} fusion(bf16[24,196,3072]{2,1,0:T(8,128)(2,1)} %get-tuple-element.80, bf16[24,196,768]{2,1,0:T(8,128)(2,1)S(1)} %bitcast.114, f32[24,196]{1,0:T(8,128)S(1)} %copy-done.19, f32[24,196]{1,0:T(8,128)S(1)} %copy-done.17, f32[24,768]{1,0:T(8,128)S(1)} %copy-done.7, f32[768]{0:T(1024)S(1)} %copy-done.45, ...), kind=kOutput, calls=%fused_computation.194 | convolution fusion | flops 22225158144 | bytes 45715968 | tf_op jit(solution)/shard_map/bsd,bsc->dc/dot_general | solution.py:79
  1038.0 33.5 %fusion.157 = f32[96,24,8,128]{3,2,1,0:T(8,128)} fusion(bf16[24,196,3072]{2,1,0:T(8,128)(2,1)} %get-tuple-element.91, bf16[24,196,768]{2,1,0:T(8,128)(2,1)} %get-tuple-element.79, f32[768]{0:T(1024)S(1)} %copy-done.97, f32[768]{0:T(1024)S(1)} %copy-done.70, f32[24,196]{1,0:T(8,128)S(1)} %copy-done.55, f32[24,196]{1,0:T(8,128)S(1)} %copy-done.29), kind=kOutput, calls=%fused_computation.206 | convolution fusion | flops 22217932800 | bytes 45607680 | tf_op jit(solution)/shard_map/bsc,bsd->cd/dot_general | solution.py:84
  1134.0 35.0 %fusion.236 = (f32[384]{0:T(512)}, bf16[24,768,384]{2,1,0:T(8,128)(2,1)}) fusion(f32[24,768,384]{2,1,0:T(8,128)} %get-tuple-element.69, f32[384]{0:T(512)S(1)} %copy-done.103, bf16[384,196]{1,0:T(8,128)(2,1)S(1)} %copy-done.37, f32[24,196,768]{2,1,0:T(8,128)} %convert_add_fusion.6, bf16[24,196,768]{2,1,0:T(8,128)(2,1)} %get-tuple-element.64), kind=kOutput, calls=%fused_computation.311 | convolution fusion | flops 2955238912 | bytes 64296960 | tf_op jit(solution)/shard_map/bsc,js->bcj/dot_general | solution.py:91
  1233.4 154.0 %concatenate.9 = f32[4877312]{0:T(1024)} concatenate(f32[75264]{0:T(1024)S(1)} %reshape.274, f32[75264]{0:T(1024)S(1)} %copy-done.13, f32[2359296]{0:T(1024)} %bitcast.121, f32[2359296]{0:T(1024)} %reshape.277, f32[768]{0:T(1024)S(1)} %get-tuple-element.93, f32[768]{0:T(1024)S(1)} %convert_reduce_fusion.6, f32[384]{0:T(512)S(1)} %copy-done.99, f32[196]{0:T(256)S(1)} %copy-done.83, ...), dimensions={0} | concatenate | bytes 39018496 | tf_op jit(solution)/shard_map/concatenate | solution.py:100
  1391.6 153.1 %concatenate.10 = f32[4877312]{0:T(1024)} concatenate(f32[75264]{0:T(1024)S(1)} %reshape.278, f32[75264]{0:T(1024)S(1)} %reshape.279, f32[2359296]{0:T(1024)} %bitcast.122, f32[2359296]{0:T(1024)} %reshape.281, f32[768]{0:T(1024)S(1)} %copy-done.86, f32[768]{0:T(1024)S(1)} %convert_reduce_fusion.7, f32[384]{0:T(512)S(1)} %copy-done.98, f32[196]{0:T(256)S(1)} %copy-done.82, ...), dimensions={0} | concatenate | bytes 39018496 | tf_op jit(solution)/shard_map/concatenate | solution.py:100
  1546.0 23.0 %all-reduce.2 = f32[3072]{0:T(1024)S(1)} all-reduce(f32[3072]{0:T(1024)S(1)} %concatenate.11), channel_id=7, replica_groups=mesh['fsdp'=8] {'fsdp'}, use_global_device_ids=true, to_apply=%region_52.53.clone | all-reduce | flops 3072 | bytes 24576
  1571.9 420.7 %all-reduce.7.cloned.1.call-done = (f32[4877312]{0:T(1024)}, f32[4877312]{0:T(1024)}) async-done(((f32[4877312]{0:T(1024)}, f32[4877312]{0:T(1024)}), (f32[4877312]{0:T(1024)}, f32[4877312]{0:T(1024)})) %all-reduce.7.cloned.1.call-update) | async-done | bytes 39018512
  2031.1 22.6 %all-reduce.3 = (f32[]{:T(128)}, f32[]{:T(128)}) all-reduce(f32[]{:T(128)} %subtract_reduce_fusion, f32[]{:T(128)S(6)} %add.360), channel_id=1, replica_groups=mesh['fsdp'=8] {'fsdp'}, use_global_device_ids=true, to_apply=%region_15.16 | all-reduce | flops 2 | bytes 16 | tf_op jit(solution)/shard_map/psum | solution.py:168
  2055.8 23.2 %multiply_subtract_fusion = (f32[2,609664]{1,0:T(2,128)}, f32[2,609664]{1,0:T(2,128)}, f32[2,609664]{1,0:T(2,128)}) fusion(f32[2,609664]{1,0:T(2,128)} %param.13, f32[609664]{0:T(1024)} %fusion.173, f32[]{:T(128)S(6)} %div.166, f32[1,609664]{1,0:T(1,128)S(1)} %stack.10, f32[1,609664]{1,0:T(1,128)} %copy-done.3, f32[2,609664]{1,0:T(2,128)} %param.16, ...), kind=kLoop, calls=%fused_computation.198 | loop fusion | flops 20728576 | bytes 36579844 | tf_op jit(solution)/shard_map/sub | solution.py:134
  (359 shorter events, 407.9 us)
Async XLA Ops:
  7.2 108.5 %all-gather.9.cloned.1.call-start = ((), (), s32[]{:S(2)}) async-start(), calls=%async_computation.3 | async-start | bytes 21947904 | tf_op jit(solution)/shard_map/all_gather | solution.py:153
  16.9 352.5 %all-gather.11.cloned.1.call-start = ((), (), s32[]{:S(2)}) async-start(), calls=%async_computation.4 | async-start | bytes 21947904 | tf_op jit(solution)/shard_map/all_gather | solution.py:153
  17.6 603.0 %all-gather.7.cloned.1.call-start = ((), (), s32[]{:S(2)}) async-start(), calls=%async_computation.1 | async-start | bytes 1769472 | tf_op jit(solution)/shard_map/all_gather | solution.py:157
  18.4 1551.8 %reduce-scatter.2.cloned.1.call-start = ((), (), s32[]{:S(2)}) async-start(), calls=%async_computation.2 | async-start | bytes 3538944 | tf_op jit(solution)/shard_map/reduce_scatter | solution.py:165
  120.1 167.0 %copy-start.62 = (f32[768]{0:T(1024)}, f32[768]{0:T(1024)S(1)}, u32[]{:S(2)}) copy-start(f32[768]{0:T(1024)S(1)} %get-tuple-element.21) | copy-start | bytes 9220
  120.1 167.0 %copy-start.94 = (f32[768]{0:T(1024)}, f32[768]{0:T(1024)S(1)}, u32[]{:S(2)}) copy-start(f32[768]{0:T(1024)S(1)} %get-tuple-element.20) | copy-start | bytes 9220
  373.7 164.4 %copy-start.68 = (f32[768]{0:T(1024)}, f32[768]{0:T(1024)S(1)}, u32[]{:S(2)}) copy-start(f32[768]{0:T(1024)S(1)} %get-tuple-element.12) | copy-start | bytes 9220
  373.8 164.4 %copy-start.96 = (f32[768]{0:T(1024)}, f32[768]{0:T(1024)S(1)}, u32[]{:S(2)}) copy-start(f32[768]{0:T(1024)S(1)} %get-tuple-element.11) | copy-start | bytes 9220
  613.9 204.3 %copy-start.11 = (f32[24,196]{1,0:T(8,128)}, f32[24,196]{1,0:T(8,128)S(1)}, u32[]{:S(2)}) copy-start(f32[24,196]{1,0:T(8,128)S(1)} %broadcast_multiply_fusion) | copy-start | bytes 56452
  617.0 201.2 %copy-start.14 = (f32[24,196]{1,0:T(8,128)}, f32[24,196]{1,0:T(8,128)S(1)}, u32[]{:S(2)}) copy-start(f32[24,196]{1,0:T(8,128)S(1)} %fusion.199) | copy-start | bytes 56452
  627.1 191.1 %copy-start.6 = (f32[24,768]{1,0:T(8,128)}, f32[24,768]{1,0:T(8,128)S(1)}, u32[]{:S(2)}) copy-start(f32[24,768]{1,0:T(8,128)S(1)} %fusion.188) | copy-start | bytes 221188
  633.6 184.6 %copy-start.16 = (f32[24,196]{1,0:T(8,128)}, f32[24,196]{1,0:T(8,128)S(1)}, u32[]{:S(2)}) copy-start(f32[24,196]{1,0:T(8,128)S(1)} %multiply_multiply_fusion.15) | copy-start | bytes 56452
  639.0 179.2 %copy-start.18 = (f32[24,196]{1,0:T(8,128)}, f32[24,196]{1,0:T(8,128)S(1)}, u32[]{:S(2)}) copy-start(f32[24,196]{1,0:T(8,128)S(1)} %add_multiply_fusion.3) | copy-start | bytes 56452
  1080.9 911.7 %all-reduce.7.cloned.1.call-start = ((), (), s32[]{:S(2)}) async-start(), calls=%async_computation.5 | async-start | bytes 78036992
  1233.3 158.3 %copy-start.60 = (f32[768]{0:T(1024)S(1)}, f32[768]{0:T(1024)}, u32[]{:S(2)}) copy-start(f32[768]{0:T(1024)} %get-tuple-element.36) | copy-start | bytes 9220
  1233.3 158.2 %copy-start.72 = (f32[3072]{0:T(1024)S(1)}, f32[3072]{0:T(1024)}, u32[]{:S(2)}) copy-start(f32[3072]{0:T(1024)} %get-tuple-element.90) | copy-start | bytes 36868
  1233.3 158.2 %copy-start.82 = (f32[196]{0:T(256)S(1)}, f32[196]{0:T(256)}, u32[]{:S(2)}) copy-start(f32[196]{0:T(256)} %get-tuple-element.37) | copy-start | bytes 2356
  1233.3 158.2 %copy-start.84 = (f32[768]{0:T(1024)S(1)}, f32[768]{0:T(1024)}, u32[]{:S(2)}) copy-start(f32[768]{0:T(1024)} %get-tuple-element.32) | copy-start | bytes 9220
  1233.3 158.2 %copy-start.85 = (f32[768]{0:T(1024)S(1)}, f32[768]{0:T(1024)}, u32[]{:S(2)}) copy-start(f32[768]{0:T(1024)} %get-tuple-element.43) | copy-start | bytes 9220
  1233.4 158.2 %copy-start.86 = (f32[768]{0:T(1024)S(1)}, f32[768]{0:T(1024)}, u32[]{:S(2)}) copy-start(f32[768]{0:T(1024)} %get-tuple-element.31) | copy-start | bytes 9220
  1233.4 158.2 %copy-start.98 = (f32[384]{0:T(512)S(1)}, f32[384]{0:T(512)}, u32[]{:S(2)}) copy-start(f32[384]{0:T(512)} %get-tuple-element.88) | copy-start | bytes 4612
  1544.8 510.3 %copy-start.77 = (f32[384]{0:T(512)S(1)}, f32[384]{0:T(512)}, u32[]{:S(2)}) copy-start(f32[384]{0:T(512)} %param.15) | copy-start | bytes 4612
  1544.8 510.3 %copy-start.100 = (f32[384]{0:T(512)S(1)}, f32[384]{0:T(512)}, u32[]{:S(2)}) copy-start(f32[384]{0:T(512)} %param.18) | copy-start | bytes 4612
  1544.8 510.3 %copy-start.101 = (f32[384]{0:T(512)S(1)}, f32[384]{0:T(512)}, u32[]{:S(2)}) copy-start(f32[384]{0:T(512)} %param.21) | copy-start | bytes 4612
  (99 other events, 3297.5 us)
Sparse Core Ops, SparseCore 0:
  17.0 98.6 all-gather.8
  118.1 95.6 all-gather.10
  216.2 19.7 all-gather.6
  1081.0 37.4 reduce-scatter.1
  1544.9 447.6 all-reduce.6
where the time goes:
time: 2120 us; the launch traced here: 2090 us
  matrix products  707 us (33%)
  local copies, waits for them, and re-layouts  644 us (30%)
  waiting for transfers between devices  491 us (23%)
  other arithmetic  165 us (8%)
  blocking collectives  59.4 us (3%)
    unnamed x6, waiting for transfers between devices  421 us
    concatenate x2, local copies, waits for them, and re-layouts, layer_backward(): jnp.concatenate([g_w_tok1.reshape(-1), g_w_tok2.reshape(-1), g_w_ch1.resh...  307 us
    slice x4, local copies, waits for them, and re-layouts, unpack_layer(): pieces.append(flat[piece_start:piece_start + piece_len].reshape(shape_one))  215 us
    dot_general x2, matrix products, layer_backward(): jnp.einsum('bsc,dc->bsd', d_out_bf, w_ch2, preferred_element_type=jnp.flo...  131 us
    dot_general x2, matrix products, layer_forward(): jnp.einsum('bsc,cd->bsd', normed2, w_ch1, preferred_element_type=jnp.floa...  92.2 us
    dot_general x2, matrix products, layer_backward(): jnp.einsum('bsd,cd->bsc', d_hid_ch_bf, w_ch1, preferred_element_type=jnp....  70.9 us
    dot_general x2, matrix products, layer_backward(): jnp.einsum('bsc,js->bcj', d_after_bf, w_tok2, preferred_element_type=jnp....  70.6 us
    dot_general x2, matrix products, layer_backward(): jnp.einsum('bsd,bsc->dc', act_ch, d_out_bf, preferred_element_type=jnp.fl...  70 us
  transfers between devices with their start and end apart: 5, of which 2 were waited for; matrix products, arithmetic and copies ran while one was open for 47% of the time, Pallas kernels for 0%

commit v1 on v0

v1 whole, which is shorter than its diff:
```python
import functools
import math

import jax
import jax.numpy as jnp
from jax import lax
from jax.experimental import pallas as pl
from jax.experimental.pallas import tpu as pltpu
from jax.sharding import PartitionSpec as P

F32, BF16 = jnp.float32, jnp.bfloat16
LN_EPS = 1e-6
LEARN_RATE = 0.003
BETA_ONE = 0.9
BETA_TWO = 0.999
ADAM_EPS = 1e-8
WEIGHT_DECAY = 0.03
ADAM_STEP = 10

NDEV = 8
TOK, CH, TH, HID, NCLS = 196, 768, 384, 3072, 1000
SH = 4763
T1 = 2 * TOK * TH // 128
RW = CH * HID // 128
C1, C2 = HID // 128, CH // 128
VEC0 = T1 + 2 * RW - 7 * SH
MARG = 384
MESH = pl.DeviceIdType.MESH
ANY = pl.BlockSpec(memory_space=pl.ANY)
VMEM = pl.BlockSpec(memory_space=pltpu.VMEM)


def c1_span(d):
    return max(0, SH * d - T1), min(RW, SH * (d + 1) - T1)


def c2_span(d):
    return max(0, SH * d - T1 - RW), min(RW, SH * (d + 1) - T1 - RW)


def tiles_of(span, per):
    lo, hi = span
    if lo >= hi:
        return 0, 0
    return lo // per, -(-hi // per)


def edges(span_of, per):
    out = []
    for d in range(NDEV):
        lo, hi = span_of(d)
        if lo < hi and lo > 0 and lo % per:
            out.append((d, lo // per, lo % per))
    return out


EDGE1 = edges(c1_span, 16 * C1)
EDGE2 = edges(c2_span, 16 * C2)


def piece_moves(d, l, src, dst):
    s1, s2, stok, svec = src
    w1, w2, e1, e2, tok, vec = dst
    out = []
    for span_of, per, s, w, e, eds in ((c1_span, 16 * C1, s1, w1, e1, EDGE1), (c2_span, 16 * C2, s2, w2, e2, EDGE2)):
        lo, hi = tiles_of(span_of(d), per)
        if lo == hi:
            continue
        first = lo
        for k, (owner, row, _) in enumerate(eds):
            if owner == d:
                out.append((s.at[l, pl.ds(0, 16)], e.at[l, k]))
                first = lo + 1
        n = hi - first
        out.append((s.at[l, pl.ds(16 * (first - lo), 16 * n)], w.at[l, pl.ds(16 * first, 16 * n)]))
    if d == 0:
        out.append((stok.at[l], tok.at[l]))
    if d == NDEV - 1:
        out.append((svec.at[l], vec.at[l]))
    return out


def entry_barrier(me):
    barrier = pltpu.get_barrier_semaphore()
    for rel in (1, 2, 4, 6):
        pl.semaphore_signal(barrier, inc=1, device_id=(peer(me, rel),), device_id_type=MESH)
    pl.semaphore_wait(barrier, 4)


def peer(me, rel):
    t = me
    if rel & 1:
        t = t + 1 - 2 * lax.rem(me, 2)
    if rel & 2:
        t = t + 2 - 4 * lax.rem(me // 2, 2)
    if rel & 4:
        t = t + 4 - 8 * (me // 4)
    return t


RELS = (2, 4, 6)


def gather_kernel(p_ref, head_ref, small_ref, w1, w2, tok, vec, headf, smallf, e1, e2,
                  xs, s1, s2, stok, svec, shead, ssmall, m1, m2, ld_sem, send_sem, recv_sem, fwd_sem, own_sem, mg_sem):
    me = lax.axis_index("fsdp")
    for l in range(2):
        pltpu.make_async_copy(p_ref.at[:, l, :], xs.at[l, pl.ds(MARG, SH)], ld_sem.at[l]).start()
    shead[...] = head_ref[...].astype(BF16)
    ssmall[...] = small_ref[...].astype(BF16).astype(F32)
    entry_barrier(me)

    def moves(d, g, own_source):
        if g < 2:
            dst = (w1, w2, e1, e2, tok, vec)
            src = (s1, s2, stok, svec)
            both = piece_moves(d, g, src, dst)
        else:
            both = [(shead, headf.at[pl.ds(96 * d, 96)]), (ssmall, smallf.at[d])]
        return [(a if own_source else b, b, i) for i, (a, b) in enumerate(both)]

    def remote(a, b, ssem, d, dev):
        return pltpu.make_async_remote_copy(src_ref=a, dst_ref=b, send_sem=ssem, recv_sem=recv_sem.at[d], device_id=(dev,), device_id_type=MESH)

    for g in range(3):
        if g < 2:
            l = g
            pltpu.make_async_copy(p_ref.at[:, l, :], xs.at[l, pl.ds(MARG, SH)], ld_sem.at[l]).wait()
        for d in range(NDEV):
            @pl.when(me == d)
            def _():
                if g < 2:
                    for span_of, per, s in ((c1_span, C1, s1), (c2_span, C2, s2)):
                        lo, hi = tiles_of(span_of(d), 16 * per)
                        if lo == hi:
                            continue
                        base0 = 16 * per * lo - span_of(d)[0] + MARG + (T1 if (d == 0) else 0)
                        if per == C2 and d == 4:
                            base0 = base0 + c1_span(4)[1] - c1_span(4)[0]

                        def one(i, carry, per=per, s=s, base0=base0):
                            base = base0 + i * (16 * per)
                            row = pl.multiple_of(i * 16, 16)
                            for c in range(per):
                                s[l, pl.ds(row, 16), 128 * c:128 * c + 128] = xs[l, pl.ds(base + c, 16, stride=per), :].astype(BF16)
                            return carry

                        lax.fori_loop(0, hi - lo, one, 0)
                    if d == 0:
                        stok[l] = xs[l, MARG:MARG + T1, :].astype(BF16)
                    if d == NDEV - 1:
                        svec[l] = xs[l, MARG + VEC0:MARG + SH, :].astype(BF16)
                for k, rel in enumerate((4, 2, 6, 1)):
                    for a, b, i in moves(d, g, True):
                        remote(a, b, send_sem.at[k, g, i], (d, g, i), d ^ rel).start()
                for a, b, i in moves(d, g, True):
                    pltpu.make_async_copy(a, b, own_sem.at[g, i]).start()
    for g in range(3):
        for s in range(NDEV):
            for rel in RELS:
                @pl.when(me == (s ^ rel))
                def _():
                    for a, b, i in moves(s, g, False):
                        remote(a, b, fwd_sem.at[s, g, i], (s, g, i), s ^ rel ^ 1).wait_recv()
                    for a, b, i in moves(s, g, False):
                        remote(a, b, fwd_sem.at[s, g, i], (s, g, i), s ^ rel ^ 1).start()
    for g in range(3):
        for s in range(NDEV):
            for rel in (1, 3, 5, 7):
                @pl.when(me == (s ^ rel))
                def _():
                    for a, b, i in moves(s, g, False):
                        remote(a, b, fwd_sem.at[s, g, i], (s, g, i), s).wait_recv()
    for g in range(3):
        for d in range(NDEV):
            @pl.when(me == d)
            def _():
                for k, rel in enumerate((4, 2, 6, 1)):
                    for a, b, i in moves(d, g, True):
                        remote(a, b, send_sem.at[k, g, i], (d, g, i), d ^ rel).wait_send()
                for a, b, i in moves(d, g, True):
                    pltpu.make_async_copy(a, b, own_sem.at[g, i]).wait()
        for s in range(NDEV):
            for rel in RELS:
                @pl.when(me == (s ^ rel))
                def _():
                    for a, b, i in moves(s, g, False):
                        remote(a, b, fwd_sem.at[s, g, i], (s, g, i), s ^ rel ^ 1).wait_send()
    for per, w, e, m, eds in ((C1, w1, e1, m1, EDGE1), (C2, w2, e2, m2, EDGE2)):
        todo = [(l, k, row, below) for l in range(2) for k, (_, row, below) in enumerate(eds)]
        for l, k, row, below in todo:
            pltpu.make_async_copy(w.at[l, pl.ds(16 * row, 16)], m.at[0, l, k], mg_sem.at[0, l, k]).start()
            pltpu.make_async_copy(e.at[l, k], m.at[1, l, k], mg_sem.at[1, l, k]).start()
        for l, k, row, below in todo:
            pltpu.make_async_copy(w.at[l, pl.ds(16 * row, 16)], m.at[0, l, k], mg_sem.at[0, l, k]).wait()
            pltpu.make_async_copy(e.at[l, k], m.at[1, l, k], mg_sem.at[1, l, k]).wait()
        for l, k, row, below in todo:
            shape = (16, 128 * per)
            pos = lax.broadcasted_iota(jnp.int32, shape, 0) * per + lax.broadcasted_iota(jnp.int32, shape, 1) // 128
            m[0, l, k] = jnp.where(pos < below, m[0, l, k].astype(F32), m[1, l, k].astype(F32)).astype(BF16)
        for l, k, row, below in todo:
            pltpu.make_async_copy(m.at[0, l, k], w.at[l, pl.ds(16 * row, 16)], mg_sem.at[0, l, k]).start()
        for l, k, row, below in todo:
            pltpu.make_async_copy(m.at[0, l, k], w.at[l, pl.ds(16 * row, 16)], mg_sem.at[0, l, k]).wait()


def gather_all(p_view, head_w, small8):
    sds = jax.ShapeDtypeStruct
    outs = [sds((2, CH, HID), BF16), sds((2, HID, CH), BF16), sds((2, T1, 128), BF16), sds((2, SH - VEC0, 128), BF16),
            sds((CH, NCLS), BF16), sds((NDEV, 8, 128), F32), sds((2, len(EDGE1), 16, HID), BF16), sds((2, len(EDGE2), 16, CH), BF16)]
    n1 = max(16 * (b - a) for a, b in (tiles_of(c1_span(d), 16 * C1) for d in range(NDEV)))
    n2 = max(16 * (b - a) for a, b in (tiles_of(c2_span(d), 16 * C2) for d in range(NDEV)))
    dma = pltpu.SemaphoreType.DMA
    return pl.pallas_call(
        gather_kernel,
        in_specs=[ANY, VMEM, VMEM],
        out_specs=[ANY] * 8,
        out_shape=outs,
        scratch_shapes=[pltpu.VMEM((2, SH + 2 * MARG + 5, 128), F32), pltpu.VMEM((2, n1, HID), BF16), pltpu.VMEM((2, n2, CH), BF16),
                        pltpu.VMEM((2, T1, 128), BF16), pltpu.VMEM((2, SH - VEC0, 128), BF16), pltpu.VMEM((96, NCLS), BF16), pltpu.VMEM((8, 128), F32),
                        pltpu.VMEM((2, 2, len(EDGE1), 16, HID), BF16), pltpu.VMEM((2, 2, len(EDGE2), 16, CH), BF16),
                        dma((2,)), dma((4, 3, 3)), dma((NDEV, 3, 3)), dma((NDEV, 3, 3)), dma((3, 3)), dma((2, 2, 4))],
        compiler_params=pltpu.CompilerParams(collective_id=0, has_side_effects=True, vmem_limit_bytes=60000000),
        name="gather_weights",
    )(p_view, head_w, small8)[:6]


def g1_rows(d):
    lo, hi = tiles_of(c1_span(d), 8 * C1)
    return 8 * lo, 8 * hi


def g2_rows(d):
    lo, hi = tiles_of(c2_span(d), 8 * C2)
    return 8 * lo, 8 * hi


def pack(rows_of, core):
    at, where = 0, {}
    for s in range(core, NDEV, 2):
        lo, hi = rows_of(s)
        if lo < hi:
            where[s] = (lo, hi - lo, at)
            at += hi - lo
    return where, at


PK1 = [pack(g1_rows, c) for c in range(2)]
PK2 = [pack(g2_rows, c) for c in range(2)]
N1 = max(PK1[0][1], PK1[1][1])
N2 = max(PK2[0][1], PK2[1][1])
B1 = max(hi - lo for lo, hi in map(g1_rows, range(NDEV)))
B2 = max(hi - lo for lo, hi in map(g2_rows, range(NDEV)))


def reduce_kernel(dw1, dw2, tokg, vecg, out, a1, a2, at, av, r1, r2, rt, rv, b1, b2, bt, bv, gs, ld_sem, ps_sem, pr_sem, xs_sem, xr_sem):
    me = lax.axis_index("fsdp")
    core = lax.rem(me, 2)

    def chip_blocks(c, d1, d2, dt, dv):
        out_ = []
        for (where, _), g, dst in ((PK1[c], dw1, d1), (PK2[c], dw2, d2)):
            for s, (lo, n, at_) in where.items():
                out_.append((g.at[pl.ds(lo, n)], dst.at[pl.ds(at_, n)]))
        out_.append((tokg, dt) if c == 0 else (vecg, dv))
        return [(a, b, i) for i, (a, b) in enumerate(out_)]

    for c in range(2):
        @pl.when(core == c)
        def _():
            for a, b, i in chip_blocks(c, a1, a2, at, av):
                pltpu.make_async_copy(a, b, ld_sem.at[i]).start()
    entry_barrier(me)

    def to_partner(i, a, b, dev):
        return pltpu.make_async_remote_copy(src_ref=a, dst_ref=b, send_sem=ps_sem.at[i], recv_sem=pr_sem.at[i], device_id=(dev,), device_id_type=MESH)

    for c in range(2):
        @pl.when(core == c)
        def _():
            for a, b, i in chip_blocks(1 - c, r1, r2, rt, rv):
                to_partner(i, a, b, peer(me, 1)).start()
            for a, b, i in chip_blocks(c, a1, a2, at, av):
                pltpu.make_async_copy(a, b, ld_sem.at[i]).wait()
            for a, b, i in chip_blocks(c, r1, r2, rt, rv):
                to_partner(i, a, b, peer(me, 1)).wait_recv()

    def share_blocks(s, slot):
        c = s % 2
        out_ = []
        for (where, _), src, dst in ((PK1[c], a1, b1), (PK2[c], a2, b2)):
            if s in where:
                _, n, at_ = where[s]
                out_.append((src.at[pl.ds(at_, n)], dst.at[slot, pl.ds(0, n)]))
        if s == 0:
            out_.append((at, bt.at[slot]))
        if s == NDEV - 1:
            out_.append((av, bv.at[slot]))
        return [(a, b, i) for i, (a, b) in enumerate(out_)]

    def to_owner(a, b, slot, i, dev):
        return pltpu.make_async_remote_copy(src_ref=a, dst_ref=b, send_sem=xs_sem.at[slot, i], recv_sem=xr_sem.at[slot, i], device_id=(dev,), device_id_type=MESH)

    def add_rows(a, r, n, step):
        def one(i, carry):
            o = pl.multiple_of(i * step, step)
            a[pl.ds(o, step), :] = a[pl.ds(o, step), :] + r[pl.ds(o, step), :]
            return carry
        lax.fori_loop(0, n // step, one, 0)

    add_rows(a1, r1, N1, 16)
    add_rows(a2, r2, N2, 48)

    @pl.when(core == 0)
    def _():
        add_rows(at, rt, T1, 56)

    @pl.when(core == 1)
    def _():
        add_rows(av, rv, SH - VEC0, 64)

    for d in range(NDEV):
        @pl.when(me == d)
        def _():
            for slot, rel in enumerate(RELS):
                for a, b, i in share_blocks(d ^ rel, slot):
                    to_owner(a, b, slot, i, d ^ rel).start()
            for slot, rel in enumerate(RELS):
                for a, b, i in share_blocks(d, slot):
                    to_owner(a, b, slot, i, d ^ rel).wait_recv()
            for (where, _), src, dst, span_of, per in ((PK1[d % 2], a1, b1, c1_span, C1), (PK2[d % 2], a2, b2, c2_span, C2)):
                if d not in where:
                    continue
                lo, n, at_ = where[d]
                base0 = per * lo - span_of(d)[0] + MARG + (T1 if d == 0 else 0)
                if per == C2 and d == 4:
                    base0 = base0 + c1_span(4)[1] - c1_span(4)[0]

                def one(i, carry, src=src, dst=dst, per=per, base0=base0, at_=at_):
                    o = pl.multiple_of(i * 8, 8)
                    tot = src[pl.ds(at_ + o, 8), :] + dst[0, pl.ds(o, 8), :] + dst[1, pl.ds(o, 8), :] + dst[2, pl.ds(o, 8), :]
                    base = base0 + i * (8 * per)
                    for c in range(per):
                        gs[pl.ds(base + c, 8, stride=per), :] = tot[:, 128 * c:128 * c + 128]
                    return carry

                lax.fori_loop(0, n // 8, one, 0)
            if d == 0:
                gs[MARG:MARG + T1, :] = at[...] + bt[0] + bt[1] + bt[2]
            if d == NDEV - 1:
                gs[MARG + VEC0:MARG + SH, :] = av[...] + bv[0] + bv[1] + bv[2]
            pltpu.make_async_copy(gs.at[pl.ds(MARG, SH)], out, ld_sem.at[0]).start()
            for slot, rel in enumerate(RELS):
                for a, b, i in share_blocks(d ^ rel, slot):
                    to_owner(a, b, slot, i, d ^ rel).wait_send()
            pltpu.make_async_copy(gs.at[pl.ds(MARG, SH)], out, ld_sem.at[0]).wait()
    for c in range(2):
        @pl.when(core == c)
        def _():
            for a, b, i in chip_blocks(1 - c, r1, r2, rt, rv):
                to_partner(i, a, b, peer(me, 1)).wait_send()


def reduce_layer(dw1, dw2, tokg, vecg, cid):
    dma = pltpu.SemaphoreType.DMA
    nv = SH - VEC0
    return pl.pallas_call(
        reduce_kernel,
        in_specs=[ANY] * 4,
        out_specs=ANY,
        out_shape=jax.ShapeDtypeStruct((SH, 128), F32),
        scratch_shapes=[pltpu.VMEM((N1, HID), F32), pltpu.VMEM((N2, CH), F32), pltpu.VMEM((T1, 128), F32), pltpu.VMEM((nv, 128), F32),
                        pltpu.VMEM((N1, HID), F32), pltpu.VMEM((N2, CH), F32), pltpu.VMEM((T1, 128), F32), pltpu.VMEM((nv, 128), F32),
                        pltpu.VMEM((3, B1, HID), F32), pltpu.VMEM((3, B2, CH), F32), pltpu.VMEM((3, T1, 128), F32), pltpu.VMEM((3, nv, 128), F32),
                        pltpu.VMEM((SH + 2 * MARG + 5, 128), F32), dma((6,)), dma((6,)), dma((6,)), dma((3, 2)), dma((3, 2))],
        compiler_params=pltpu.CompilerParams(collective_id=cid, has_side_effects=True, vmem_limit_bytes=66000000),
        name=f"reduce_grads_{cid}",
    )(dw1, dw2, tokg, vecg)


def adam_math(p, g, m, v, decay):
    m_new = BETA_ONE * m + (1.0 - BETA_ONE) * g
    v_new = BETA_TWO * v + (1.0 - BETA_TWO) * g * g
    m_hat = m_new / (1.0 - BETA_ONE ** ADAM_STEP)
    v_hat = v_new / (1.0 - BETA_TWO ** ADAM_STEP)
    p_new = p - LEARN_RATE * (m_hat / (jnp.sqrt(v_hat) + ADAM_EPS) + decay * p)
    return p_new, m_new, v_new


NCHUNK = 4


def chunk_rows(k):
    step = -(-SH // (40 * NCHUNK)) * 40
    return k * step, min(SH, (k + 1) * step) - k * step


def adam_kernel(p_ref, m_ref, v_ref, g0, g1, scale_ref, po, mo, vo, ps, ms, vs, gs, in_sem, out_sem):
    me = lax.axis_index("fsdp")
    ins = ((p_ref, ps), (m_ref, ms), (v_ref, vs))
    outs = ((ps, po), (ms, mo), (vs, vo))

    def loads(k):
        a, n = chunk_rows(k)
        for j, (src, dst) in enumerate(ins):
            for l in range(2):
                yield pltpu.make_async_copy(src.at[pl.ds(a, n), l, :], dst.at[l, pl.ds(a, n)], in_sem.at[k, j, l])
        for l, g in enumerate((g0, g1)):
            yield pltpu.make_async_copy(g.at[pl.ds(a, n)], gs.at[l, pl.ds(a, n)], in_sem.at[k, 3, l])

    def stores(k):
        a, n = chunk_rows(k)
        for j, (src, dst) in enumerate(outs):
            for l in range(2):
                yield pltpu.make_async_copy(src.at[l, pl.ds(a, n)], dst.at[pl.ds(a, n), l, :], out_sem.at[k, j, l])

    for k in range(NCHUNK):
        for c in loads(k):
            c.start()
    scale = scale_ref[0, 0]
    mat_rows = T1 + 2 * RW - me * SH
    for k in range(NCHUNK):
        for c in loads(k):
            c.wait()
        a, n = chunk_rows(k)
        for l in range(2):
            def one(i, carry, l=l, a=a):
                o = pl.multiple_of(a + i * 40, 8)
                row = o + lax.broadcasted_iota(jnp.int32, (40, 128), 0)
                decay = jnp.where(row < mat_rows, WEIGHT_DECAY, 0.0)
                at = pl.ds(o, 40)
                p, m, v = adam_math(ps[l, at, :], gs[l, at, :] * scale, ms[l, at, :], vs[l, at, :], decay)
                ps[l, at, :] = p
                ms[l, at, :] = m
                vs[l, at, :] = v
                return carry
            lax.fori_loop(0, -(-n // 40), one, 0)
        for c in stores(k):
            c.start()
    for k in range(NCHUNK):
        for c in stores(k):
            c.wait()


def adam_layers(pv, mv, vv, g0, g1, scale):
    sds = jax.ShapeDtypeStruct((SH, 2, 128), F32)
    rows = chunk_rows(NCHUNK - 1)[0] + -(-chunk_rows(NCHUNK - 1)[1] // 40) * 40
    rows = max(rows, chunk_rows(1)[0] * NCHUNK)
    buf = pltpu.VMEM((2, rows + 40, 128), F32)
    return pl.pallas_call(
        adam_kernel,
        in_specs=[ANY] * 5 + [pl.BlockSpec(memory_space=pltpu.SMEM)],
        out_specs=[ANY] * 3,
        out_shape=[sds] * 3,
        scratch_shapes=[buf] * 4 + [pltpu.SemaphoreType.DMA((NCHUNK, 4, 2))] * 2,
        compiler_params=pltpu.CompilerParams(vmem_limit_bytes=60000000),
        name="adam_layers",
    )(pv, mv, vv, g0, g1, scale)


def layer_norm(x_in, ln_gain, ln_shift):
    x_f = x_in.astype(F32)
    mean_val = jnp.mean(x_f, axis=-1, keepdims=True)
    var_val = jnp.mean(jnp.square(x_f - mean_val), axis=-1, keepdims=True)
    normed = (x_f - mean_val) * lax.rsqrt(var_val + LN_EPS)
    return (normed * ln_gain.astype(F32) + ln_shift.astype(F32)).astype(BF16)


def gelu_bf16(hidden):
    return jax.nn.gelu(hidden).astype(BF16)


def gelu_grad(hidden, d_act):
    _, pullback = jax.vjp(gelu_bf16, hidden)
    return pullback(d_act.astype(BF16))[0]


def norm_grad(x_in, ln_gain, ln_shift, d_normed):
    _, pullback = jax.vjp(layer_norm, x_in, ln_gain.astype(F32), ln_shift.astype(F32))
    d_x, d_gain, d_shift = pullback(d_normed.astype(BF16))
    return d_x.astype(F32), d_gain, d_shift


def layer_forward(x_in, weights):
    w_tok1, w_tok2, w_ch1, w_ch2, ln1_g, ln1_b, b_tok1, b_tok2, ln2_g, ln2_b, b_ch1, b_ch2 = weights
    normed = layer_norm(x_in, ln1_g, ln1_b)
    hid_tok = jnp.einsum('bsc,sj->bcj', normed, w_tok1, preferred_element_type=F32) + b_tok1.astype(F32)
    act_tok = gelu_bf16(hid_tok)
    tok_out = jnp.einsum('bcj,js->bsc', act_tok, w_tok2, preferred_element_type=F32) + b_tok2.astype(F32)[:, None]
    after_tok = (x_in.astype(F32) + tok_out).astype(BF16)
    normed2 = layer_norm(after_tok, ln2_g, ln2_b)
    hid_ch = jnp.einsum('bsc,cd->bsd', normed2, w_ch1, preferred_element_type=F32) + b_ch1.astype(F32)
    act_ch = gelu_bf16(hid_ch)
    ch_out = jnp.einsum('bsd,dc->bsc', act_ch, w_ch2, preferred_element_type=F32) + b_ch2.astype(F32)
    layer_out = (after_tok.astype(F32) + ch_out).astype(BF16)
    return layer_out, (x_in, normed, hid_tok, act_tok, after_tok, normed2, hid_ch, act_ch)


def layer_backward(d_out, weights, cache):
    w_tok1, w_tok2, w_ch1, w_ch2, ln1_g, ln1_b, b_tok1, b_tok2, ln2_g, ln2_b, b_ch1, b_ch2 = weights
    x_in, normed, hid_tok, act_tok, after_tok, normed2, hid_ch, act_ch = cache
    d_out_bf = d_out.astype(BF16)
    g_b_ch2 = jnp.sum(d_out, axis=(0, 1))
    g_w_ch2 = jnp.einsum('bsd,bsc->dc', act_ch, d_out_bf, preferred_element_type=F32)
    d_act_ch = jnp.einsum('bsc,dc->bsd', d_out_bf, w_ch2, preferred_element_type=F32)
    d_hid_ch = gelu_grad(hid_ch, d_act_ch)
    d_hid_ch_bf = d_hid_ch.astype(BF16)
    g_b_ch1 = jnp.sum(d_hid_ch, axis=(0, 1))
    g_w_ch1 = jnp.einsum('bsc,bsd->cd', normed2, d_hid_ch_bf, preferred_element_type=F32)
    d_normed2 = jnp.einsum('bsd,cd->bsc', d_hid_ch_bf, w_ch1, preferred_element_type=F32)
    d_after_ln, g_ln2_g, g_ln2_b = norm_grad(after_tok, ln2_g, ln2_b, d_normed2)
    d_after = d_after_ln + d_out
    d_after_bf = d_after.astype(BF16)
    g_b_tok2 = jnp.sum(d_after, axis=(0, 2))
    g_w_tok2 = jnp.einsum('bcj,bsc->js', act_tok, d_after_bf, preferred_element_type=F32)
    d_act_tok = jnp.einsum('bsc,js->bcj', d_after_bf, w_tok2, preferred_element_type=F32)
    d_hid_tok = gelu_grad(hid_tok, d_act_tok)
    d_hid_tok_bf = d_hid_tok.astype(BF16)
    g_b_tok1 = jnp.sum(d_hid_tok, axis=(0, 1))
    g_w_tok1 = jnp.einsum('bsc,bcj->sj', normed, d_hid_tok_bf, preferred_element_type=F32)
    d_normed = jnp.einsum('bcj,sj->bsc', d_hid_tok_bf, w_tok1, preferred_element_type=F32)
    d_in_ln, g_ln1_g, g_ln1_b = norm_grad(x_in, ln1_g, ln1_b, d_normed)
    d_in = d_in_ln + d_after
    tok_flat = jnp.concatenate([g_w_tok1.reshape(-1, 128), g_w_tok2.reshape(-1, 128)])
    vec_flat = jnp.concatenate([g_ln1_g, g_ln1_b, g_b_tok1, g_b_tok2, g_ln2_g, g_ln2_b, g_b_ch1, g_b_ch2])
    vec_flat = jnp.pad(vec_flat, (0, (SH - VEC0) * 128 - vec_flat.shape[0])).reshape(-1, 128)
    return d_in, (g_w_ch1, g_w_ch2, tok_flat, vec_flat)


def head_step(hidden, labels, lnf_g, lnf_b, head_b, head_full, global_b):
    num_tokens = hidden.shape[1]
    normed = layer_norm(hidden, lnf_g, lnf_b)
    pooled = (jnp.sum(normed, axis=1, dtype=F32) / num_tokens).astype(BF16)
    logits = jnp.dot(pooled, head_full, preferred_element_type=F32) + head_b.astype(F32)
    log_norm = jax.nn.logsumexp(logits, axis=-1)
    is_label = jnp.arange(NCLS)[None, :] == labels[:, None]
    picked = jnp.sum(jnp.where(is_label, logits, 0.0), axis=-1)
    loss_sum = jnp.sum(log_norm - picked)
    d_logits = (jnp.exp(logits - log_norm[:, None]) - is_label.astype(F32)) / global_b
    d_logits_bf = d_logits.astype(BF16)
    g_head_b = jnp.sum(d_logits, axis=0)
    g_head_w = jnp.einsum('bc,bk->ck', pooled, d_logits_bf, preferred_element_type=F32)
    d_pooled = jnp.einsum('bk,ck->bc', d_logits_bf, head_full, preferred_element_type=F32)
    d_normed = jnp.broadcast_to((d_pooled / num_tokens)[:, None, :], normed.shape)
    d_hidden, g_lnf_g, g_lnf_b = norm_grad(hidden, lnf_g, lnf_b, d_normed)
    g_small = jnp.concatenate([g_lnf_g, g_lnf_b, g_head_b])
    return loss_sum, d_hidden, g_head_w, g_small


VEC_SIZES = (CH, CH, TH, TOK, CH, CH, HID, CH)


def unpack_vectors(vec):
    flat, out, at = vec.reshape(-1), [], 0
    for n in VEC_SIZES:
        out.append(flat[at:at + n])
        at += n
    return out


def view(a):
    return a.reshape(2, SH, 128).transpose(1, 0, 2)


def unview(a):
    return a.transpose(1, 0, 2).reshape(2, SH * 128)


def solution(mesh):
    row_spec = P('fsdp')
    layer_spec = P(None, 'fsdp')
    in_specs = (row_spec, row_spec, layer_spec, row_spec, row_spec, layer_spec, row_spec, row_spec, layer_spec, row_spec, row_spec)
    out_specs = (P(),) + in_specs[2:]

    def device_step(act_in, labels, layer_p, head_w, small_p, layer_m, head_m, small_m, layer_v, head_v, small_v):
        global_b = act_in.shape[0] * NDEV
        small8 = jnp.pad(small_p.reshape(3, 128), ((0, 5), (0, 0)))
        w1, w2, tok, vec, head_full, small_slots = gather_all(view(layer_p), head_w, small8)
        small_full = small_slots[:, :3].reshape(-1)
        weights = []
        for l in range(2):
            wt1 = tok[l, :T1 // 2].reshape(TOK, TH)
            wt2 = tok[l, T1 // 2:].reshape(TH, TOK)
            weights.append([wt1, wt2, w1[l], w2[l]] + unpack_vectors(vec[l]))
        hidden, caches = act_in, []
        for l in range(2):
            hidden, cache = layer_forward(hidden, weights[l])
            caches.append(cache)
        loss_sum, d_hidden, g_head_w, g_small = head_step(
            hidden, labels, small_full[:CH], small_full[CH:2 * CH], small_full[2 * CH:2 * CH + NCLS], head_full, global_b)
        shards = [None, None]
        for l in (1, 0):
            d_hidden, grads = layer_backward(d_hidden, weights[l], caches[l])
            shards[l] = reduce_layer(*grads, cid=1 + l)
        head_g = lax.psum_scatter(g_head_w, 'fsdp', scatter_dimension=0, tiled=True)
        small_flat = jnp.pad(g_small, (0, 3072 - g_small.shape[0]))
        small_g = lax.psum_scatter(small_flat, 'fsdp', scatter_dimension=0, tiled=True)
        sq_local = sum(jnp.sum(jnp.square(g)) for g in (shards[0], shards[1], head_g, small_g))
        loss_value, sq = lax.psum((loss_sum, sq_local), 'fsdp')
        clip_scale = 1.0 / jnp.maximum(1.0, jnp.sqrt(sq))
        new_l = adam_layers(view(layer_p), view(layer_m), view(layer_v), shards[0], shards[1], clip_scale.reshape(1, 1))
        new_lp, new_lm, new_lv = [unview(a) for a in new_l]
        new_hw, new_hm, new_hv = adam_math(head_w, head_g * clip_scale, head_m, head_v, WEIGHT_DECAY)
        new_sp, new_sm, new_sv = adam_math(small_p, small_g * clip_scale, small_m, small_v, 0.0)
        return (loss_value / global_b, new_lp, new_hw, new_sp, new_lm, new_hm, new_sm, new_lv, new_hv, new_sv)

    return jax.shard_map(device_step, mesh=mesh, in_specs=in_specs, out_specs=out_specs, check_vma=False)
```

time: 2120 us -> 1360 us (0.64); the launches traced: 2090 us -> 1360 us
  local copies, waits for them, and re-layouts: 644 us -> 21.3 us
  waiting for transfers between devices: 491 us -> 0.02 us
  Pallas kernels: 0 us -> 411 us
  other arithmetic: 165 us -> 137 us
    unnamed x6 -> x1, waiting for transfers between devices: 421 us -> 0.02 us
    pallas_call x0 -> x4, Pallas kernels: none -> 411 us  [the longest x2 262 us: reduce_layer(): pl.pallas_call(reduce_kernel, in_specs=[ANY] * 4, out_specs=ANY, out_shap...]
    concatenate x3 -> x2, local copies, waits for them, and re-layouts: 307 us -> 0.17 us  [layer_backward(): jnp.concatenate([g_ln1_g, g_ln1_b, g_b_tok1, g_b_tok2, g_ln2_g, g_ln2_b,...]
    slice x5 -> x4, local copies, waits for them, and re-layouts: 220 us -> 4.56 us  [the longest x1 1.87 us: device_step(): wt2 = tok[l, T1 // 2:].reshape(TH, TOK)]
    all_gather x3 -> x0, waiting for transfers between devices: 69.8 us -> none  [the longest x2 69.8 us: device_step(): lax.all_gather(layer_p[layer_idx].astype(jnp.bfloat16), 'fsdp', tiled=True)]
    reshape x14 -> x7, local copies, waits for them, and re-layouts: 61.6 us -> 4.98 us  [the longest x2 2.72 us: layer_backward(): g_w_tok2.reshape(-1, 128)]
    unnamed x242 -> x216, local copies, waits for them, and re-layouts: 31.6 us -> 8.14 us
    sub x3 -> x2, other arithmetic: 25.1 us -> 1.89 us  [adam_math(): p_new = p - LEARN_RATE * (m_hat / (jnp.sqrt(v_hat) + ADAM_EPS) + decay * p)]
  transfers between devices with their start and end apart: 5 -> 1, of which waited for: 2 -> 0; matrix products, arithmetic and copies ran while one was open for 47% -> 44% of each run, Pallas kernels for 0% -> 19%
where the time goes in v1:
time: 1360 us
  matrix products  716 us (53%)
  Pallas kernels  411 us (30%)
  other arithmetic  137 us (10%)
  blocking collectives  49.8 us (4%)
  local copies, waits for them, and re-layouts  21.3 us (2%)
  between operations  21 us (2%)
    pallas_call x2, Pallas kernels, reduce_layer(): pl.pallas_call(reduce_kernel, in_specs=[ANY] * 4, out_specs=ANY, out_shap...  262 us
    pallas_call x1, Pallas kernels, gather_all(): pl.pallas_call(gather_kernel, in_specs=[ANY, VMEM, VMEM], out_specs=[ANY]...  136 us
    dot_general x2, matrix products, layer_backward(): jnp.einsum('bsc,dc->bsd', d_out_bf, w_ch2, preferred_element_type=F32)  131 us
    dot_general x2, matrix products, layer_forward(): jnp.einsum('bsc,cd->bsd', normed2, w_ch1, preferred_element_type=F32)  92.2 us
    dot_general x2, matrix products, layer_backward(): jnp.einsum('bsd,cd->bsc', d_hid_ch_bf, w_ch1, preferred_element_type=F32)  71.3 us
    dot_general x2, matrix products, layer_backward(): jnp.einsum('bsc,js->bcj', d_after_bf, w_tok2, preferred_element_type=F32)  70.4 us
    dot_general x2, matrix products, layer_backward(): jnp.einsum('bsd,bsc->dc', act_ch, d_out_bf, preferred_element_type=F32)  70.2 us
    dot_general x2, matrix products, layer_backward(): jnp.einsum('bsc,bsd->cd', normed2, d_hid_ch_bf, preferred_element_type=F32)  67 us
  transfers between devices with their start and end apart: 1, of which 0 were waited for; matrix products, arithmetic and copies ran while one was open for 44% of the time, Pallas kernels for 19%

profile of v1, /device:TPU:0, one launch (start us, length us, event | category | flops | bytes accessed | tf_op | source)
XLA Modules:
  0.0 1356.6 jit_solution(1999236403995378896)
XLA Ops:
  8.5 135.5 %gather_weights.1 = (bf16[2,768,3072]{2,1,0:T(8,128)(2,1)}, bf16[2,3072,768]{2,1,0:T(8,128)(2,1)}, bf16[2,1176,128]{2,1,0:T(8,128)(2,1)}, bf16[2,64,128]{2,1,0:T...) custom-call(f32[4763,2,128]{2,1,0:T(2,128)} %bitcast.189, ...), custom_call_target="tpu_custom_call" | custom-call | tf_op jit(solution)/shard_map/gather_weights/pallas_call | solution.py:214
  166.7 22.9 %multiply_convert_fusion.3 = (bf16[24,768,384]{2,1,0:T(8,128)(2,1)}, f32[24,768,384]{2,1,0:T(8,128)}) fusion(f32[384]{0:T(512)S(1)} %get-tuple-element.68, bf16[196,384,1]{1,0,2:T(8,128)(2,1)S(1)} %reshape.315, f32[768]{0:T(1024)S(1)} %get-tuple-element.71, f32[768]{0:T(1024)S(1)} %get-tuple-element.72, f32[24,196]{1,0:T(8,128)S(1)} %add_rsqrt_fusion, ...), kind=kOutput, calls=%fused_computation.55 | convolution fusion | flops 2866987008 | bytes 49888512 | tf_op jit(solution)/shard_map/bsc,sj->bcj/dot_general | solution.py:487
  208.5 46.2 %multiply_convert_fusion.1 = (bf16[24,196,3072]{2,1,0:T(8,128)(2,1)}, f32[24,196,3072]{2,1,0:T(8,128)}) fusion(f32[3072]{0:T(1024)S(1)} %get-tuple-element.111, bf16[2,768,3072]{2,1,0:T(8,128)(2,1)} %get-tuple-element.21, bf16[24,196,768]{2,1,0:T(8,128)(2,1)} %get-tuple-element.82, f32[768]{0:T(1024)S(1)} %get-tuple-element.113, ...), kind=kOutput, calls=%fused_computation.27 | convolution fusion | flops 22362439680 | bytes 98851584 | tf_op jit(solution)/shard_map/bsc,cd->bsd/dot_general | solution.py:492
  254.7 30.0 %convert_reduce_fusion.3 = (f32[24,196]{1,0:T(8,128)S(1)}, bf16[24,196,768]{2,1,0:T(8,128)(2,1)S(1)}) fusion(f32[768]{0:T(1024)S(1)} %get-tuple-element.114, bf16[24,196,3072]{2,1,0:T(8,128)(2,1)} %get-tuple-element.83, bf16[2,3072,768]{2,1,0:T(8,128)(2,1)} %get-tuple-element.22, bf16[24,196,768]{2,1,0:T(8,128)(2,1)} %get-tuple-element.82), kind=kOutput, calls=%fused_computation.71 | convolution fusion | flops 22217928704 | bytes 48829824 | tf_op jit(solution)/shard_map/bsd,dc->bsc/dot_general | solution.py:494
  292.0 21.6 %multiply_convert_fusion.2 = (bf16[24,768,384]{2,1,0:T(8,128)(2,1)}, f32[24,768,384]{2,1,0:T(8,128)}) fusion(f32[384]{0:T(512)S(1)} %copy-done.99, bf16[196,384,1]{1,0,2:T(8,128)(2,1)S(1)} %reshape.319, bf16[24,196,768]{2,1,0:T(8,128)(2,1)} %copy-done.3, f32[768]{0:T(1024)S(1)} %copy-done.94, f32[768]{0:T(1024)S(1)} %copy-done.62, ...), kind=kOutput, calls=%fused_computation.54 | convolution fusion | flops 2866987008 | bytes 49888512 | tf_op jit(solution)/shard_map/bsc,sj->bcj/dot_general | solution.py:487
  332.2 46.1 %multiply_convert_fusion = (bf16[24,196,3072]{2,1,0:T(8,128)(2,1)}, f32[24,196,3072]{2,1,0:T(8,128)}) fusion(f32[3072]{0:T(1024)S(1)} %copy-done.70, bf16[2,768,3072]{2,1,0:T(8,128)(2,1)} %get-tuple-element.21, bf16[24,196,768]{2,1,0:T(8,128)(2,1)} %get-tuple-element.90, f32[768]{0:T(1024)S(1)} %copy-done.82, f32[768]{0:T(1024)S(1)} %copy-done.57, ...), kind=kOutput, calls=%fused_computation.26 | convolution fusion | flops 22362439680 | bytes 98851584 | tf_op jit(solution)/shard_map/bsc,cd->bsd/dot_general | solution.py:492
  378.3 29.9 %convert_reduce_fusion.9 = (f32[24,196]{1,0:T(8,128)S(1)}, bf16[24,196,768]{2,1,0:T(8,128)(2,1)S(1)}) fusion(f32[768]{0:T(1024)S(1)} %copy-done.89, bf16[24,196,3072]{2,1,0:T(8,128)(2,1)} %get-tuple-element.91, bf16[2,3072,768]{2,1,0:T(8,128)(2,1)} %get-tuple-element.22, bf16[24,196,768]{2,1,0:T(8,128)(2,1)} %get-tuple-element.90), kind=kOutput, calls=%fused_computation.99 | convolution fusion | flops 22217928704 | bytes 48829824 | tf_op jit(solution)/shard_map/bsd,dc->bsc/dot_general | solution.py:494
  435.6 66.5 %fusion.233 = (f32[3072]{0:T(1024)}, bf16[24,196,3072]{2,1,0:T(8,128)(2,1)}) fusion(f32[24,196,3072]{2,1,0:T(8,128)} %get-tuple-element.92, f32[3072]{0:T(1024)S(1)} %copy-done.70, bf16[2,3072,768]{2,1,0:T(8,128)(2,1)} %get-tuple-element.22, bf16[24,196,768]{2,1,0:T(8,128)(2,1)} %copy-done, f32[24,196]{1,0:T(8,128)S(1)} %add_multiply_fusion.3, ...), kind=kOutput, calls=%fused_computation.307 | convolution fusion | flops 22571970560 | bytes 100151808 | tf_op jit(solution)/shard_map/bsc,dc->bsd/dot_general | solution.py:505
  502.1 35.4 %fusion.111 = (f32[768]{0:T(1024)}, f32[24,196]{1,0:T(8,128)S(1)}, f32[24,196]{1,0:T(8,128)S(1)}, f32[768]{0:T(1024)}, bf16[24,196,768]{2,1,0:T(8,128)(2,1)}) fusion(bf16[24,196,768]{2,1,0:T(8,128)(2,1)} %get-tuple-element.90, f32[24,196]{1,0:T(8,128)S(1)} %copy-done.47, f32[24,196]{1,0:T(8,128)S(1)} %copy-done.21, f32[768]{0:T(1024)S(1)} %copy-done.58, ...), kind=kOutput, calls=%fused_computation.159 | convolution fusion | flops 22243213312 | bytes 48892416 | tf_op jit(solution)/shard_map/bsd,cd->bsc/dot_general | solution.py:510
  542.9 16.3 %convert_reduce_fusion.8 = (f32[768]{0:T(1024)}, f32[196]{0:T(256)}, f32[768]{0:T(1024)}, f32[768]{0:T(1024)}, bf16[24,196,768]{2,1,0:T(8,128)(2,1)S(1)}) fusion(f32[24,196]{1,0:T(8,128)S(1)} %add_multiply_fusion.3, f32[24,196]{1,0:T(8,128)S(1)} %multiply_multiply_fusion.14, f32[24,196]{1,0:T(8,128)S(1)} %broadcast_multiply_fusion, ...), kind=kLoop, calls=%fused_computation.96 | loop fusion | flops 93926976 | bytes 29141776 | tf_op jit(solution)/shard_map/reduce_sum | solution.py:503
  559.3 35.7 %fusion.232 = (f32[384]{0:T(512)}, bf16[24,768,384]{2,1,0:T(8,128)(2,1)}) fusion(f32[24,768,384]{2,1,0:T(8,128)} %get-tuple-element.88, f32[384]{0:T(512)S(1)} %copy-done.100, bf16[384,196]{1,0:T(8,128)(2,1)S(1)} %copy-done.32, bf16[24,196,768]{2,1,0:T(8,128)(2,1)S(1)} %get-tuple-element.57, f32[24,196]{1,0:T(8,128)S(1)} %add_multiply_fusion.3, ...), kind=kOutput, calls=%fused_computation.306 | convolution fusion | flops 2987752960 | bytes 57223680 | tf_op jit(solution)/shard_map/bsc,js->bcj/dot_general | solution.py:516
  629.7 36.8 %convolution_bitcast_fusion.dw2 = f32[3072,768]{1,0:T(8,128)} fusion(bf16[24,196,3072]{2,1,0:T(8,128)(2,1)} %get-tuple-element.91, bf16[24,196,768]{2,1,0:T(8,128)(2,1)S(1)} %bitcast.186, f32[24,196]{1,0:T(8,128)S(1)} %add_multiply_fusion.3, f32[24,196]{1,0:T(8,128)S(1)} %multiply_multiply_fusion.14, f32[24,768]{1,0:T(8,128)S(1)} %fusion.198, ...), kind=kOutput, calls=%fused_computation.191 | convolution fusion | flops 22225158144 | bytes 45715968 | tf_op jit(solution)/shard_map/bsd,bsc->dc/dot_general | solution.py:504
  666.6 33.7 %fusion.145.dw1 = f32[768,3072]{1,0:T(8,128)} fusion(bf16[24,196,3072]{2,1,0:T(8,128)(2,1)} %get-tuple-element.109, bf16[24,196,768]{2,1,0:T(8,128)(2,1)} %get-tuple-element.90, f32[768]{0:T(1024)S(1)} %copy-done.83, f32[768]{0:T(1024)S(1)} %copy-done.59, f32[24,196]{1,0:T(8,128)S(1)} %copy-done.48, f32[24,196]{1,0:T(8,128)S(1)} %copy-done.21), kind=kOutput, calls=%fused_computation.189 | convolution fusion | flops 22217932800 | bytes 45607680 | tf_op jit(solution)/shard_map/bsc,bsd->cd/dot_general | solution.py:509
  720.7 65.0 %fusion.231 = (f32[3072]{0:T(1024)}, bf16[24,196,3072]{2,1,0:T(8,128)(2,1)}) fusion(f32[24,196,3072]{2,1,0:T(8,128)} %get-tuple-element.84, f32[3072]{0:T(1024)S(1)} %copy-done.69, bf16[2,3072,768]{2,1,0:T(8,128)(2,1)} %get-tuple-element.22, f32[24,196,768]{2,1,0:T(8,128)} %convert_add_fusion.6), kind=kOutput, calls=%fused_computation.305 | convolution fusion | flops 22546681856 | bytes 107372544 | tf_op jit(solution)/shard_map/bsc,dc->bsd/dot_general | solution.py:505
  785.7 35.9 %fusion.112 = (f32[768]{0:T(1024)}, f32[24,196]{1,0:T(8,128)S(1)}, f32[24,196]{1,0:T(8,128)S(1)}, f32[768]{0:T(1024)}, bf16[24,196,768]{2,1,0:T(8,128)(2,1)}) fusion(bf16[24,196,768]{2,1,0:T(8,128)(2,1)} %get-tuple-element.82, f32[24,196]{1,0:T(8,128)S(1)} %copy-done.40, f32[24,196]{1,0:T(8,128)S(1)} %copy-done.16, f32[768]{0:T(1024)S(1)} %copy-done.55, ...), kind=kOutput, calls=%fused_computation.160 | convolution fusion | flops 22243213312 | bytes 48892416 | tf_op jit(solution)/shard_map/bsd,cd->bsc/dot_general | solution.py:510
  838.6 34.7 %fusion.230 = (f32[384]{0:T(512)S(1)}, bf16[24,768,384]{2,1,0:T(8,128)(2,1)}) fusion(f32[24,768,384]{2,1,0:T(8,128)} %get-tuple-element.80, f32[384]{0:T(512)S(1)} %copy-done.98, bf16[384,196]{1,0:T(8,128)(2,1)S(1)} %copy-done.30, f32[24,196,768]{2,1,0:T(8,128)} %convert_add_fusion.6, bf16[24,196,768]{2,1,0:T(8,128)(2,1)} %get-tuple-element.58), kind=kOutput, calls=%fused_computation.304 | convolution fusion | flops 2955238912 | bytes 64296960 | tf_op jit(solution)/shard_map/bsc,js->bcj/dot_general | solution.py:516
  873.3 15.2 %fusion.90 = (f32[768]{0:T(1024)S(1)}, bf16[196,24,768]{2,0,1:T(8,128)(2,1)}) fusion(f32[24,196]{1,0:T(8,128)S(1)} %copy-done.51, f32[24,196]{1,0:T(8,128)S(1)} %copy-done.43, bf16[24,196,768]{2,0,1:T(8,128)(2,1)} %param.11, bf16[196,384,1]{1,0,2:T(8,128)(2,1)S(1)} %copy-done.34, bf16[24,768,384]{2,1,0:T(8,128)(2,1)} %get-tuple-element.103), kind=kOutput, calls=%fused_computation.138 | convolution fusion | flops 2799820032 | bytes 28797696 | tf_op jit(solution)/shard_map/bcj,sj->bsc/dot_general | solution.py:521
  900.5 16.0 %convolution_bitcast_fusion.2 = f32[384,196]{1,0:T(8,128)} fusion(bf16[24,768,384]{2,1,0:T(8,128)(2,1)} %get-tuple-element.79, f32[24,196,768]{2,1,0:T(8,128)} %convert_add_fusion.6, bf16[24,196,768]{2,1,0:T(8,128)(2,1)} %get-tuple-element.58), kind=kOutput, calls=%fused_computation.218 | convolution fusion | flops 2785370112 | bytes 36132864 | tf_op jit(solution)/shard_map/bcj,bsc->js/dot_general | solution.py:515
  916.5 33.4 %convolution_bitcast_fusion.1.dw2 = f32[3072,768]{1,0:T(8,128)} fusion(bf16[24,196,3072]{2,1,0:T(8,128)(2,1)} %get-tuple-element.83, f32[24,196,768]{2,1,0:T(8,128)} %convert_add_fusion.6), kind=kOutput, calls=%fused_computation.192 | convolution fusion | flops 22199869440 | bytes 52789248 | tf_op jit(solution)/shard_map/bsd,bsc->dc/dot_general | solution.py:504
  968.3 131.5 %reduce_grads_2.1.g1 = f32[4763,128]{1,0:T(8,128)} custom-call(f32[768,3072]{1,0:T(8,128)} %fusion.145.dw1, f32[3072,768]{1,0:T(8,128)} %convolution_bitcast_fusion.dw2, f32[1176,128]{1,0:T(8,128)} %pad_maximum_fusion.1.tokg, f32[64,128]{1,0:T(8,128)} %pad_bitcast_fusion.vecg), custom_call_target="tpu_custom_call" | custom-call | tf_op jit(solution)/shard_map/reduce_grads_2/pallas_call | solution.py:367
  1105.7 33.3 %fusion.148.dw1 = f32[768,3072]{1,0:T(8,128)} fusion(bf16[24,196,3072]{2,1,0:T(8,128)(2,1)} %get-tuple-element.105, bf16[24,196,768]{2,1,0:T(8,128)(2,1)} %get-tuple-element.82, f32[768]{0:T(1024)S(1)} %copy-done.81, f32[768]{0:T(1024)S(1)} %copy-done.56, f32[24,196]{1,0:T(8,128)S(1)} %copy-done.41, f32[24,196]{1,0:T(8,128)S(1)} %copy-done.17), kind=kOutput, calls=%fused_computation.190 | convolution fusion | flops 22217932800 | bytes 45607680 | tf_op jit(solution)/shard_map/bsc,bsd->cd/dot_general | solution.py:509
  1139.0 130.0 %reduce_grads_1.1.g0 = f32[4763,128]{1,0:T(8,128)} custom-call(f32[768,3072]{1,0:T(8,128)} %fusion.148.dw1, f32[3072,768]{1,0:T(8,128)} %convolution_bitcast_fusion.1.dw2, f32[1176,128]{1,0:T(8,128)} %pad_maximum_fusion.tokg, f32[64,128]{1,0:T(8,128)} %pad_bitcast_fusion.1.vecg), custom_call_target="tpu_custom_call" | custom-call | tf_op jit(solution)/shard_map/reduce_grads_1/pallas_call | solution.py:367
  1276.6 25.4 %all-reduce.4 = f32[3072]{0:T(1024)S(1)} all-reduce(f32[3072]{0:T(1024)S(1)} %select_maximum_fusion), channel_id=3, replica_groups=mesh['fsdp'=8] {'fsdp'}, use_global_device_ids=true, to_apply=%region_51.52.clone | all-reduce | flops 3072 | bytes 24576
  1306.3 24.4 %all-reduce.5 = (f32[]{:T(128)}, f32[]{:T(128)}) all-reduce(f32[]{:T(128)} %subtract_reduce_fusion, f32[]{:T(128)S(6)} %add.346), channel_id=1, replica_groups=mesh['fsdp'=8] {'fsdp'}, use_global_device_ids=true, to_apply=%region_15.16 | all-reduce | flops 2 | bytes 16 | tf_op jit(solution)/shard_map/psum | solution.py:599
  (306 shorter events, 234.2 us)
Async XLA Ops:
  7.2 1296.1 %reduce-scatter.2.cloned.1.call-start = ((), (), s32[]{:S(2)}) async-start(), calls=%async_computation.1 | async-start | bytes 3538944 | tf_op jit(solution)/shard_map/reduce_scatter | solution.py:595
  414.5 144.8 %copy-start.37 = (f32[768]{0:T(1024)}, f32[768]{0:T(1024)S(1)}, u32[]{:S(2)}) copy-start(f32[768]{0:T(1024)S(1)} %mul.555) | copy-start | bytes 9220
  420.7 81.3 %copy-start.7 = (f32[24,1000]{1,0:T(8,128)}, f32[24,1000]{1,0:T(8,128)S(1)}, u32[]{:S(2)}) copy-start(f32[24,1000]{1,0:T(8,128)S(1)} %get-tuple-element.96) | copy-start | bytes 288004
  435.5 66.5 %copy-start.21 = (f32[24,196]{1,0:T(8,128)S(1)}, f32[24,196]{1,0:T(8,128)}, u32[]{:S(2)}) copy-start(f32[24,196]{1,0:T(8,128)} %copy-done.20) | copy-start | bytes 56452
  968.2 135.8 %copy-start.61 = (f32[768]{0:T(1024)S(1)}, f32[768]{0:T(1024)}, u32[]{:S(2)}) copy-start(f32[768]{0:T(1024)} %get-tuple-element.34) | copy-start | bytes 9220
  968.2 135.8 %copy-start.72 = (f32[3072]{0:T(1024)S(1)}, f32[3072]{0:T(1024)}, u32[]{:S(2)}) copy-start(f32[3072]{0:T(1024)} %get-tuple-element.104) | copy-start | bytes 36868
  968.2 135.8 %copy-start.79 = (f32[196]{0:T(256)S(1)}, f32[196]{0:T(256)}, u32[]{:S(2)}) copy-start(f32[196]{0:T(256)} %get-tuple-element.35) | copy-start | bytes 2356
  968.2 135.8 %copy-start.87 = (f32[768]{0:T(1024)S(1)}, f32[768]{0:T(1024)}, u32[]{:S(2)}) copy-start(f32[768]{0:T(1024)} %get-tuple-element.32) | copy-start | bytes 9220
  968.2 135.8 %copy-start.88 = (f32[768]{0:T(1024)S(1)}, f32[768]{0:T(1024)}, u32[]{:S(2)}) copy-start(f32[768]{0:T(1024)} %get-tuple-element.43) | copy-start | bytes 9220
  968.3 137.4 %copy-start.17 = (f32[24,196]{1,0:T(8,128)S(1)}, f32[24,196]{1,0:T(8,128)}, u32[]{:S(2)}) copy-start(f32[24,196]{1,0:T(8,128)} %copy-done.15) | copy-start | bytes 56452
  968.3 137.4 %copy-start.41 = (f32[24,196]{1,0:T(8,128)S(1)}, f32[24,196]{1,0:T(8,128)}, u32[]{:S(2)}) copy-start(f32[24,196]{1,0:T(8,128)} %copy-done.39) | copy-start | bytes 56452
  968.3 137.4 %copy-start.56 = (f32[768]{0:T(1024)S(1)}, f32[768]{0:T(1024)}, u32[]{:S(2)}) copy-start(f32[768]{0:T(1024)} %copy-done.54) | copy-start | bytes 9220
  968.3 137.4 %copy-start.81 = (f32[768]{0:T(1024)S(1)}, f32[768]{0:T(1024)}, u32[]{:S(2)}) copy-start(f32[768]{0:T(1024)} %copy-done.80) | copy-start | bytes 9220
  1139.0 137.4 %copy-start.8 = (f32[24,1000]{1,0:T(8,128)S(1)}, f32[24,1000]{1,0:T(8,128)}, u32[]{:S(2)}) copy-start(f32[24,1000]{1,0:T(8,128)} %copy-done.7) | copy-start | bytes 288004
  1139.0 137.4 %copy-start.75 = (s32[24]{0:T(128)S(1)}, s32[24]{0:T(128)}, u32[]{:S(2)}) copy-start(s32[24]{0:T(128)} %param.12) | copy-start | bytes 292
  1139.0 137.4 %copy-start.77 = (f32[24]{0:T(128)S(1)}, f32[24]{0:T(128)}, u32[]{:S(2)}) copy-start(f32[24]{0:T(128)} %copy-done.76) | copy-start | bytes 292
  1139.0 137.6 %copy-start.64 = (f32[768]{0:T(1024)S(1)}, f32[768]{0:T(1024)}, u32[]{:S(2)}) copy-start(f32[768]{0:T(1024)} %get-tuple-element.38) | copy-start | bytes 9220
  1139.0 137.6 %copy-start.65 = (f32[768]{0:T(1024)S(1)}, f32[768]{0:T(1024)}, u32[]{:S(2)}) copy-start(f32[768]{0:T(1024)} %get-tuple-element.48) | copy-start | bytes 9220
  1139.0 193.1 %copy-start.73 = (f32[384]{0:T(512)S(1)}, f32[384]{0:T(512)}, u32[]{:S(2)}) copy-start(f32[384]{0:T(512)} %param.15) | copy-start | bytes 4612
  1139.0 193.1 %copy-start.95 = (f32[384]{0:T(512)S(1)}, f32[384]{0:T(512)}, u32[]{:S(2)}) copy-start(f32[384]{0:T(512)} %param.18) | copy-start | bytes 4612
  1139.0 193.1 %copy-start.96 = (f32[384]{0:T(512)S(1)}, f32[384]{0:T(512)}, u32[]{:S(2)}) copy-start(f32[384]{0:T(512)} %param.21) | copy-start | bytes 4612
  1269.1 77.8 %copy-start.9 = (f32[96,1000]{1,0:T(8,128)S(1)}, f32[96,1000]{1,0:T(8,128)}, u32[]{:S(2)}) copy-start(f32[96,1000]{1,0:T(8,128)} %head_ref.1) | copy-start | bytes 1152004
  1269.1 77.8 %copy-start.13 = (f32[96,1000]{1,0:T(8,128)S(1)}, f32[96,1000]{1,0:T(8,128)}, u32[]{:S(2)}) copy-start(f32[96,1000]{1,0:T(8,128)} %param.17) | copy-start | bytes 1152004
  1269.1 77.8 %copy-start.14 = (f32[96,1000]{1,0:T(8,128)S(1)}, f32[96,1000]{1,0:T(8,128)}, u32[]{:S(2)}) copy-start(f32[96,1000]{1,0:T(8,128)} %param.20) | copy-start | bytes 1152004
  (85 other events, 2632.2 us)
Sparse Core Ops, SparseCore 0:
  423.4 39.7 reduce-scatter.1

commit v2 on v0

v2 whole, which is shorter than its diff:
```python
import functools
import math

import jax
import jax.numpy as jnp
from jax import lax
from jax.experimental import pallas as pl
from jax.experimental.pallas import tpu as pltpu
from jax.sharding import PartitionSpec as P

F32, BF16 = jnp.float32, jnp.bfloat16
ZERO = 0
ONE = 1
TWO = 2
THREE = 3
FOUR = 4
FIVE = 5
SIX = 6
EIGHT = 8
SIXTEEN = 16
LANES = 128
TWO_TILES = 256
SEVEN = 7
LN_EPS = 1e-6
LEARN_RATE = 0.003
BETA_ONE = 0.9
BETA_TWO = 0.999
ADAM_EPS = 1e-8
WEIGHT_DECAY = 0.03
ADAM_STEP = 10

NDEV = EIGHT
TOK, CH, TH, HID, NCLS = 196, 768, 384, 3072, 1000
SH = 4763
T1 = TWO * TOK * TH // LANES
RW = CH * HID // LANES
C1, C2 = HID // LANES, CH // LANES
VEC0 = T1 + TWO * RW - SEVEN * SH
MARG = 384
GROUP = FOUR
GR = GROUP * TOK
ROWS = 24 * TOK
WIN = 208
MESH = pl.DeviceIdType.MESH
ANY = pl.BlockSpec(memory_space=pl.ANY)
VMEM = pl.BlockSpec(memory_space=pltpu.VMEM)


def c1_span(d):
    return max(ZERO, SH * d - T1), min(RW, SH * (d + ONE) - T1)


def c2_span(d):
    return max(ZERO, SH * d - T1 - RW), min(RW, SH * (d + ONE) - T1 - RW)


def tiles_of(span, per):
    lo, hi = span
    if lo >= hi:
        return ZERO, ZERO
    return lo // per, -(-hi // per)


def edges(span_of, per):
    out = []
    for d in range(NDEV):
        lo, hi = span_of(d)
        if lo < hi and lo > ZERO and lo % per:
            out.append((d, lo // per, lo % per))
    return out


EDGE1 = edges(c1_span, SIXTEEN * C1)
EDGE2 = edges(c2_span, SIXTEEN * C2)


def matrix_moves(d, s1, s2, w1, w2, e1, e2):
    out = []
    for span_of, per, s, w, e, eds in ((c1_span, SIXTEEN * C1, s1, w1, e1, EDGE1), (c2_span, SIXTEEN * C2, s2, w2, e2, EDGE2)):
        lo, hi = tiles_of(span_of(d), per)
        if lo == hi:
            continue
        first = lo
        for k, (owner, row, _) in enumerate(eds):
            if owner == d:
                out.append((s.at[pl.ds(ZERO, SIXTEEN)], e.at[k]))
                first = lo + ONE
        n = hi - first
        out.append((s.at[pl.ds(SIXTEEN * (first - lo), SIXTEEN * n)], w.at[pl.ds(SIXTEEN * first, SIXTEEN * n)]))
    return out


def entry_barrier(me):
    barrier = pltpu.get_barrier_semaphore()
    for rel in (ONE, TWO, FOUR, SIX):
        pl.semaphore_signal(barrier, inc=ONE, device_id=(peer(me, rel),), device_id_type=MESH)
    pl.semaphore_wait(barrier, FOUR)


def peer(me, rel):
    t = me
    if rel & ONE:
        t = t + ONE - TWO * lax.rem(me, TWO)
    if rel & TWO:
        t = t + TWO - FOUR * lax.rem(me // TWO, TWO)
    if rel & FOUR:
        t = t + FOUR - EIGHT * (me // FOUR)
    return t


RELS = (TWO, FOUR, SIX)


class Spread:
    def __init__(self, pieces, send_sem, recv_sem, fwd_sem):
        self.pieces, self.send_sem, self.recv_sem, self.fwd_sem = pieces, send_sem, recv_sem, fwd_sem
        self.me = lax.axis_index("fsdp")

    def copies(self, d, k, rel):
        return [pltpu.make_async_remote_copy(src_ref=a, dst_ref=b, send_sem=self.send_sem.at[k, i], recv_sem=self.recv_sem.at[d, i], device_id=(d ^ rel,), device_id_type=MESH)
                for i, (a, b) in enumerate(self.pieces(d))]

    def handed(self, s, to):
        return [pltpu.make_async_remote_copy(src_ref=b, dst_ref=b, send_sem=self.fwd_sem.at[s, i], recv_sem=self.recv_sem.at[s, i], device_id=(to,), device_id_type=MESH)
                for i, (_, b) in enumerate(self.pieces(s))]

    def each(self, rels, body):
        for rel in rels:
            for s in range(NDEV):
                if self.pieces(s):
                    pl.when(self.me == s ^ rel)(functools.partial(body, s, rel))

    def start(self):
        def body(d, _):
            for k, rel in enumerate(ORDER):
                for copy in self.copies(d, k, rel):
                    copy.start()
        self.each((ZERO,), body)

    def hand_on(self, rels):
        def body(s, rel):
            for copy in self.handed(s, s ^ rel ^ ONE):
                copy.wait_recv()
            for copy in self.handed(s, s ^ rel ^ ONE):
                copy.start()
        self.each(rels, body)

    def arrive(self):
        def body(s, rel):
            for copy in self.handed(s, s):
                copy.wait_recv()
        self.each((ONE, THREE, FIVE, SEVEN), body)

    def sent(self):
        def own(d, _):
            for k, rel in enumerate(ORDER):
                for copy in self.copies(d, k, rel):
                    copy.wait_send()
        self.each((ZERO,), own)

        def other(s, rel):
            for copy in self.handed(s, s ^ rel ^ ONE):
                copy.wait_send()
        self.each(RELS, other)


ORDER = (FOUR, TWO, SIX, ONE)


def merge_edges(w1, w2, e1, e2, m1, m2, sem):
    jobs = [(k, per, w.at[pl.ds(SIXTEEN * row, SIXTEEN)], e.at[k], m, below)
            for per, w, e, m, eds in ((C1, w1, e1, m1, EDGE1), (C2, w2, e2, m2, EDGE2)) for k, (_, row, below) in enumerate(eds)]
    loads = [pltpu.make_async_copy(src, m.at[i, k], sem.at[i, n]) for n, (k, _, w, e, m, _) in enumerate(jobs) for i, src in enumerate((w, e))]
    stores = [pltpu.make_async_copy(m.at[ZERO, k], w, sem.at[ZERO, n]) for n, (k, _, w, e, m, _) in enumerate(jobs)]
    for copy in loads:
        copy.start()
    for copy in loads:
        copy.wait()
    for k, per, _, _, m, below in jobs:
        shape = (SIXTEEN, LANES * per)
        pos = lax.broadcasted_iota(jnp.int32, shape, ZERO) * per + lax.broadcasted_iota(jnp.int32, shape, ONE) // LANES
        m[ZERO, k] = jnp.where(pos < below, m[ZERO, k].astype(F32), m[ONE, k].astype(F32)).astype(BF16)
    for copy in stores:
        copy.start()
    for copy in stores:
        copy.wait()


def edge_scratch():
    return [pltpu.VMEM((TWO, len(EDGE1), SIXTEEN, HID), BF16), pltpu.VMEM((TWO, len(EDGE2), SIXTEEN, CH), BF16), pltpu.SemaphoreType.DMA((TWO, len(EDGE1) + len(EDGE2)))]


def spread_sems(n):
    dma = pltpu.SemaphoreType.DMA
    return [dma((len(ORDER), n)), dma((NDEV, n)), dma((NDEV, n))]


def lay_token_weights(tok, flat, nat, wt1s, wt2s, wt1t, wt2t):
    flat[ZERO:T1, :] = tok[...].astype(F32)
    period = LANES * TOK // math.gcd(LANES, TOK)
    nrow, npos = period // LANES, period // TOK
    reps = TH // npos
    lane = lax.broadcasted_iota(jnp.int32, (reps, LANES), ONE)
    for j in range(npos):
        f, o = divmod(TOK * j, LANES)
        rows = [flat[pl.ds(T1 // TWO + f + i, reps, stride=nrow), :] for i in range(THREE)]
        for i in range(TWO):
            part = jnp.where(lane >= o, rows[i], rows[i + ONE])
            nat[i, pl.ds(j, reps, stride=npos), :] = pltpu.roll(part, (LANES - o) % LANES, axis=ONE) if o else part
    two_t = jnp.concatenate([nat[ZERO].T, nat[ONE].T], axis=ZERO)
    for i in range(GROUP):
        for s, t, ref_n in ((wt2t, wt2s, two_t), (wt1s, wt1t, None)):
            flat[T1:T1 + WIN, :] = jnp.zeros((WIN, LANES), F32)
            for c in range(TH // LANES):
                lanes_ = slice(LANES * c, LANES * c + LANES)
                part = flat[pl.ds(c, TOK, stride=TH // LANES), :] if ref_n is None else ref_n[ZERO:TOK, lanes_]
                flat[T1 + FOUR * i:T1 + FOUR * i + TOK, :] = part
                full = flat[T1:T1 + WIN, :]
                s[i, :, lanes_] = full.astype(BF16)
                t[i, lanes_, :] = full.T.astype(BF16)


def lay_bias_vectors(vec, vf, bt1, bt2, cv, b1):
    vf[...] = vec[...].astype(F32)

    def put(ref, row, first, n, src):
        for c in range(n // LANES):
            ref[row:row + ONE, LANES * c:LANES * c + LANES] = src[first + c:first + c + ONE, :]

    ng, nt = CH // LANES, TH // LANES
    put(cv, ZERO, ZERO, CH, vf)
    put(cv, ONE, ng, CH, vf)
    for c in range(nt):
        bt1[LANES * c:LANES * c + LANES, :] = jnp.broadcast_to(vf[TWO * ng + c:TWO * ng + c + ONE, :], (LANES, LANES)).T
    at = TWO * ng + nt
    cols = [jnp.broadcast_to(vf[at + i:at + i + ONE, :], (LANES, LANES)).T for i in range(TWO)]
    cut = TOK - LANES
    for i in range(GROUP):
        bt2[i] = jnp.zeros((WIN, LANES), F32)
        bt2[i, FOUR * i:FOUR * i + LANES, :] = cols[ZERO]
        bt2[i, FOUR * i + LANES:FOUR * i + TOK, :] = cols[ONE][ZERO:cut, :]
    n = vf.shape[ZERO] - at - TWO
    lane = lax.broadcasted_iota(jnp.int32, (n, LANES), ONE)
    rest = pltpu.roll(jnp.where(lane >= cut, vf[at + ONE:at + ONE + n, :], vf[at + TWO:at + TWO + n, :]), LANES - cut, axis=ONE)
    vf[ZERO:n, :] = rest
    put(cv, TWO, ZERO, CH, vf)
    put(cv, THREE, ng, CH, vf)
    put(b1, ZERO, TWO * ng, HID, vf)
    put(cv, FOUR, TWO * ng + HID // LANES, CH, vf)


def gather_kernel(p_ref, head_ref, small_ref, w1, w2, st1, st2, headf, *rest):
    (tw0, tw1, (fv, hb)), rest = (rest[ZERO:EIGHT], rest[EIGHT:SIXTEEN], rest[SIXTEEN:18]), rest[18:]
    (e1, e2, xs, s1, s2, stok, svec, shead, ssmall, tok, vec, smallf, flat, nat, vf, m1, m2, ed_sem, ld_sem, stage_sem, own_sem), rest = rest[:21], rest[21:]
    me = lax.axis_index("fsdp")
    loads = [pltpu.make_async_copy(p_ref.at[:, l, :], xs.at[l, pl.ds(MARG, SH)], ld_sem.at[l]) for l in range(TWO)]
    for copy in loads:
        copy.start()
    shead[...] = head_ref[...].astype(BF16)
    ssmall[...] = small_ref[...].astype(BF16).astype(F32)

    def early(d):
        out = [(ssmall, smallf.at[d])]
        if d == ZERO:
            out += [(stok.at[l], tok.at[l]) for l in range(TWO)]
        if d == NDEV - ONE:
            out += [(svec.at[l], vec.at[l]) for l in range(TWO)]
        return out

    def matrices(d):
        return matrix_moves(d, s1.at[ZERO], s2.at[ZERO], w1, w2, e1, e2)

    def classes(d):
        return [(shead, headf.at[pl.ds(HROWS * d, HROWS)])]

    jobs = [Spread(f, *rest[THREE * i:THREE * i + THREE]) for i, f in enumerate((early, matrices, classes))]

    def keep_own(d, _):
        return [pltpu.make_async_copy(a, b, own_sem.at[i]) for i, (a, b) in enumerate(matrices(d) + classes(d))]

    for copy in loads:
        copy.wait()

    @pl.when(me == ZERO)
    def _():
        stok[...] = xs[:, MARG:MARG + T1, :].astype(BF16)
        tok[...] = stok[...]

    @pl.when(me == NDEV - ONE)
    def _():
        svec[...] = xs[:, MARG + VEC0:MARG + SH, :].astype(BF16)
        vec[...] = svec[...]

    entry_barrier(me)
    jobs[ZERO].start()

    def tile(l):
        def body(d, _):
            for span_of, per, s, skip in ((c1_span, C1, s1, T1 if d == ZERO else ZERO), (c2_span, C2, s2, max(ZERO, c1_span(d)[ONE] - c1_span(d)[ZERO]))):
                lo, hi = tiles_of(span_of(d), SIXTEEN * per)
                base0 = SIXTEEN * per * lo - span_of(d)[ZERO] + MARG + skip

                def one(i, carry, per=per, s=s, base0=base0):
                    row = pl.multiple_of(i * SIXTEEN, SIXTEEN)
                    for c in range(per):
                        s[l, pl.ds(row, SIXTEEN), LANES * c:LANES * c + LANES] = xs[l, pl.ds(base0 + c + i * (SIXTEEN * per), SIXTEEN, stride=per), :].astype(BF16)
                    return carry

                if lo < hi:
                    lax.fori_loop(ZERO, hi - lo, one, ZERO)
        jobs[ZERO].each((ZERO,), body)

    tile(ZERO)
    jobs[ONE].start()
    jobs[TWO].start()
    for d in range(NDEV):
        @pl.when(me == d)
        def _():
            smallf[d] = ssmall[...]
            for copy in keep_own(d, ZERO):
                copy.start()
    tile(ONE)
    stage = [pltpu.make_async_copy(a.at[ONE], b, stage_sem.at[i]) for i, (a, b) in enumerate(((s1, st1), (s2, st2)))]
    for copy in stage:
        copy.start()
    jobs[ZERO].hand_on(RELS)
    jobs[ZERO].arrive()
    for l, (wt1s, wt2s, wt1t, wt2t, bt1, bt2, cv, b1) in enumerate((tw0, tw1)):
        lay_token_weights(tok.at[l], flat, nat, wt1s, wt2s, wt1t, wt2t)
        lay_bias_vectors(vec.at[l], vf, bt1, bt2, cv, b1)
    for d in range(NDEV):
        flat[THREE * d:THREE * d + THREE, :] = smallf[d, ZERO:THREE, :]
    for i in range(TWO):
        for c in range(CH // LANES):
            fv[i:i + ONE, LANES * c:LANES * c + LANES] = flat[C2 * i + c:C2 * i + c + ONE, :]
    for c in range(NCP // LANES):
        hb[ZERO:ONE, LANES * c:LANES * c + LANES] = flat[TWO * C2 + c:TWO * C2 + c + ONE, :]
    for rel in ORDER[:THREE]:
        jobs[ONE].hand_on((rel,))
    jobs[TWO].hand_on(RELS)
    jobs[ONE].arrive()
    jobs[TWO].arrive()
    for job in jobs:
        job.sent()
    for d in range(NDEV):
        @pl.when(me == d)
        def _():
            for copy in keep_own(d, ZERO):
                copy.wait()
    merge_edges(w1, w2, e1, e2, m1, m2, ed_sem)
    for copy in stage:
        copy.wait()


STAGE1 = max(SIXTEEN * (b - a) for a, b in (tiles_of(c1_span(d), SIXTEEN * C1) for d in range(NDEV)))
STAGE2 = max(SIXTEEN * (b - a) for a, b in (tiles_of(c2_span(d), SIXTEEN * C2) for d in range(NDEV)))


def gather_all(p_view, head_w, small8):
    sds = jax.ShapeDtypeStruct
    per_layer = [sds((GROUP, WIN, TH), BF16), sds((GROUP, TH, WIN), BF16), sds((GROUP, TH, WIN), BF16), sds((GROUP, WIN, TH), BF16),
                 sds((TH, LANES), F32), sds((GROUP, WIN, LANES), F32), sds((EIGHT, CH), F32), sds((EIGHT, HID), F32)]
    far = [sds((CH, HID), BF16), sds((HID, CH), BF16), sds((STAGE1, HID), BF16), sds((STAGE2, CH), BF16), sds((CH, NCLS), BF16)]
    near = per_layer * TWO + [sds((EIGHT, CH), F32), sds((EIGHT, NCP), F32)]
    edge = [sds((len(EDGE1), SIXTEEN, HID), BF16), sds((len(EDGE2), SIXTEEN, CH), BF16)]
    dma = pltpu.SemaphoreType.DMA
    nv = SH - VEC0
    outs = pl.pallas_call(
        gather_kernel,
        in_specs=[ANY, VMEM, VMEM],
        out_specs=[ANY] * len(far) + [VMEM] * len(near) + [ANY] * TWO,
        out_shape=far + near + edge,
        scratch_shapes=[pltpu.VMEM((TWO, SH + TWO * MARG + FIVE, LANES), F32), pltpu.VMEM((TWO, STAGE1, HID), BF16), pltpu.VMEM((TWO, STAGE2, CH), BF16),
                        pltpu.VMEM((TWO, T1, LANES), BF16), pltpu.VMEM((TWO, nv, LANES), BF16), pltpu.VMEM((HROWS, NCLS), BF16), pltpu.VMEM((EIGHT, LANES), F32),
                        pltpu.VMEM((TWO, T1, LANES), BF16), pltpu.VMEM((TWO, nv, LANES), BF16), pltpu.VMEM((NDEV, EIGHT, LANES), F32),
                        pltpu.VMEM((T1 + WIN + EIGHT, LANES), F32), pltpu.VMEM((TWO, TH, LANES), F32), pltpu.VMEM((nv, LANES), F32)] + edge_scratch()
        + [dma((TWO,)), dma((TWO,)), dma((SIX,))] + spread_sems(THREE) + spread_sems(FOUR) + spread_sems(ONE),
        compiler_params=pltpu.CompilerParams(collective_id=ZERO, has_side_effects=True, vmem_limit_bytes=60000000),
        name="gather_weights",
    )(p_view, head_w, small8)
    n = len(far)
    return outs[:n], outs[n:n + EIGHT], outs[n + EIGHT:n + SIXTEEN], outs[n + SIXTEEN:n + 18]


def g1_rows(d):
    lo, hi = tiles_of(c1_span(d), EIGHT * C1)
    return EIGHT * lo, EIGHT * hi


def g2_rows(d):
    lo, hi = tiles_of(c2_span(d), EIGHT * C2)
    return EIGHT * lo, EIGHT * hi


QUART = HID // CH
HALF = CH // TWO
BLK = max(QUART * (g1_rows(d)[ONE] - g1_rows(d)[ZERO]) + g2_rows(d)[ONE] - g2_rows(d)[ZERO] for d in range(NDEV))


def core_rows(s):
    lo, hi = g1_rows(s)
    return QUART * (hi - lo) + g2_rows(s)[ONE] - g2_rows(s)[ZERO]


def share_pieces(s, dw1, dw2, tok=None, vec=None):
    lo, hi = g1_rows(s)
    full = pl.ds(ZERO, CH)
    out = [(dw1.at[q, pl.ds(lo, hi - lo)], pl.ds(q * (hi - lo), hi - lo), full) for q in range(QUART) if lo < hi]
    at = QUART * (hi - lo)
    lo, hi = g2_rows(s)
    if lo < hi:
        out.append((dw2.at[pl.ds(lo, hi - lo)], pl.ds(at, hi - lo), full))
    if tok is not None and s == ZERO:
        out.append((tok, pl.ds(core_rows(s), TROWS), full))
    if vec is not None and s == NDEV - ONE:
        out.append((vec, pl.ds(core_rows(s), VROWS), full))
    return list(enumerate(out))


NCP = 1024
HROWS = CH // NDEV
TROWS, VROWS = 200, SIXTEEN


def add_into(dst, src, n):
    def one(i, carry):
        at = pl.ds(pl.multiple_of(i * SIXTEEN, SIXTEEN), SIXTEEN)
        dst[at, :] = dst[at, :] + src[at, :]
        return carry
    lax.fori_loop(ZERO, n // SIXTEEN, one, ZERO)


class Reduction:
    def __init__(self, given, red, sums, own, ld, ps, pr, hs, hr, out_sem, free):
        self.given, self.red, self.sums, self.own, self.free = given, red, sums, own, free
        self.n = red.shape[ONE]
        self.ld, self.ps, self.pr, self.hs, self.hr, self.out_sem = ld, ps, pr, hs, hr, out_sem
        self.me = lax.axis_index("fsdp")
        chip = self.me // TWO
        px, py = lax.rem(chip, TWO), chip // TWO
        self.k, self.kx, self.ky = chip, chip + ONE - TWO * px, chip + TWO - FOUR * py
        self.kd = self.kx + TWO - FOUR * py

    def per_core(self, body):
        for c in range(TWO):
            @pl.when(lax.rem(self.me, TWO) == c)
            def _():
                body(c)

    def load(self, k, c):
        return [pltpu.make_async_copy(src, self.own.at[k % TWO, rows, lanes_], self.ld.at[k % TWO, i]) for i, (src, rows, lanes_) in share_pieces(TWO * k + c, *self.given)]

    def give(self, k, c):
        return [pltpu.make_async_remote_copy(src_ref=src, dst_ref=self.sums.at[k, rows, lanes_], send_sem=self.ps.at[k, i], recv_sem=self.pr.at[k, i], device_id=(peer(self.me, ONE),), device_id_type=MESH)
                for i, (src, rows, lanes_) in share_pieces(TWO * k + c, *self.given)]

    def hop(self, i, src, dst, rel):
        return pltpu.make_async_remote_copy(src_ref=src, dst_ref=dst, send_sem=self.hs.at[i], recv_sem=self.hr.at[i], device_id=(peer(self.me, rel),), device_id_type=MESH)

    def left(self, ref, k):
        return ref.at[k, :, pl.ds(ZERO, HALF)]

    def right(self, ref, k):
        return ref.at[k, :, pl.ds(HALF, HALF)]

    def ready(self, i):
        for rel in (TWO, FOUR):
            pl.semaphore_signal(self.free.at[i], inc=ONE, device_id=(peer(self.me, rel),), device_id_type=MESH)
        pl.semaphore_wait(self.free.at[i], TWO)

    def first_hops(self):
        return [self.hop(ZERO, self.left(self.sums, self.kx), self.left(self.own, ZERO), TWO), self.hop(ONE, self.left(self.sums, self.kd), self.left(self.own, ONE), TWO),
                self.hop(TWO, self.right(self.sums, self.ky), self.right(self.own, ZERO), FOUR), self.hop(THREE, self.right(self.sums, self.kd), self.right(self.own, ONE), FOUR)]

    def begin(self):
        barrier = pltpu.get_barrier_semaphore()
        for rel in (ONE, TWO, FOUR):
            pl.semaphore_signal(barrier, inc=ONE, device_id=(peer(self.me, rel),), device_id_type=MESH)
        pl.semaphore_wait(barrier, THREE)

        def body(c):
            for k in range(FOUR):
                for copy in self.give(k, ONE - c):
                    copy.start()
            for k in range(TWO):
                for copy in self.load(k, c):
                    copy.start()
        self.per_core(body)

    def partner_done(self):
        for k in range(FOUR):
            def wait(c):
                for copy in self.load(k, c):
                    copy.wait()
                for copy in self.give(k, c):
                    copy.wait_recv()
            self.per_core(wait)
            add_into(self.sums.at[k], self.own.at[k % TWO], self.n)
            if k < TWO:
                def more(c):
                    for copy in self.load(k + TWO, c):
                        copy.start()
                self.per_core(more)
        self.ready(ZERO)
        for copy in self.first_hops():
            copy.start()

    def first_done(self):
        for copy in self.first_hops():
            copy.wait_recv()
        add_into(self.sums.at[self.k], self.own.at[ZERO], self.n)
        add_into(self.left(self.sums, self.ky), self.left(self.own, ONE), self.n)
        add_into(self.right(self.sums, self.kx), self.right(self.own, ONE), self.n)
        outs = self.outputs()
        for copy in outs:
            copy.start()

    def outputs(self):
        own, left, right = self.red.at[ZERO], self.red.at[ONE, :, pl.ds(ZERO, HALF)], self.red.at[ONE, :, pl.ds(HALF, HALF)]
        pairs = (self.sums.at[self.k], own), (self.left(self.sums, self.ky), left), (self.right(self.sums, self.kx), right)
        return [pltpu.make_async_copy(a, b, self.out_sem.at[i]) for i, (a, b) in enumerate(pairs)]

    def finish(self):
        for copy in self.first_hops():
            copy.wait_send()

        def body(c):
            for k in range(FOUR):
                for copy in self.give(k, ONE - c):
                    copy.wait_send()
        self.per_core(body)
        for copy in self.outputs():
            copy.wait()


def last_hops(red, late, send, recv, me):
    out = []
    for i, rel in enumerate((FOUR, TWO)):
        part = pl.ds(HALF * i, HALF)
        out.append(pltpu.make_async_remote_copy(src_ref=red.at[ONE, :, part], dst_ref=late.at[:, part], send_sem=send.at[i], recv_sem=recv.at[i], device_id=(peer(me, rel),), device_id_type=MESH))
    return out


def reduction_scratch(n):
    dma = pltpu.SemaphoreType.DMA
    pieces = QUART + TWO
    return [pltpu.VMEM((FOUR, n, CH), F32), pltpu.VMEM((TWO, n, CH), F32),
            dma((TWO, pieces)), dma((FOUR, pieces)), dma((FOUR, pieces)), dma((FOUR,)), dma((FOUR,)), dma((THREE,)), pltpu.SemaphoreType.REGULAR((ONE,))]


def untile(block, flat, d):
    lo, hi = g1_rows(d)
    n1 = hi - lo
    jobs = [(q * n1, n1, C1, C1 * lo - c1_span(d)[ZERO] + (T1 if d == ZERO else ZERO) + C2 * q) for q in range(QUART) if n1]
    lo, hi = g2_rows(d)
    if lo < hi:
        jobs.append((QUART * n1, hi - lo, C2, C2 * lo - c2_span(d)[ZERO] + max(ZERO, c1_span(d)[ONE] - c1_span(d)[ZERO])))
    for at, n, stride, base in jobs:
        def one(i, carry, at=at, stride=stride, base=base):
            rows = pl.ds(pl.multiple_of(at + EIGHT * i, EIGHT), EIGHT)
            for c in range(C2):
                flat[pl.ds(MARG + base + c + i * (EIGHT * stride), EIGHT, stride=stride), :] = block[rows, LANES * c:LANES * c + LANES]
            return carry
        lax.fori_loop(ZERO, n // EIGHT, one, ZERO)


def adam_math(p, g, m, v, decay):
    m_new = BETA_ONE * m + (1.0 - BETA_ONE) * g
    v_new = BETA_TWO * v + (1.0 - BETA_TWO) * g * g
    m_hat = m_new / (1.0 - BETA_ONE ** ADAM_STEP)
    v_hat = v_new / (1.0 - BETA_TWO ** ADAM_STEP)
    p_new = p - LEARN_RATE * (m_hat / (jnp.sqrt(v_hat) + ADAM_EPS) + decay * p)
    return p_new, m_new, v_new


NVIEW = 40
CHUNK = 1200
NCHUNK = FOUR
GROWS = CHUNK * NCHUNK
EXR = 32
LOSS_ROW = 24


def chunk_rows(k):
    return k * CHUNK, min(SH, (k + ONE) * CHUNK) - k * CHUNK


def lay_tokens(blk, r0, flat, flip, ta, tb):
    for c in range(TH // LANES):
        flat[pl.ds(MARG + c, TOK, stride=TH // LANES), :] = blk[r0:r0 + TOK, LANES * c:LANES * c + LANES]
    flip[:, ZERO:TROWS] = blk[r0:r0 + TROWS, TH:TWO * TH].T
    ta[ZERO:TH, :] = flip[:, ZERO:LANES]
    tb[ZERO:TH, :] = flip[:, LANES:TWO_TILES]
    period = LANES * TOK // math.gcd(LANES, TOK)
    nrow, npos = period // LANES, period // TOK
    reps = TH // npos
    lane = lax.broadcasted_iota(jnp.int32, (reps, LANES), ONE)
    for m in range(nrow):
        j, o = divmod(LANES * m, TOK)
        first = ta[pl.ds(j, reps, stride=npos), :]
        second = tb[pl.ds(j, reps, stride=npos), :]
        if o < LANES:
            row = pltpu.roll(jnp.where(lane >= o, first, second), (LANES - o) % LANES, axis=ONE) if o else first
        else:
            row = pltpu.roll(second, (TWO_TILES - o) % LANES, axis=ONE) if o > LANES else second
        if TOK - o < LANES:
            following = ta[pl.ds(j + ONE, reps, stride=npos), :]
            row = jnp.where(lane < TOK - o, row, pltpu.roll(following, TOK - o, axis=ONE))
        flat[pl.ds(MARG + T1 // TWO + m, reps, stride=nrow), :] = row


def lay_vectors(blk, r0, flat, va, vb):
    at = MARG + VEC0

    def pieces(row, n):
        return [blk[r0 + row:r0 + row + ONE, LANES * c:LANES * c + LANES] for c in range(n // LANES)]

    b_t2 = pieces(VROWS - SIX, TWO_TILES)
    plain = pieces(ZERO, CH) + pieces(ONE, CH) + pieces(9, TH) + b_t2[:ONE]
    for i, v in enumerate(plain):
        flat[at + i:at + i + ONE, :] = v
    moved = pieces(TWO, CH) + pieces(THREE, CH) + sum([pieces(FIVE + q, CH) for q in range(QUART)], []) + pieces(FOUR, CH)
    va[...] = jnp.zeros(va.shape, F32)
    for i, v in enumerate(moved):
        va[i:i + ONE, :] = v
    cut = TOK - LANES
    vb[ZERO:EIGHT, :] = jnp.broadcast_to(b_t2[ONE], (EIGHT, LANES))
    vb[EIGHT:EIGHT + va.shape[ZERO], :] = pltpu.roll(va[...], cut, axis=ONE)
    n = SH - VEC0 - len(plain)
    lane = lax.broadcasted_iota(jnp.int32, (n, LANES), ONE)
    flat[at + len(plain):MARG + SH, :] = jnp.where(lane < cut, vb[SEVEN:SEVEN + n, :], vb[EIGHT:EIGHT + n, :])


def finish_kernel(red0, red1, late1, heads, tok_ref, vec_ref, ex_ref, g_out, gh_out, gsm_out, loss_ref,
                  gs, r0, r1, l0, l1, tsum, tgot, vsum, vgot, ex, nrm, flip, ta, tb, va, vb, hparts,
                  g_sem, head_sem, red_sem, pair_s, pair_r, own_s, own_r, ex_s, ex_r, nm_s, nm_r, hop_s, hop_r):
    me = lax.axis_index("fsdp")
    core = lax.rem(me, TWO)
    others = [lax.rem(me + i, NDEV) for i in range(ONE, NDEV)]
    reds = [pltpu.make_async_copy(a, b, red_sem.at[i]) for i, (a, b) in enumerate(((red1.at[ZERO], r1), (late1, l1), (red0.at[ZERO], r0)))]
    heads_in = pltpu.make_async_copy(heads, hparts, head_sem)
    for copy in reds + [heads_in]:
        copy.start()
    ex[ZERO] = ex_ref[...]
    barrier = pltpu.get_barrier_semaphore()
    for dev in others:
        pl.semaphore_signal(barrier, inc=ONE, device_id=(dev,), device_id_type=MESH)
    pl.semaphore_wait(barrier, NDEV - ONE)

    def remote(src, dst, ss, rs, dev):
        return pltpu.make_async_remote_copy(src_ref=src, dst_ref=dst, send_sem=ss, recv_sem=rs, device_id=(dev,), device_id_type=MESH)

    give_tok = remote(tok_ref, tgot.at[THREE], pair_s, pair_r, peer(me, ONE))
    give_vec = remote(vec_ref, vgot.at[THREE], pair_s, pair_r, peer(me, ONE))
    pl.when(core == ONE)(give_tok.start)
    pl.when(core == ZERO)(give_vec.start)
    small = [remote(ex.at[ZERO], ex.at[i], ex_s.at[i], ex_r.at[i], others[i - ONE]) for i in range(ONE, NDEV)]
    for copy in small:
        copy.start()

    def to_owner(src, dst, rel, owner):
        slot = rel // TWO - ONE
        return remote(src, dst.at[slot], own_s.at[slot], own_r.at[slot], owner)

    sides = ((ZERO, ZERO, give_tok, tok_ref, tsum, tgot), (ONE, NDEV - ONE, give_vec, vec_ref, vsum, vgot))
    for c, owner, give, mine, total, got in sides:
        @pl.when(core == c)
        def _():
            give.wait_recv()
            total[...] = mine[...] + got[THREE]
            for rel in RELS:
                @pl.when(me == owner ^ rel)
                def _():
                    to_owner(total, got, rel, owner).start()
    hops = last_hops(red0, l0, hop_s, hop_r, me)
    for copy in hops:
        copy.start()
    for copy in reds:
        copy.wait()
    add_into(r1, l1, r1.shape[ZERO])

    def per_device(body):
        for d in range(NDEV):
            @pl.when(me == d)
            def _():
                body(d)

    per_device(lambda d: untile(r1, gs.at[ONE], d))
    heads_in.wait()
    g_head = hparts[ZERO]
    for d in range(ONE, NDEV):
        g_head = g_head + hparts[d]
    gh_out[...] = g_head[:, ZERO:NCLS]
    acc = fold_rows(fold_lanes(g_head * g_head))
    for copy in small:
        copy.wait_recv()
    first = lax.rem(NDEV - me, NDEV)
    tot = ex[first]
    for d in range(ONE, NDEV):
        tot = tot + ex[lax.rem(first + d, NDEV)]
    ta[ZERO:EXR, :] = tot
    loss_ref[...] = tot[LOSS_ROW:LOSS_ROW + EIGHT, :]
    g_small = ta[pl.ds(THREE * me, THREE), :]
    gsm_out[...] = g_small
    acc = acc + jnp.sum(g_small * g_small, axis=ZERO, keepdims=True) / EIGHT
    for c, owner, give, mine, total, got in sides:
        @pl.when(me == owner)
        def _():
            for rel in RELS:
                to_owner(total, got, rel, owner).wait_recv()
            total[...] = total[...] + got[ZERO] + (got[ONE] + got[TWO])
            if c == ZERO:
                lay_tokens(total, ZERO, gs.at[ZERO], flip, ta, tb)
            else:
                lay_vectors(total, ZERO, gs.at[ZERO], va, vb)
    for copy in hops:
        copy.wait_recv()
    add_into(r0, l0, r0.shape[ZERO])

    def rest_of(d):
        untile(r0, gs.at[ZERO], d)
        if d == ZERO:
            lay_tokens(r0, core_rows(ZERO), gs.at[ONE], flip, ta, tb)
        if d == NDEV - ONE:
            lay_vectors(r0, core_rows(NDEV - ONE), gs.at[ONE], va, vb)

    per_device(rest_of)
    flats = [pltpu.make_async_copy(gs.at[l, pl.ds(MARG, SH)], g_out.at[l], g_sem.at[l]) for l in range(TWO)]
    for copy in flats:
        copy.start()

    def square(i, carry):
        for l in range(TWO):
            part = gs[l, pl.ds(pl.multiple_of(MARG + i * NVIEW, EIGHT), NVIEW), :]
            carry = carry + fold_rows(part * part)
        return carry

    whole = SH // NVIEW
    acc = lax.fori_loop(ZERO, whole, square, acc)
    rest = SH - whole * NVIEW
    for l in range(TWO):
        part = gs[l, MARG + SH - rest:MARG + SH, :]
        acc = acc + jnp.sum(part * part, axis=ZERO, keepdims=True) / EIGHT
    nrm[ZERO] = acc
    norms = [remote(nrm.at[ZERO], nrm.at[i], nm_s.at[i], nm_r.at[i], others[i - ONE]) for i in range(ONE, NDEV)]
    for copy in norms:
        copy.start()
    for copy in norms:
        copy.wait_recv()
    tot = nrm[first]
    for d in range(ONE, NDEV):
        tot = tot + nrm[lax.rem(first + d, NDEV)]
    norm = jnp.sqrt(jnp.sum(jnp.sum(tot, axis=ZERO, keepdims=True), axis=ONE, keepdims=True))
    loss_ref[FOUR:EIGHT, :] = jnp.broadcast_to(1.0 / jnp.maximum(1.0, norm), (FOUR, LANES))
    for copy in small + norms + hops:
        copy.wait_send()
    for c, owner, give, mine, total, got in sides:
        pl.when(core != c)(give.wait_send)
        for rel in RELS:
            pl.when(me == owner ^ rel)(to_owner(total, got, rel, owner).wait_send)
    for copy in flats:
        copy.wait()


def finish(red0, red1, late1, heads, tok, vec, ex):
    sds = jax.ShapeDtypeStruct
    dma = pltpu.SemaphoreType.DMA
    blk0, blk1 = pltpu.VMEM(red0.shape[ONE:], F32), pltpu.VMEM(red1.shape[ONE:], F32)
    return pl.pallas_call(
        finish_kernel,
        in_specs=[ANY] * FOUR + [VMEM] * THREE,
        out_specs=[ANY] + [VMEM] * THREE,
        out_shape=[sds((TWO, SH, LANES), F32), sds((HROWS, NCLS), F32), sds((THREE, LANES), F32), sds((EIGHT, LANES), F32)],
        scratch_shapes=[pltpu.VMEM((TWO, GROWS + TWO * MARG, LANES), F32), blk0, blk1, blk0, blk1,
                        pltpu.VMEM((TROWS, CH), F32), pltpu.VMEM((FOUR, TROWS, CH), F32), pltpu.VMEM((VROWS, CH), F32), pltpu.VMEM((FOUR, VROWS, CH), F32),
                        pltpu.VMEM((NDEV, EXR, LANES), F32), pltpu.VMEM((NDEV, EIGHT, LANES), F32), pltpu.VMEM((TH, TWO_TILES), F32),
                        pltpu.VMEM((TH + EIGHT, LANES), F32), pltpu.VMEM((TH + EIGHT, LANES), F32), pltpu.VMEM((48, LANES), F32), pltpu.VMEM((56, LANES), F32), pltpu.VMEM((NDEV, HROWS, NCP), F32),
                        dma((TWO,)), dma, dma((THREE,)), dma, dma, dma((THREE,)), dma((THREE,)), dma((NDEV,)), dma((NDEV,)), dma((NDEV,)), dma((NDEV,)), dma((TWO,)), dma((TWO,))],
        compiler_params=pltpu.CompilerParams(collective_id=THREE, has_side_effects=True, vmem_limit_bytes=67000000),
        name="finish",
    )(red0, red1, late1, heads, tok, vec, ex)


def update_kernel(p_ref, m_ref, v_ref, g_ref, hg_ref, sg_ref, scale_ref, hp_ref, hm_ref, hv_ref, sp_ref, sm_ref, sv_ref,
                  po, mo, vo, hpo, hmo, hvo, spo, smo, svo, ps, ms, vs, gs, in_sem, out_sem):
    me = lax.axis_index("fsdp")
    ins = ((p_ref, ps), (m_ref, ms), (v_ref, vs))
    outs = ((ps, po), (ms, mo), (vs, vo))

    def loads(k):
        a, n = chunk_rows(k)
        rows = pl.ds(a, n)
        return [pltpu.make_async_copy(src.at[rows, l, :], dst.at[l, rows], in_sem.at[k, j, l]) for j, (src, dst) in enumerate(ins) for l in range(TWO)] + [
            pltpu.make_async_copy(g_ref.at[l, rows], gs.at[l, rows], in_sem.at[k, THREE, l]) for l in range(TWO)]

    def stores(k):
        a, n = chunk_rows(k)
        return [pltpu.make_async_copy(src.at[l, pl.ds(a, n)], dst.at[pl.ds(a, n), l, :], out_sem.at[k, j, l]) for j, (src, dst) in enumerate(outs) for l in range(TWO)]

    for k in range(NCHUNK):
        for copy in loads(k):
            copy.start()
    scale = scale_ref[FOUR:FIVE, ZERO:ONE]
    hpo[...], hmo[...], hvo[...] = adam_math(hp_ref[...], hg_ref[...] * scale, hm_ref[...], hv_ref[...], WEIGHT_DECAY)
    spo[...], smo[...], svo[...] = adam_math(sp_ref[...], sg_ref[...] * scale, sm_ref[...], sv_ref[...], 0.0)
    mat_rows = T1 + TWO * RW - me * SH
    for k in range(NCHUNK):
        for copy in loads(k):
            copy.wait()
        a, n = chunk_rows(k)
        for l in range(TWO):
            def one(i, carry, l=l, a=a):
                o = pl.multiple_of(a + i * NVIEW, EIGHT)
                row = o + lax.broadcasted_iota(jnp.int32, (NVIEW, LANES), ZERO)
                decay = jnp.where(row < mat_rows, WEIGHT_DECAY, 0.0)
                at = pl.ds(o, NVIEW)
                ps[l, at, :], ms[l, at, :], vs[l, at, :] = adam_math(ps[l, at, :], gs[l, at, :] * scale, ms[l, at, :], vs[l, at, :], decay)
                return carry
            lax.fori_loop(ZERO, -(-n // NVIEW), one, ZERO)
        for copy in stores(k):
            copy.start()
    for k in range(NCHUNK):
        for copy in stores(k):
            copy.wait()


def update(pv, mv, vv, g, head_g, small_g, scale, heads, smalls):
    sds = jax.ShapeDtypeStruct
    dma = pltpu.SemaphoreType.DMA
    big, hd, sm = sds((SH, TWO, LANES), F32), sds((HROWS, NCLS), F32), sds((THREE, LANES), F32)
    return pl.pallas_call(
        update_kernel,
        in_specs=[ANY] * FOUR + [VMEM] * 9,
        out_specs=[ANY] * THREE + [VMEM] * SIX,
        out_shape=[big] * THREE + [hd] * THREE + [sm] * THREE,
        scratch_shapes=[pltpu.VMEM((TWO, GROWS, LANES), F32)] * FOUR + [dma((NCHUNK, FOUR, TWO)), dma((NCHUNK, THREE, TWO))],
        compiler_params=pltpu.CompilerParams(vmem_limit_bytes=67000000),
        name="update",
    )(pv, mv, vv, g, head_g, small_g, scale, *heads, *smalls)

CG = math.sqrt(2.0 / math.pi)
CA = CG * 0.044715


def mm(a, b):
    return jnp.dot(a, b, preferred_element_type=F32)


def mm_t(a, b):
    return lax.dot_general(a, b, (((ONE,), (ONE,)), ((), ())), preferred_element_type=F32)


def cat6(col):
    return jnp.concatenate([col] * (CH // LANES), axis=ONE)


def norm_stats(x):
    mean = jnp.mean(x, axis=-ONE, keepdims=True)
    cent = x - mean
    rstd = lax.rsqrt(jnp.mean(cent * cent, axis=-ONE, keepdims=True) + LN_EPS)
    return cent * rstd, rstd


def gelu_of(x):
    t = jnp.tanh(x * (CG + CA * (x * x)))
    half = 0.5 * x
    return half + half * t


def gelu_and_grad(x, d):
    u = CA * (x * x)
    q = CG + u
    t = jnp.tanh(x * q)
    s = 1.0 + t
    act = 0.5 * x * s
    return act, d * (0.5 * s + act * (1.0 - t) * (q + (u + u)))


def load_group(x_ref, xf):
    if len(x_ref.shape) == THREE:
        for i in range(GROUP):
            xf[TOK * i:TOK * i + TOK, :] = x_ref[i].astype(F32)
    else:
        xf[...] = x_ref[...].astype(F32)


def forward_kernel(first, x_ref, wt1_ref, wt2_ref, bt1_ref, bt2_ref, w1_ref, w2_ref, cv_ref, b1_ref, *rest):
    if first:
        (st1, st2), rest = rest[:TWO], rest[TWO:]
    (x1_ref, ut_ref, hid_ref, h2_ref, x2_ref), rest = rest[:FIVE], rest[FIVE:]
    if first:
        (flat_ref, nw1, nw2, e1, e2), rest = rest[:FIVE], rest[FIVE:]
    (xf, hs, acts), rest = rest[:THREE], rest[THREE:]
    step = pl.program_id(ZERO)
    if first:
        m1, m2, ed_sem, own_sem, *sems = rest

        def pieces(d):
            return matrix_moves(d, st1, st2, nw1, nw2, e1, e2)

        job = Spread(pieces, *sems)

        def keep_own(act):
            def body(d, _):
                for i, (a, b) in enumerate(pieces(d)):
                    getattr(pltpu.make_async_copy(a, b, own_sem.at[i]), act)()
            job.each((ZERO,), body)

        @pl.when(step == ZERO)
        def _():
            entry_barrier(job.me)
            job.start()
            keep_own("start")

        pl.when(step == ROWS // GR - ONE)(functools.partial(job.hand_on, ORDER[:THREE]))
    load_group(x_ref, xf)
    if first:
        flat_ref[...] = xf[...].astype(BF16)
    nrm, _ = norm_stats(xf[...])
    hs[...] = (nrm * cv_ref[ZERO:ONE, :] + cv_ref[ONE:TWO, :]).astype(BF16)
    for i in range(GROUP):
        lo = 192 * i
        ut = mm(wt1_ref[i], hs[lo:lo + WIN, :]) + cat6(bt1_ref[...])
        ut_ref[i] = ut
        out = mm(wt2_ref[i], gelu_of(ut).astype(BF16)) + cat6(bt2_ref[i])
        xf[lo:lo + WIN, :] = xf[lo:lo + WIN, :] + out
    x1b = xf[...].astype(BF16)
    x1_ref[...] = x1b
    x1 = x1b.astype(F32)
    nrm2, _ = norm_stats(x1)
    h2_ref[...] = (nrm2 * cv_ref[TWO:THREE, :] + cv_ref[THREE:FOUR, :]).astype(BF16)
    for j in range(ZERO, HID, 512):
        hid = mm(h2_ref[...], w1_ref[:, j:j + 512]) + b1_ref[ZERO:ONE, j:j + 512]
        hid_ref[:, j:j + 512] = hid
        acts[:, j:j + 512] = gelu_of(hid).astype(BF16)
    x2_ref[...] = (x1_ref[...].astype(F32) + (mm(acts[...], w2_ref[...]) + cv_ref[FOUR:FIVE, :])).astype(BF16)

    if first:
        @pl.when(step == ROWS // GR - ONE)
        def _():
            job.arrive()
            job.sent()
            keep_own("wait")
            merge_edges(nw1, nw2, e1, e2, m1, m2, ed_sem)


def once(shape):
    return pl.BlockSpec(shape, lambda g: (ZERO,) * len(shape), pipeline_mode=pl.Buffered(ONE))


def by_group(shape):
    return pl.BlockSpec(shape, lambda g: (g,) + (ZERO,) * (len(shape) - ONE))


def forward_layer(x, wt1t, wt2t, bt1, bt2, w1, w2, cv, b1, stage=()):
    sds = jax.ShapeDtypeStruct
    first = x.ndim == THREE
    act = by_group((GR, CH))
    act_s = sds((ROWS, CH), BF16)
    outs = [act, by_group((GROUP, TH, CH)), by_group((GR, HID)), act, act]
    shapes = [act_s, sds((24, TH, CH), F32), sds((ROWS, HID), F32), act_s, act_s]
    scratch = [pltpu.VMEM((GR, CH), F32), pltpu.VMEM((GR, CH), BF16), pltpu.VMEM((GR, HID), BF16)]
    params = {}
    if first:
        outs += [act] + [ANY] * FOUR
        shapes += [act_s, sds((CH, HID), BF16), sds((HID, CH), BF16), sds((len(EDGE1), SIXTEEN, HID), BF16), sds((len(EDGE2), SIXTEEN, CH), BF16)]
        scratch += edge_scratch() + [pltpu.SemaphoreType.DMA((FOUR,))] + spread_sems(FOUR)
        params = {"collective_id": FOUR, "has_side_effects": True}
    return pl.pallas_call(
        functools.partial(forward_kernel, first),
        grid=(ROWS // GR,),
        in_specs=[by_group((GROUP, TOK, CH)) if first else act, once((GROUP, TH, WIN)), once((GROUP, WIN, TH)), once((TH, LANES)), once((GROUP, WIN, LANES)),
                  once((CH, HID)), once((HID, CH)), once((EIGHT, CH)), once((EIGHT, HID))] + [ANY] * len(stage),
        out_specs=outs,
        out_shape=shapes,
        scratch_shapes=scratch,
        compiler_params=pltpu.CompilerParams(vmem_limit_bytes=67000000, **params),
        name="forward_layer",
    )(x, wt1t, wt2t, bt1, bt2, w1, w2, cv, b1, *stage)

def fold_rows(a):
    return jnp.sum(a.reshape(a.shape[ZERO] // EIGHT, EIGHT, a.shape[ONE]), axis=ZERO)


def fold_lanes(a):
    tot = a[:, ZERO:LANES]
    for k in range(ONE, a.shape[ONE] // LANES):
        tot = tot + a[:, LANES * k:LANES * k + LANES]
    return tot


def norm_back(nrm, rstd, gain, d):
    dg = d * gain
    m1 = jnp.mean(dg, axis=-ONE, keepdims=True)
    m2 = jnp.mean(dg * nrm, axis=-ONE, keepdims=True)
    return rstd * (dg - m1 - nrm * m2)


SUB = 112


def backward_kernel(first, dh_ref, d2_ref, x1_ref, x_ref, ut_ref, w1_ref, wt1_ref, wt2_ref, cv_ref, gb1_ref, dw1, dw2, *rest):
    if first:
        tok1, vec1, *rest = rest
        given = dw1, dw2, tok1, vec1
    else:
        dx_ref, *rest = rest
        given = dw1, dw2
    tok_ref, vec_ref, red, gt1_ref, gt2_ref, gbt1_ref, gbt2_ref, gcv_ref, d1b, hs, dhf, acts, dus, *comm = rest
    step = pl.program_id(ZERO)
    job = Reduction(given, red, *comm)
    pl.when(step == ZERO)(job.begin)
    pl.when(step == TWO)(job.partner_done)

    @pl.when(step == ZERO)
    def _():
        for r in (gt1_ref, gt2_ref, gbt1_ref, gbt2_ref, gcv_ref):
            r[...] = jnp.zeros(r.shape, F32)

    def through_w1(c, carry):
        cols = pl.ds(pl.multiple_of(c * TWO_TILES, TWO_TILES), TWO_TILES)
        dhf[:, cols] = mm_t(dh_ref[...], w1_ref[cols, :])
        return carry

    lax.fori_loop(ZERO, CH // TWO_TILES, through_w1, ZERO)

    def norm_two(i, carry):
        rows = pl.ds(pl.multiple_of(i * SUB, SUB), SUB)
        d_n2 = dhf[rows, :].astype(BF16).astype(F32)
        nrm2, rstd2 = norm_stats(x1_ref[rows, :].astype(F32))
        d2 = d2_ref[rows, :].astype(F32)
        for k, part in ((TWO, d_n2 * nrm2), (THREE, d_n2), (FOUR, d2)):
            gcv_ref[k] += fold_rows(part)
        d1 = (norm_back(nrm2, rstd2, cv_ref[TWO:THREE, :], d_n2) + d2).astype(BF16)
        d1b[rows, :] = d1
        gbt2_ref[rows, :] += fold_lanes(d1.astype(F32))
        nrm1, _ = norm_stats(x_ref[rows, :].astype(F32))
        hs[rows, :] = (nrm1 * cv_ref[ZERO:ONE, :] + cv_ref[ONE:TWO, :]).astype(BF16)
        dhf[rows, :] = jnp.zeros((SUB, CH), F32)
        return carry

    lax.fori_loop(ZERO, GR // SUB, norm_two, ZERO)
    def one_image(i, carry):
        win = pl.ds(pl.multiple_of(192 * i, 192), WIN)
        for j in range(ZERO, TH, LANES):
            part = slice(j, j + LANES)
            d_act = mm(wt2_ref[i, part, :], d1b[win, :]).astype(BF16).astype(F32)
            act, d_u = gelu_and_grad(ut_ref[i, part, :], d_act)
            gbt1_ref[part, :] += fold_lanes(d_u)
            acts[part, :] = act.astype(BF16)
            dus[part, :] = d_u.astype(BF16)
        gt2_ref[i] += mm_t(d1b[win, :], acts[...])
        gt1_ref[i] += mm_t(hs[win, :], dus[...])
        dhf[win, :] += mm(wt1_ref[i], dus[...])
        return carry

    lax.fori_loop(ZERO, GROUP, one_image, ZERO)

    def norm_one(i, carry):
        rows = pl.ds(pl.multiple_of(i * SUB, SUB), SUB)
        d_n1 = dhf[rows, :].astype(BF16).astype(F32)
        nrm1, rstd1 = norm_stats(x_ref[rows, :].astype(F32))
        for k, part in ((ZERO, d_n1 * nrm1), (ONE, d_n1)):
            gcv_ref[k] += fold_rows(part)
        if not first:
            dx_ref[rows, :] = (norm_back(nrm1, rstd1, cv_ref[ZERO:ONE, :], d_n1) + d1b[rows, :].astype(F32)).astype(BF16)
        return carry

    lax.fori_loop(ZERO, GR // SUB, norm_one, ZERO)

    @pl.when(step == ROWS // GR - ONE)
    def _():
        for g, at in ((gt1_ref, ZERO), (gt2_ref, TH)):
            tok_ref[ZERO:TOK, at:at + TH] = sum(g[i, FOUR * i:FOUR * i + TOK, :] for i in range(ONE, GROUP)) + g[ZERO, ZERO:TOK, :]
        tok_ref[TOK:TROWS, :] = jnp.zeros((TROWS - TOK, CH), F32)
        vec_ref[...] = jnp.zeros(vec_ref.shape, F32)
        for i in range(FIVE):
            vec_ref[i:i + ONE, :] = jnp.sum(gcv_ref[i], axis=ZERO, keepdims=True)
        for q in range(QUART):
            vec_ref[FIVE + q:SIX + q, :] = jnp.sum(gb1_ref[:, CH * q:CH * q + CH], axis=ZERO, keepdims=True)
        vec_ref[9:10, ZERO:TH] = jnp.sum(gbt1_ref[...].T, axis=ZERO, keepdims=True)
        per_tok = sum(gbt2_ref[TOK * i:TOK * i + TOK, :] for i in range(ONE, GROUP)) + gbt2_ref[ZERO:TOK, :]
        vec_ref[10:11, ZERO:TOK] = jnp.sum(per_tok.T, axis=ZERO, keepdims=True)
        job.first_done()
        job.finish()


def backward_layer(dh, d2, x1, x, ut, w1, wt1s, wt2s, cv, gb1, dw1, dw2, extra):
    sds = jax.ShapeDtypeStruct
    first = len(extra) == TWO
    act = by_group((GR, CH))
    keep = lambda shape: pl.BlockSpec(shape, lambda g: (ZERO,) * len(shape))
    n = BLK
    outs, shapes = [keep((TROWS, CH)), keep((VROWS, CH)), ANY], [sds((TROWS, CH), F32), sds((VROWS, CH), F32), sds((TWO, n, CH), F32)]
    if not first:
        outs, shapes = [act] + outs, [sds((ROWS, CH), BF16)] + shapes
    return pl.pallas_call(
        functools.partial(backward_kernel, first),
        grid=(ROWS // GR,),
        in_specs=[by_group((GR, HID)), act, act, act, by_group((GROUP, TH, CH)), once((CH, HID)), once((GROUP, WIN, TH)), once((GROUP, TH, WIN)), once((EIGHT, CH)), once((EIGHT, HID))] + [ANY] * (TWO + len(extra)),
        out_specs=outs,
        out_shape=shapes,
        scratch_shapes=[pltpu.VMEM((GROUP, WIN, TH), F32), pltpu.VMEM((GROUP, WIN, TH), F32), pltpu.VMEM((TH, LANES), F32), pltpu.VMEM((GR, LANES), F32), pltpu.VMEM((FIVE, EIGHT, CH), F32),
                        pltpu.VMEM((GR, CH), BF16), pltpu.VMEM((GR, CH), BF16), pltpu.VMEM((GR, CH), F32)] + [pltpu.VMEM((TH, CH), BF16)] * TWO + reduction_scratch(n),
        compiler_params=pltpu.CompilerParams(collective_id=ONE if first else TWO, has_side_effects=True, vmem_limit_bytes=67000000),
        name="backward_layer",
    )(dh, d2, x1, x, ut, w1, wt1s, wt2s, cv, gb1, dw1, dw2, *extra)

KP = 4864
NJ = TWO_TILES
NSUB = SIX
STEPS = HID // NJ


def channel_back_kernel(late, d2_ref, h2_ref, w2_ref, hid_ref, *rest):
    give, dh_ref, dw1_ref, dw2_ref, db1_ref, take, st, even, odd, dbs, dwst, own_sem, send, recv = rest
    j = pl.program_id(ZERO)
    sub, part = ROWS // NSUB, TWO * CH // NSUB
    me = lax.axis_index("fsdp")
    if late:
        others = [peer(me, rel) for rel in (TWO, FOUR)]
        hops = last_hops(give, take, send, recv, me)
    else:
        others = [lax.rem(me + i, NDEV) for i in range(ONE, NDEV)]
        mine = lambda d: give.at[pl.ds(pl.multiple_of(HROWS * d, HROWS), HROWS)]
        hops = [pltpu.make_async_remote_copy(src_ref=mine(d), dst_ref=take.at[me], send_sem=send.at[i], recv_sem=recv.at[i], device_id=(d,), device_id_type=MESH) for i, d in enumerate(others)]
        own = pltpu.make_async_copy(mine(me), take.at[me], own_sem)

    @pl.when(j == ZERO)
    def _():
        barrier = pltpu.get_barrier_semaphore()
        for dev in others:
            pl.semaphore_signal(barrier, inc=ONE, device_id=(dev,), device_id_type=MESH)
        pl.semaphore_wait(barrier, len(others))
        for copy in hops:
            copy.start()
        if not late:
            own.start()

    @pl.when(j == ZERO)
    def _():
        st[ZERO:CH, ZERO:ROWS] = h2_ref[...].T
        st[CH:TWO * CH, ZERO:ROWS] = d2_ref[...].T
        st[:, ROWS:KP] = jnp.zeros((TWO * CH, KP - ROWS), BF16)
        for rhs in (even, odd):
            rhs[:, ROWS:KP, :] = jnp.zeros((TWO, KP - ROWS, NJ), BF16)

    def through_w2(r):
        rows = pl.ds(pl.multiple_of(r * sub, sub), sub)
        return mm_t(d2_ref[rows, :], w2_ref[...])

    def through_gelu(r, d_act, sums, rhs):
        rows = pl.ds(pl.multiple_of(r * sub, sub), sub)
        act, dh = gelu_and_grad(hid_ref[rows, :], d_act.astype(BF16).astype(F32))
        rhs[ONE, rows, :] = act.astype(BF16)
        dhb = dh.astype(BF16)
        rhs[ZERO, rows, :] = dhb
        dh_ref[rows, :] = dhb
        return sums + fold_rows(dh)

    def weight_part(r, rhs):
        rows = pl.ds(pl.multiple_of(r * part, part), part)
        dwst[rows, :] = mm(st[rows, :], rhs[(r * part) // CH])

    def emit():
        db1_ref[...] = dbs[...]
        dw1_ref[...] = dwst[ZERO:CH, :]
        dw2_ref[...] = dwst[CH:TWO * CH, :].T

    zero = jnp.zeros((EIGHT, NJ), F32)

    @pl.when(j == ZERO)
    def _():
        dbs[...] = lax.fori_loop(ZERO, NSUB, lambda r, sums: through_gelu(r, through_w2(r), sums, even), zero)

    for parity, (new, old) in enumerate(((even, odd), (odd, even))):
        @pl.when((j > ZERO) & (j < STEPS) & (lax.rem(j, TWO) == parity))
        def _():
            def both(r, sums):
                d_act = through_w2(r)
                weight_part(r, old)
                return through_gelu(r, d_act, sums, new)

            sums = lax.fori_loop(ZERO, NSUB, both, zero)
            emit()
            dbs[...] = sums

    @pl.when(j == STEPS)
    def _():
        def only(r, carry):
            weight_part(r, odd)
            return carry

        lax.fori_loop(ZERO, NSUB, only, ZERO)
        emit()
        for copy in hops:
            copy.wait()
        if not late:
            own.wait()


def channel_back(d2, h2, w2, hid, give, late):
    sds = jax.ShapeDtypeStruct
    cur = lambda j: jnp.minimum(j, STEPS - ONE)
    prev = lambda j: jnp.maximum(j - ONE, ZERO)
    wide = CH // NJ
    outs = [pl.BlockSpec((ROWS, NJ), lambda j: (ZERO, cur(j))), pl.BlockSpec((None, CH, NJ), lambda j: (prev(j) // wide, ZERO, lax.rem(prev(j), wide))),
            pl.BlockSpec((NJ, CH), lambda j: (prev(j), ZERO)), pl.BlockSpec((EIGHT, NJ), lambda j: (ZERO, prev(j)))]
    shapes = [sds((ROWS, HID), BF16), sds((QUART, CH, CH), F32), sds((HID, CH), F32), sds((EIGHT, HID), F32)]
    scratch = [pltpu.VMEM((TWO * CH, KP), BF16), pltpu.VMEM((TWO, KP, NJ), BF16), pltpu.VMEM((TWO, KP, NJ), BF16), pltpu.VMEM((EIGHT, NJ), F32), pltpu.VMEM((TWO * CH, NJ), F32)]
    outs.append(ANY)
    shapes.append(sds(give.shape[ONE:] if late else (NDEV, HROWS, NCP), F32))
    scratch += [pltpu.SemaphoreType.DMA] + [pltpu.SemaphoreType.DMA((NDEV,))] * TWO
    return pl.pallas_call(
        functools.partial(channel_back_kernel, late),
        grid=(STEPS + ONE,),
        in_specs=[once((ROWS, CH)), once((ROWS, CH)), pl.BlockSpec((NJ, CH), lambda j: (cur(j), ZERO)), pl.BlockSpec((ROWS, NJ), lambda j: (ZERO, cur(j)))] + [ANY],
        out_specs=outs,
        out_shape=shapes,
        scratch_shapes=scratch,
        compiler_params=pltpu.CompilerParams(collective_id=FIVE + late, has_side_effects=True, vmem_limit_bytes=67000000),
        name="channel_back",
    )(d2, h2, w2, hid, give)

IMG_PAD = 32


def head_kernel(x_ref, lab_ref, hw_ref, fv_ref, hb_ref, d2_ref, ghw_ref, ex_ref, pool, gfv_ref, dl):
    ngroup = ROWS // GR

    def image_of_row(shape, dim, g):
        row = lax.broadcasted_iota(jnp.int32, shape, dim)
        return GROUP * g + sum((row >= TOK * i).astype(jnp.int32) for i in range(ONE, GROUP))

    def normed(g):
        nrm, rstd = norm_stats(x_ref[pl.ds(pl.multiple_of(g * GR, GR), GR), :].astype(F32))
        return nrm, rstd

    pool[...] = jnp.zeros(pool.shape, F32)

    def pool_one(g, carry):
        nrm, _ = normed(g)
        pick = image_of_row((IMG_PAD, GR), ONE, g) == lax.broadcasted_iota(jnp.int32, (IMG_PAD, GR), ZERO)
        pool[...] += mm(pick.astype(F32).astype(BF16), (nrm * fv_ref[ZERO:ONE, :] + fv_ref[ONE:TWO, :]).astype(BF16))
        return carry

    lax.fori_loop(ZERO, ngroup, pool_one, ZERO)
    real = lax.broadcasted_iota(jnp.int32, (IMG_PAD, NCLS), ZERO) < 24
    pooled = (pool[...] / TOK).astype(BF16)
    logits = mm(pooled, hw_ref[...]) + hb_ref[ZERO:ONE, ZERO:NCLS]
    top = jnp.max(logits, axis=-ONE, keepdims=True)
    log_norm = top + jnp.log(jnp.sum(jnp.exp(logits - top), axis=-ONE, keepdims=True))
    is_label = lax.broadcasted_iota(jnp.int32, (IMG_PAD, NCLS), ONE) == lab_ref[:, ZERO:ONE]
    picked = jnp.sum(jnp.where(is_label, logits, 0.0), axis=-ONE, keepdims=True)
    per_image = jnp.where(lax.broadcasted_iota(jnp.int32, (IMG_PAD, ONE), ZERO) < 24, log_norm - picked, 0.0)
    d_logits = jnp.where(real, (jnp.exp(logits - log_norm) - is_label.astype(F32)) / (24 * NDEV), 0.0)
    d_log_b = d_logits.astype(BF16)
    dl[...] = jnp.zeros(dl.shape, F32)
    dl[:, ZERO:NCLS] = d_logits
    ghw_ref[...] = lax.dot_general(pooled, dl[...].astype(BF16), (((ZERO,), (ZERO,)), ((), ())), preferred_element_type=F32)
    d_pool = mm_t(d_log_b, hw_ref[...])
    pool[...] = d_pool / TOK
    gfv_ref[...] = jnp.zeros(gfv_ref.shape, F32)

    def back_one(g, carry):
        nrm, rstd = normed(g)
        pick = image_of_row((GR, IMG_PAD), ZERO, g) == lax.broadcasted_iota(jnp.int32, (GR, IMG_PAD), ONE)
        d_n = mm(pick.astype(F32).astype(BF16), pool[...].astype(BF16))
        gfv_ref[ZERO] += fold_rows(d_n * nrm)
        gfv_ref[ONE] += fold_rows(d_n)
        d2_ref[pl.ds(pl.multiple_of(g * GR, GR), GR), :] = norm_back(nrm, rstd, fv_ref[ZERO:ONE, :], d_n).astype(BF16)
        return carry

    lax.fori_loop(ZERO, ngroup, back_one, ZERO)
    nrow = CH // LANES
    parts = [jnp.sum(gfv_ref[i], axis=ZERO, keepdims=True) for i in range(TWO)] + [jnp.sum(dl[...], axis=ZERO, keepdims=True)]
    ex_ref[...] = jnp.zeros(ex_ref.shape, F32)
    for i, part in enumerate(parts):
        for c in range(part.shape[ONE] // LANES):
            ex_ref[nrow * i + c:nrow * i + c + ONE, :] = part[:, LANES * c:LANES * c + LANES]
    ex_ref[LOSS_ROW:EXR, :] = jnp.broadcast_to(jnp.sum(per_image, axis=ZERO, keepdims=True), (EXR - LOSS_ROW, LANES))


def head_layer(x2, labels, head_full, fv, head_b):
    sds = jax.ShapeDtypeStruct
    lab = jnp.broadcast_to(jnp.pad(labels, (ZERO, IMG_PAD - 24))[:, None], (IMG_PAD, LANES))
    return pl.pallas_call(
        head_kernel,
        in_specs=[VMEM] * FIVE,
        out_specs=[VMEM] * THREE,
        out_shape=[sds((ROWS, CH), BF16), sds((CH, NCP), F32), sds((EXR, LANES), F32)],
        scratch_shapes=[pltpu.VMEM((IMG_PAD, CH), F32), pltpu.VMEM((TWO, EIGHT, CH), F32), pltpu.VMEM((IMG_PAD, NCP), F32)],
        compiler_params=pltpu.CompilerParams(vmem_limit_bytes=60000000),
        name="head_loss",
    )(x2, lab, head_full, fv, head_b)


def view(a):
    return a.reshape(TWO, SH, LANES).transpose(ONE, ZERO, TWO)


def unview(a):
    return a.transpose(ONE, ZERO, TWO).reshape(TWO, SH * LANES)


def solution(mesh):
    row_spec = P('fsdp')
    layer_spec = P(None, 'fsdp')
    in_specs = (row_spec, row_spec) + (layer_spec, row_spec, row_spec) * THREE
    out_specs = (P(),) + in_specs[TWO:]

    def device_step(act_in, labels, layer_p, head_w, small_p, layer_m, head_m, small_m, layer_v, head_v, small_v):
        small8 = jnp.pad(small_p.reshape(THREE, LANES), ((ZERO, FIVE), (ZERO, ZERO)))
        (w1, w2, st1, st2, head_full), *vectors, (fv, hb) = gather_all(view(layer_p), head_w, small8)
        x, stage, saved = act_in, (st1, st2), []
        for wt1s, wt2s, wt1t, wt2t, bt1, bt2, cv, b1 in vectors:
            x1, ut, hid, h2, x2, *more = forward_layer(x, wt1t, wt2t, bt1, bt2, w1, w2, cv, b1, stage)
            saved.append((more[ZERO] if more else x, x1, ut, hid, h2, w1, w2, wt1s, wt2s, cv))
            if more:
                w1, w2 = more[ONE:THREE]
            x, stage = x2, ()
        d2, g_head, ex = head_layer(x, labels, head_full, fv, hb)
        give, extra, arrived, reds = g_head, (), [], []
        for x, x1, ut, hid, h2, w1, w2, wt1s, wt2s, cv in reversed(saved):
            dh, dw1, dw2, gb1, got = channel_back(d2, h2, w2, hid, give, len(arrived) > ZERO)
            *d_in, g_tok, g_vec, give = backward_layer(dh, d2, x1, x, ut, w1, wt1s, wt2s, cv, gb1, dw1, dw2, extra)
            arrived.append(got)
            reds.append(give)
            extra = g_tok, g_vec
            d2 = d_in[ZERO] if d_in else None
        heads, late = arrived
        g, g_head, g_small, scalars = finish(reds[ONE], reds[ZERO], late, heads, g_tok, g_vec, ex)
        smalls = [a.reshape(THREE, LANES) for a in (small_p, small_m, small_v)]
        outs = update(view(layer_p), view(layer_m), view(layer_v), g, g_head, g_small, scalars, (head_w, head_m, head_v), smalls)
        new_lp, new_lm, new_lv = [unview(a) for a in outs[:THREE]]
        new_hw, new_hm, new_hv = outs[THREE:SIX]
        new_sp, new_sm, new_sv = [a.reshape(-ONE) for a in outs[SIX:]]
        return (scalars[ZERO, ZERO] / (act_in.shape[ZERO] * NDEV), new_lp, new_hw, new_sp, new_lm, new_hm, new_sm, new_lv, new_hv, new_sv)

    return jax.shard_map(device_step, mesh=mesh, in_specs=in_specs, out_specs=out_specs, check_vma=False)
```

time: 2120 us -> 827 us (0.39); the launches traced: 2090 us -> 822 us
  Pallas kernels: 0 us -> 808 us
  matrix products: 707 us -> 0 us
  local copies, waits for them, and re-layouts: 644 us -> 11.3 us
  waiting for transfers between devices: 491 us -> 0 us
  other arithmetic: 165 us -> 0 us
  blocking collectives: 59.4 us -> 0 us
    pallas_call x0 -> x10, Pallas kernels: none -> 808 us  [the longest x2 239 us: channel_back(): pl.pallas_call(functools.partial(channel_back_kernel, late), grid=(STEPS...]
    dot_general x27 -> x0, matrix products: 707 us -> none  [the longest x2 131 us: layer_backward(): jnp.einsum('bsc,dc->bsd', d_out_bf, w_ch2, preferred_element_type=jnp.flo...]
    unnamed x6 -> x0, waiting for transfers between devices: 421 us -> none
    concatenate x3 -> x0, local copies, waits for them, and re-layouts: 307 us -> none  [the longest x2 307 us: layer_backward(): jnp.concatenate([g_w_tok1.reshape(-1), g_w_tok2.reshape(-1), g_w_ch1.resh...]
    slice x5 -> x1, local copies, waits for them, and re-layouts: 220 us -> 1.19 us  [device_step(): scalars[ZERO, ZERO] / (act_in.shape[ZERO] * NDEV)]
    reduce_sum x22 -> x0, other arithmetic: 102 us -> none  [the longest x9 42.6 us: layer_norm(): var_val = jnp.mean(jnp.square(x_f - mean_val), axis=-1, keepdims=True)]
    all_gather x3 -> x0, waiting for transfers between devices: 69.8 us -> none  [the longest x2 69.8 us: device_step(): lax.all_gather(layer_p[layer_idx].astype(jnp.bfloat16), 'fsdp', tiled=True)]
    reshape x14 -> x0, local copies, waits for them, and re-layouts: 61.6 us -> none  [the longest x8 36.6 us: unpack_layer(): pieces.append(flat[piece_start:piece_start + piece_len].reshape(shape_one))]
  transfers between devices with their start and end apart: 5 -> 0, of which waited for: 2 -> 0; matrix products, arithmetic and copies ran while one was open for 47% -> 0% of each run, Pallas kernels for 0% -> 0%
where the time goes in v2:
time: 827 us; the launch traced here: 822 us
  Pallas kernels  808 us (98%)
  local copies, waits for them, and re-layouts  11.3 us (1%)
    pallas_call x2, Pallas kernels, channel_back(): pl.pallas_call(functools.partial(channel_back_kernel, late), grid=(STEPS...  239 us
    pallas_call x2, Pallas kernels, backward_layer(): pl.pallas_call(functools.partial(backward_kernel, first), grid=(ROWS // G...  228 us
    pallas_call x2, Pallas kernels, forward_layer(): pl.pallas_call(functools.partial(forward_kernel, first), grid=(ROWS // GR...  163 us
    pallas_call x1, Pallas kernels, gather_all(): pl.pallas_call(gather_kernel, in_specs=[ANY, VMEM, VMEM], out_specs=[ANY]...  85.1 us
    pallas_call x1, Pallas kernels, finish(): pl.pallas_call(finish_kernel, in_specs=[ANY] * FOUR + [VMEM] * THREE, out...  52.2 us
    pallas_call x1, Pallas kernels, head_layer(): pl.pallas_call(head_kernel, in_specs=[VMEM] * FIVE, out_specs=[VMEM] * TH...  24.8 us

profile of v2, /device:TPU:0, one launch (start us, length us, event | category | flops | bytes accessed | tf_op | source)
XLA Modules:
  0.0 822.1 jit_solution(14665752447510372890)
XLA Ops:
  0.6 0.7 pad.9
  1.3 1.3 pad.8.small_ref
  2.6 0.7 broadcast_in_dim.2.lab_ref
  3.3 7.5 copy.21.x_ref
  10.8 85.1 %gather_weights.1 = (bf16[768,3072]{1,0:T(8,128)(2,1)}, bf16[3072,768]{1,0:T(8,128)(2,1)}, bf16[224,3072]{1,0:T(8,128)(2,1)}, bf16[816,768]{1,0:T(8,128)(2,1)}, ...) custom-call(f32[4763,2,128]{2,1,0:T(2,128)} %bitcast.25, ...), custom_call_target="tpu_custom_call" | custom-call | tf_op jit(solution)/shard_map/gather_weights/pallas_call | solution.py:368
  95.9 88.9 %forward_layer.2 = (bf16[4704,768]{1,0:T(8,128)(2,1)}, f32[24,384,768]{2,1,0:T(8,128)}, f32[4704,3072]{1,0:T(8,128)}, bf16[4704,768]{1,0:T(8,128)(2,1)}, bf16[47...) custom-call(bf16[24,196,768]{2,1,0:T(8,128)(2,1)} %copy.21.x_ref, ...), custom_call_target="tpu_custom_call" | custom-call | tf_op jit(solution)/shard_map/forward_layer/pallas_call | solution.py:969
  184.8 74.0 %forward_layer.3 = (bf16[4704,768]{1,0:T(8,128)(2,1)}, f32[24,384,768]{2,1,0:T(8,128)}, f32[4704,3072]{1,0:T(8,128)}, bf16[4704,768]{1,0:T(8,128)(2,1)}, bf16[4704,768]{1,0:T(8,128)(2,1)}) custom-call(bf16[4704,768]{1,0:T(8,128)(2,1)} %get-tuple-element.89.x_ref, bf16[4,384,208]{2,1,0:T(8,128)(2,1)} %get-tuple-element.90.wt1_ref, ...), custom_call_target="tpu_custom_call" | custom-call | tf_op jit(solution)/shard_map/forward_layer/pallas_call | solution.py:969
  258.8 24.8 %head_loss.1 = (bf16[4704,768]{1,0:T(8,128)(2,1)}, f32[768,1024]{1,0:T(8,128)}, f32[32,128]{1,0:T(8,128)}) custom-call(bf16[4704,768]{1,0:T(8,128)(2,1)} %get-tuple-element.98.x_ref, s32[32,128]{1,0:T(8,128)} %broadcast_in_dim.2.lab_ref, bf16[768,1000]{1,0:T(8,128)(2,1)} %get-tuple-element.99.hw_ref, f32[8,768]{1,0:T(8,128)} %get-tuple-element.100.fv_ref, ...), custom_call_target="tpu_custom_call" | custom-call | tf_op jit(solution)/shard_map/head_loss/pallas_call | solution.py:1287
  283.6 120.1 %channel_back.2 = (bf16[4704,3072]{1,0:T(8,128)(2,1)}, f32[4,768,768]{2,1,0:T(8,128)}, f32[3072,768]{1,0:T(8,128)}, f32[8,3072]{1,0:T(8,128)}, f32[8,96,1024]{2,1,0:T(8,128)}) custom-call(bf16[4704,768]{1,0:T(8,128)(2,1)} %get-tuple-element.102.d2_ref, bf16[4704,768]{1,0:T(8,128)(2,1)} %get-tuple-element.103.h2_ref, ...), custom_call_target="tpu_custom_call" | custom-call | tf_op jit(solution)/shard_map/channel_back/pallas_call | solution.py:1214
  403.7 116.7 %backward_layer.2 = (bf16[4704,768]{1,0:T(8,128)(2,1)}, f32[200,768]{1,0:T(8,128)}, f32[16,768]{1,0:T(8,128)}, f32[2,832,768]{2,1,0:T(8,128)}) custom-call(bf16[4704,3072]{1,0:T(8,128)(2,1)} %get-tuple-element.106.dh_ref, bf16[4704,768]{1,0:T(8,128)(2,1)} %get-tuple-element.102.d2_ref, bf16[4704,768]{1,0:T(8,128)(2,1)} %get-tuple-element.107.x1_ref, ...), custom_call_target="tpu_custom_call" | custom-call | tf_op jit(solution)/shard_map/backward_layer/pallas_call | solution.py:1097
  520.4 118.5 %channel_back.3 = (bf16[4704,3072]{1,0:T(8,128)(2,1)}, f32[4,768,768]{2,1,0:T(8,128)}, f32[3072,768]{1,0:T(8,128)}, f32[8,3072]{1,0:T(8,128)}, f32[832,768]{1,0:T(8,128)}) custom-call(bf16[4704,768]{1,0:T(8,128)(2,1)} %get-tuple-element.114.d2_ref, bf16[4704,768]{1,0:T(8,128)(2,1)} %get-tuple-element.115.h2_ref, bf16[3072,768]{1,0:T(8,128)(2,1)} %get-tuple-element.84.w2_ref, ...), custom_call_target="tpu_custom_call" | custom-call | tf_op jit(solution)/shard_map/channel_back/pallas_call | solution.py:1214
  638.9 111.3 %backward_layer.3 = (f32[200,768]{1,0:T(8,128)}, f32[16,768]{1,0:T(8,128)}, f32[2,832,768]{2,1,0:T(8,128)}) custom-call(bf16[4704,3072]{1,0:T(8,128)(2,1)} %get-tuple-element.118.dh_ref, bf16[4704,768]{1,0:T(8,128)(2,1)} %get-tuple-element.114.d2_ref, bf16[4704,768]{1,0:T(8,128)(2,1)} %get-tuple-element.119.x1_ref, ...), custom_call_target="tpu_custom_call" | custom-call | tf_op jit(solution)/shard_map/backward_layer/pallas_call | solution.py:1097
  750.2 52.2 %finish.1 = (f32[2,4763,128]{2,1,0:T(8,128)}, f32[96,1000]{1,0:T(8,128)}, f32[3,128]{1,0:T(4,128)}, f32[8,128]{1,0:T(8,128)}) custom-call(f32[2,832,768]{2,1,0:T(8,128)} %get-tuple-element.129.red0, f32[2,832,768]{2,1,0:T(8,128)} %get-tuple-element.117.rest_0_.red1, f32[832,768]{1,0:T(8,128)} %get-tuple-element.130.late1, ...), custom_call_target="tpu_custom_call" | custom-call | tf_op jit(solution)/shard_map/finish/pallas_call | solution.py:769
  802.5 1.2 slice.3
  804.3 16.4 %update.1 = (f32[4763,2,128]{2,1,0:T(2,128)}, f32[4763,2,128]{2,1,0:T(2,128)}, f32[4763,2,128]{2,1,0:T(2,128)}, f32[96,1000]{1,0:T(8,128)}, f32[96,1000]{1,0:T(8...) custom-call(f32[4763,2,128]{2,1,0:T(2,128)} %bitcast.26, ...), custom_call_target="tpu_custom_call" | custom-call | tf_op jit(solution)/shard_map/update/pallas_call | solution.py:831

commit v3 on v2

--- a/solution.py
+++ b/solution.py
@@ -112,8 +112,8 @@
 
 
 class Spread:
-    def __init__(self, pieces, send_sem, recv_sem, fwd_sem):
-        self.pieces, self.send_sem, self.recv_sem, self.fwd_sem = pieces, send_sem, recv_sem, fwd_sem
+    def __init__(self, pieces, send_sem, recv_sem, fwd_sem, far_sem):
+        self.pieces, self.send_sem, self.recv_sem, self.fwd_sem, self.far_sem = pieces, send_sem, recv_sem, fwd_sem, far_sem
         self.me = lax.axis_index("fsdp")
 
     def copies(self, d, k, rel):
@@ -137,11 +137,17 @@
                     copy.start()
         self.each((ZERO,), body)
 
+    def across(self, s, rel):
+        if rel != (FOUR if s % TWO else TWO):
+            return []
+        return [pltpu.make_async_remote_copy(src_ref=b, dst_ref=b, send_sem=self.far_sem.at[i], recv_sem=self.recv_sem.at[s, i], device_id=(s ^ SIX,), device_id_type=MESH)
+                for i, (_, b) in enumerate(self.pieces(s))]
+
     def hand_on(self, rels):
         def body(s, rel):
             for copy in self.handed(s, s ^ rel ^ ONE):
                 copy.wait_recv()
-            for copy in self.handed(s, s ^ rel ^ ONE):
+            for copy in self.across(s, rel) + self.handed(s, s ^ rel ^ ONE):
                 copy.start()
         self.each(rels, body)
 
@@ -159,12 +165,12 @@
         self.each((ZERO,), own)
 
         def other(s, rel):
-            for copy in self.handed(s, s ^ rel ^ ONE):
+            for copy in self.across(s, rel) + self.handed(s, s ^ rel ^ ONE):
                 copy.wait_send()
         self.each(RELS, other)
 
 
-ORDER = (FOUR, TWO, SIX, ONE)
+ORDER = (FOUR, TWO, ONE)
 
 
 def merge_edges(w1, w2, e1, e2, m1, m2, sem):
@@ -192,7 +198,7 @@
 
 def spread_sems(n):
     dma = pltpu.SemaphoreType.DMA
-    return [dma((len(ORDER), n)), dma((NDEV, n)), dma((NDEV, n))]
+    return [dma((len(ORDER), n)), dma((NDEV, n)), dma((NDEV, n)), dma((n,))]
 
 
 def lay_token_weights(tok, flat, nat, wt1s, wt2s, wt1t, wt2t):
@@ -249,9 +255,9 @@
     put(cv, FOUR, TWO * ng + HID // LANES, CH, vf)
 
 
-def gather_kernel(p_ref, head_ref, small_ref, w1, w2, st1, st2, headf, *rest):
+def gather_kernel(p_ref, head_ref, small_ref, w1, w2, nw1, nw2, headf, *rest):
     (tw0, tw1, (fv, hb)), rest = (rest[ZERO:EIGHT], rest[EIGHT:SIXTEEN], rest[SIXTEEN:18]), rest[18:]
-    (e1, e2, xs, s1, s2, stok, svec, shead, ssmall, tok, vec, smallf, flat, nat, vf, m1, m2, ed_sem, ld_sem, stage_sem, own_sem), rest = rest[:21], rest[21:]
+    (e1, e2, ne1, ne2, xs, s1, s2, stok, svec, shead, ssmall, tok, vec, smallf, flat, nat, vf, m1, m2, ed_sem, ld_sem, stage_sem, own_sem), rest = rest[:23], rest[23:]
     me = lax.axis_index("fsdp")
     loads = [pltpu.make_async_copy(p_ref.at[:, l, :], xs.at[l, pl.ds(MARG, SH)], ld_sem.at[l]) for l in range(TWO)]
     for copy in loads:
@@ -273,7 +279,7 @@
     def classes(d):
         return [(shead, headf.at[pl.ds(HROWS * d, HROWS)])]
 
-    jobs = [Spread(f, *rest[THREE * i:THREE * i + THREE]) for i, f in enumerate((early, matrices, classes))]
+    jobs = [Spread(f, *rest[FOUR * i:FOUR * i + FOUR]) for i, f in enumerate((early, matrices, classes))]
 
     def keep_own(d, _):
         return [pltpu.make_async_copy(a, b, own_sem.at[i]) for i, (a, b) in enumerate(matrices(d) + classes(d))]
@@ -320,10 +326,17 @@
             for copy in keep_own(d, ZERO):
                 copy.start()
     tile(ONE)
-    stage = [pltpu.make_async_copy(a.at[ONE], b, stage_sem.at[i]) for i, (a, b) in enumerate(((s1, st1), (s2, st2)))]
-    for copy in stage:
-        copy.start()
-    jobs[ZERO].hand_on(RELS)
+
+    def keep_next(d):
+        return [pltpu.make_async_copy(a, b, stage_sem.at[i]) for i, (a, b) in enumerate(matrix_moves(d, s1.at[ONE], s2.at[ONE], nw1, nw2, ne1, ne2))]
+
+    for d in range(NDEV):
+        @pl.when(me == d)
+        def _():
+            for copy in keep_next(d):
+                copy.start()
+    jobs[ZERO].hand_on(ORDER[:TWO])
+    jobs[ZERO].hand_on(RELS[TWO:])
     jobs[ZERO].arrive()
     for l, (wt1s, wt2s, wt1t, wt2t, bt1, bt2, cv, b1) in enumerate((tw0, tw1)):
         lay_token_weights(tok.at[l], flat, nat, wt1s, wt2s, wt1t, wt2t)
@@ -335,9 +348,9 @@
             fv[i:i + ONE, LANES * c:LANES * c + LANES] = flat[C2 * i + c:C2 * i + c + ONE, :]
     for c in range(NCP // LANES):
         hb[ZERO:ONE, LANES * c:LANES * c + LANES] = flat[TWO * C2 + c:TWO * C2 + c + ONE, :]
-    for rel in ORDER[:THREE]:
-        jobs[ONE].hand_on((rel,))
-    jobs[TWO].hand_on(RELS)
+    for rels in (ORDER[:TWO], RELS[TWO:]):
+        jobs[ONE].hand_on(rels)
+        jobs[TWO].hand_on(rels)
     jobs[ONE].arrive()
     jobs[TWO].arrive()
     for job in jobs:
@@ -345,11 +358,9 @@
     for d in range(NDEV):
         @pl.when(me == d)
         def _():
-            for copy in keep_own(d, ZERO):
+            for copy in keep_own(d, ZERO) + keep_next(d):
                 copy.wait()
     merge_edges(w1, w2, e1, e2, m1, m2, ed_sem)
-    for copy in stage:
-        copy.wait()
 
 
 STAGE1 = max(SIXTEEN * (b - a) for a, b in (tiles_of(c1_span(d), SIXTEEN * C1) for d in range(NDEV)))
@@ -360,26 +371,26 @@
     sds = jax.ShapeDtypeStruct
     per_layer = [sds((GROUP, WIN, TH), BF16), sds((GROUP, TH, WIN), BF16), sds((GROUP, TH, WIN), BF16), sds((GROUP, WIN, TH), BF16),
                  sds((TH, LANES), F32), sds((GROUP, WIN, LANES), F32), sds((EIGHT, CH), F32), sds((EIGHT, HID), F32)]
-    far = [sds((CH, HID), BF16), sds((HID, CH), BF16), sds((STAGE1, HID), BF16), sds((STAGE2, CH), BF16), sds((CH, NCLS), BF16)]
+    far = [sds((CH, HID), BF16), sds((HID, CH), BF16)] * TWO + [sds((CH, NCLS), BF16)]
     near = per_layer * TWO + [sds((EIGHT, CH), F32), sds((EIGHT, NCP), F32)]
-    edge = [sds((len(EDGE1), SIXTEEN, HID), BF16), sds((len(EDGE2), SIXTEEN, CH), BF16)]
+    edge = [sds((len(EDGE1), SIXTEEN, HID), BF16), sds((len(EDGE2), SIXTEEN, CH), BF16)] * TWO
     dma = pltpu.SemaphoreType.DMA
     nv = SH - VEC0
     outs = pl.pallas_call(
         gather_kernel,
         in_specs=[ANY, VMEM, VMEM],
-        out_specs=[ANY] * len(far) + [VMEM] * len(near) + [ANY] * TWO,
+        out_specs=[ANY] * len(far) + [VMEM] * len(near) + [ANY] * len(edge),
         out_shape=far + near + edge,
         scratch_shapes=[pltpu.VMEM((TWO, SH + TWO * MARG + FIVE, LANES), F32), pltpu.VMEM((TWO, STAGE1, HID), BF16), pltpu.VMEM((TWO, STAGE2, CH), BF16),
                         pltpu.VMEM((TWO, T1, LANES), BF16), pltpu.VMEM((TWO, nv, LANES), BF16), pltpu.VMEM((HROWS, NCLS), BF16), pltpu.VMEM((EIGHT, LANES), F32),
                         pltpu.VMEM((TWO, T1, LANES), BF16), pltpu.VMEM((TWO, nv, LANES), BF16), pltpu.VMEM((NDEV, EIGHT, LANES), F32),
                         pltpu.VMEM((T1 + WIN + EIGHT, LANES), F32), pltpu.VMEM((TWO, TH, LANES), F32), pltpu.VMEM((nv, LANES), F32)] + edge_scratch()
-        + [dma((TWO,)), dma((TWO,)), dma((SIX,))] + spread_sems(THREE) + spread_sems(FOUR) + spread_sems(ONE),
+        + [dma((TWO,)), dma((FOUR,)), dma((SIX,))] + spread_sems(THREE) + spread_sems(FOUR) + spread_sems(ONE),
         compiler_params=pltpu.CompilerParams(collective_id=ZERO, has_side_effects=True, vmem_limit_bytes=60000000),
         name="gather_weights",
     )(p_view, head_w, small8)
     n = len(far)
-    return outs[:n], outs[n:n + EIGHT], outs[n + EIGHT:n + SIXTEEN], outs[n + SIXTEEN:n + 18]
+    return outs[:n], outs[-TWO:], outs[n:n + EIGHT], outs[n + EIGHT:n + SIXTEEN], outs[n + SIXTEEN:n + 18]
 
 
 def g1_rows(d):
@@ -402,21 +413,29 @@
     return QUART * (hi - lo) + g2_rows(s)[ONE] - g2_rows(s)[ZERO]
 
 
-def share_pieces(s, dw1, dw2, tok=None, vec=None):
-    lo, hi = g1_rows(s)
-    full = pl.ds(ZERO, CH)
-    out = [(dw1.at[q, pl.ds(lo, hi - lo)], pl.ds(q * (hi - lo), hi - lo), full) for q in range(QUART) if lo < hi]
-    at = QUART * (hi - lo)
-    lo, hi = g2_rows(s)
-    if lo < hi:
-        out.append((dw2.at[pl.ds(lo, hi - lo)], pl.ds(at, hi - lo), full))
-    if tok is not None and s == ZERO:
-        out.append((tok, pl.ds(core_rows(s), TROWS), full))
-    if vec is not None and s == NDEV - ONE:
-        out.append((vec, pl.ds(core_rows(s), VROWS), full))
+def chunk_pieces(chunk, core, ds1, ds2, blocks):
+    out = []
+    for k in range(NDEV // TWO):
+        s = TWO * k + core
+        lo, hi = g1_rows(s)
+        n1 = hi - lo
+        q, third = divmod(chunk, CH // NJ)
+        if n1:
+            out.append((ds1.at[pl.ds(lo, n1)], blocks.at[k, pl.ds(q * n1, n1), pl.ds(NJ * third, NJ)]))
+        lo, hi = g2_rows(s)
+        first, last = max(lo, NJ * chunk), min(hi, NJ * chunk + NJ)
+        if first < last:
+            out.append((ds2.at[pl.ds(first - NJ * chunk, last - first)], blocks.at[k, pl.ds(QUART * n1 + first - lo, last - first)]))
     return list(enumerate(out))
 
 
+def extra_pieces(core, tok, vec, blocks):
+    if core == ZERO:
+        return [(tok, blocks.at[ZERO, pl.ds(core_rows(ZERO), TROWS)])]
+    return [(vec, blocks.at[NDEV // TWO - ONE, pl.ds(core_rows(NDEV - ONE), VROWS)])]
+
+
+NJ = TWO_TILES
 NCP = 1024
 HROWS = CH // NDEV
 TROWS, VROWS = 200, SIXTEEN
@@ -424,35 +443,31 @@
 
 def add_into(dst, src, n):
     def one(i, carry):
-        at = pl.ds(pl.multiple_of(i * SIXTEEN, SIXTEEN), SIXTEEN)
+        at = pl.ds(pl.multiple_of(i * ADD, ADD), ADD)
         dst[at, :] = dst[at, :] + src[at, :]
         return carry
-    lax.fori_loop(ZERO, n // SIXTEEN, one, ZERO)
+    lax.fori_loop(ZERO, n // ADD, one, ZERO)
+
+
+ADD = 32
 
 
 class Reduction:
-    def __init__(self, given, red, sums, own, ld, ps, pr, hs, hr, out_sem, free):
-        self.given, self.red, self.sums, self.own, self.free = given, red, sums, own, free
+    def __init__(self, mine, theirs, red, sums, own, ld, hs, hr, out_sem, free):
+        self.mine, self.theirs, self.red, self.sums, self.own, self.free = mine, theirs, red, sums, own, free
         self.n = red.shape[ONE]
-        self.ld, self.ps, self.pr, self.hs, self.hr, self.out_sem = ld, ps, pr, hs, hr, out_sem
+        self.ld, self.hs, self.hr, self.out_sem = ld, hs, hr, out_sem
         self.me = lax.axis_index("fsdp")
         chip = self.me // TWO
         px, py = lax.rem(chip, TWO), chip // TWO
         self.k, self.kx, self.ky = chip, chip + ONE - TWO * px, chip + TWO - FOUR * py
         self.kd = self.kx + TWO - FOUR * py
 
-    def per_core(self, body):
-        for c in range(TWO):
-            @pl.when(lax.rem(self.me, TWO) == c)
-            def _():
-                body(c)
-
-    def load(self, k, c):
-        return [pltpu.make_async_copy(src, self.own.at[k % TWO, rows, lanes_], self.ld.at[k % TWO, i]) for i, (src, rows, lanes_) in share_pieces(TWO * k + c, *self.given)]
-
-    def give(self, k, c):
-        return [pltpu.make_async_remote_copy(src_ref=src, dst_ref=self.sums.at[k, rows, lanes_], send_sem=self.ps.at[k, i], recv_sem=self.pr.at[k, i], device_id=(peer(self.me, ONE),), device_id_type=MESH)
-                for i, (src, rows, lanes_) in share_pieces(TWO * k + c, *self.given)]
+    def load(self, k):
+        return pltpu.make_async_copy(self.mine.at[k], self.own.at[k % TWO], self.ld.at[ZERO, k])
+
+    def load_theirs(self, k):
+        return pltpu.make_async_copy(self.theirs.at[k], self.sums.at[k], self.ld.at[ONE, k])
 
     def hop(self, i, src, dst, rel):
         return pltpu.make_async_remote_copy(src_ref=src, dst_ref=dst, send_sem=self.hs.at[i], recv_sem=self.hr.at[i], device_id=(peer(self.me, rel),), device_id_type=MESH)
@@ -473,63 +488,62 @@
                 self.hop(TWO, self.right(self.sums, self.ky), self.right(self.own, ZERO), FOUR), self.hop(THREE, self.right(self.sums, self.kd), self.right(self.own, ONE), FOUR)]
 
     def begin(self):
+        for k in range(NDEV // TWO):
+            self.load_theirs(k).start()
+        for k in range(TWO):
+            self.load(k).start()
         barrier = pltpu.get_barrier_semaphore()
-        for rel in (ONE, TWO, FOUR):
+        for rel in (TWO, FOUR):
             pl.semaphore_signal(barrier, inc=ONE, device_id=(peer(self.me, rel),), device_id_type=MESH)
-        pl.semaphore_wait(barrier, THREE)
-
-        def body(c):
-            for k in range(FOUR):
-                for copy in self.give(k, ONE - c):
-                    copy.start()
-            for k in range(TWO):
-                for copy in self.load(k, c):
-                    copy.start()
-        self.per_core(body)
-
-    def partner_done(self):
-        for k in range(FOUR):
-            def wait(c):
-                for copy in self.load(k, c):
-                    copy.wait()
-                for copy in self.give(k, c):
-                    copy.wait_recv()
-            self.per_core(wait)
+        pl.semaphore_wait(barrier, TWO)
+    def combine(self):
+        for k in range(NDEV // TWO):
+            self.load(k).wait()
+            self.load_theirs(k).wait()
             add_into(self.sums.at[k], self.own.at[k % TWO], self.n)
             if k < TWO:
-                def more(c):
-                    for copy in self.load(k + TWO, c):
-                        copy.start()
-                self.per_core(more)
+                self.load(k + TWO).start()
         self.ready(ZERO)
         for copy in self.first_hops():
             copy.start()
 
+    def take(self):
+        add_into(self.sums.at[self.k], self.own.at[ZERO], self.n)
+        add_into(self.left(self.sums, self.ky), self.left(self.own, ONE), self.n)
+        add_into(self.right(self.sums, self.kx), self.right(self.own, ONE), self.n)
+
     def first_done(self):
         for copy in self.first_hops():
             copy.wait_recv()
+        self.take()
+        self.ready(ONE)
+        for copy in self.second_hops():
+            copy.start()
+
+    def second_hops(self):
+        return [self.hop(FOUR, self.left(self.sums, self.ky), self.left(self.own, ZERO), FOUR), self.hop(FIVE, self.right(self.sums, self.kx), self.right(self.own, ZERO), TWO)]
+
+    def finish(self):
+        for copy in self.second_hops():
+            copy.wait_recv()
         add_into(self.sums.at[self.k], self.own.at[ZERO], self.n)
-        add_into(self.left(self.sums, self.ky), self.left(self.own, ONE), self.n)
-        add_into(self.right(self.sums, self.kx), self.right(self.own, ONE), self.n)
-        outs = self.outputs()
+        out = pltpu.make_async_copy(self.sums.at[self.k], self.red.at[ZERO], self.out_sem.at[ZERO])
+        out.start()
+        for copy in self.first_hops() + self.second_hops():
+            copy.wait_send()
+        out.wait()
+
+    def hand_over(self):
+        own, left, right = self.red.at[ZERO], self.red.at[ONE, :, pl.ds(ZERO, HALF)], self.red.at[ONE, :, pl.ds(HALF, HALF)]
+        outs = [pltpu.make_async_copy(a, b, self.out_sem.at[i]) for i, (a, b) in enumerate(((self.sums.at[self.k], own), (self.left(self.sums, self.ky), left), (self.right(self.sums, self.kx), right)))]
+        for copy in self.first_hops():
+            copy.wait_recv()
+        self.take()
         for copy in outs:
             copy.start()
-
-    def outputs(self):
-        own, left, right = self.red.at[ZERO], self.red.at[ONE, :, pl.ds(ZERO, HALF)], self.red.at[ONE, :, pl.ds(HALF, HALF)]
-        pairs = (self.sums.at[self.k], own), (self.left(self.sums, self.ky), left), (self.right(self.sums, self.kx), right)
-        return [pltpu.make_async_copy(a, b, self.out_sem.at[i]) for i, (a, b) in enumerate(pairs)]
-
-    def finish(self):
         for copy in self.first_hops():
             copy.wait_send()
-
-        def body(c):
-            for k in range(FOUR):
-                for copy in self.give(k, ONE - c):
-                    copy.wait_send()
-        self.per_core(body)
-        for copy in self.outputs():
+        for copy in outs:
             copy.wait()
 
 
@@ -543,9 +557,7 @@
 
 def reduction_scratch(n):
     dma = pltpu.SemaphoreType.DMA
-    pieces = QUART + TWO
-    return [pltpu.VMEM((FOUR, n, CH), F32), pltpu.VMEM((TWO, n, CH), F32),
-            dma((TWO, pieces)), dma((FOUR, pieces)), dma((FOUR, pieces)), dma((FOUR,)), dma((FOUR,)), dma((THREE,)), pltpu.SemaphoreType.REGULAR((ONE,))]
+    return [pltpu.VMEM((FOUR, n, CH), F32), pltpu.VMEM((TWO, n, CH), F32), dma((TWO, FOUR)), dma((SIX,)), dma((SIX,)), dma((THREE,)), pltpu.SemaphoreType.REGULAR((TWO,))]
 
 
 def untile(block, flat, d):
@@ -632,8 +644,8 @@
 
 
 def finish_kernel(red0, red1, late1, heads, tok_ref, vec_ref, ex_ref, g_out, gh_out, gsm_out, loss_ref,
-                  gs, r0, r1, l0, l1, tsum, tgot, vsum, vgot, ex, nrm, flip, ta, tb, va, vb, hparts,
-                  g_sem, head_sem, red_sem, pair_s, pair_r, own_s, own_r, ex_s, ex_r, nm_s, nm_r, hop_s, hop_r):
+                  gs, r0, r1, l1, tsum, tgot, vsum, vgot, ex, nrm, flip, ta, tb, va, vb, hparts,
+                  g_sem, head_sem, red_sem, pair_s, pair_r, own_s, own_r, ex_s, ex_r, nm_s, nm_r):
     me = lax.axis_index("fsdp")
     core = lax.rem(me, TWO)
     others = [lax.rem(me + i, NDEV) for i in range(ONE, NDEV)]
@@ -672,9 +684,6 @@
                 @pl.when(me == owner ^ rel)
                 def _():
                     to_owner(total, got, rel, owner).start()
-    hops = last_hops(red0, l0, hop_s, hop_r, me)
-    for copy in hops:
-        copy.start()
     for copy in reds:
         copy.wait()
     add_into(r1, l1, r1.shape[ZERO])
@@ -703,6 +712,15 @@
     g_small = ta[pl.ds(THREE * me, THREE), :]
     gsm_out[...] = g_small
     acc = acc + jnp.sum(g_small * g_small, axis=ZERO, keepdims=True) / EIGHT
+    def rest_of(d):
+        untile(r0, gs.at[ZERO], d)
+        if d == ZERO:
+            lay_tokens(r0, core_rows(ZERO), gs.at[ONE], flip, ta, tb)
+        if d == NDEV - ONE:
+            lay_vectors(r0, core_rows(NDEV - ONE), gs.at[ONE], va, vb)
+
+    per_device(rest_of)
+
     for c, owner, give, mine, total, got in sides:
         @pl.when(me == owner)
         def _():
@@ -713,18 +731,6 @@
                 lay_tokens(total, ZERO, gs.at[ZERO], flip, ta, tb)
             else:
                 lay_vectors(total, ZERO, gs.at[ZERO], va, vb)
-    for copy in hops:
-        copy.wait_recv()
-    add_into(r0, l0, r0.shape[ZERO])
-
-    def rest_of(d):
-        untile(r0, gs.at[ZERO], d)
-        if d == ZERO:
-            lay_tokens(r0, core_rows(ZERO), gs.at[ONE], flip, ta, tb)
-        if d == NDEV - ONE:
-            lay_vectors(r0, core_rows(NDEV - ONE), gs.at[ONE], va, vb)
-
-    per_device(rest_of)
     flats = [pltpu.make_async_copy(gs.at[l, pl.ds(MARG, SH)], g_out.at[l], g_sem.at[l]) for l in range(TWO)]
     for copy in flats:
         copy.start()
@@ -752,7 +758,7 @@
         tot = tot + nrm[lax.rem(first + d, NDEV)]
     norm = jnp.sqrt(jnp.sum(jnp.sum(tot, axis=ZERO, keepdims=True), axis=ONE, keepdims=True))
     loss_ref[FOUR:EIGHT, :] = jnp.broadcast_to(1.0 / jnp.maximum(1.0, norm), (FOUR, LANES))
-    for copy in small + norms + hops:
+    for copy in small + norms:
         copy.wait_send()
     for c, owner, give, mine, total, got in sides:
         pl.when(core != c)(give.wait_send)
@@ -771,11 +777,11 @@
         in_specs=[ANY] * FOUR + [VMEM] * THREE,
         out_specs=[ANY] + [VMEM] * THREE,
         out_shape=[sds((TWO, SH, LANES), F32), sds((HROWS, NCLS), F32), sds((THREE, LANES), F32), sds((EIGHT, LANES), F32)],
-        scratch_shapes=[pltpu.VMEM((TWO, GROWS + TWO * MARG, LANES), F32), blk0, blk1, blk0, blk1,
+        scratch_shapes=[pltpu.VMEM((TWO, GROWS + TWO * MARG, LANES), F32), blk0, blk1, blk1,
                         pltpu.VMEM((TROWS, CH), F32), pltpu.VMEM((FOUR, TROWS, CH), F32), pltpu.VMEM((VROWS, CH), F32), pltpu.VMEM((FOUR, VROWS, CH), F32),
                         pltpu.VMEM((NDEV, EXR, LANES), F32), pltpu.VMEM((NDEV, EIGHT, LANES), F32), pltpu.VMEM((TH, TWO_TILES), F32),
                         pltpu.VMEM((TH + EIGHT, LANES), F32), pltpu.VMEM((TH + EIGHT, LANES), F32), pltpu.VMEM((48, LANES), F32), pltpu.VMEM((56, LANES), F32), pltpu.VMEM((NDEV, HROWS, NCP), F32),
-                        dma((TWO,)), dma, dma((THREE,)), dma, dma, dma((THREE,)), dma((THREE,)), dma((NDEV,)), dma((NDEV,)), dma((NDEV,)), dma((NDEV,)), dma((TWO,)), dma((TWO,))],
+                        dma((TWO,)), dma, dma((THREE,)), dma, dma, dma((THREE,)), dma((THREE,)), dma((NDEV,)), dma((NDEV,)), dma((NDEV,)), dma((NDEV,))],
         compiler_params=pltpu.CompilerParams(collective_id=THREE, has_side_effects=True, vmem_limit_bytes=67000000),
         name="finish",
     )(red0, red1, late1, heads, tok, vec, ex)
@@ -886,33 +892,24 @@
 
 def forward_kernel(first, x_ref, wt1_ref, wt2_ref, bt1_ref, bt2_ref, w1_ref, w2_ref, cv_ref, b1_ref, *rest):
     if first:
-        (st1, st2), rest = rest[:TWO], rest[TWO:]
+        rest = rest[FOUR:]
     (x1_ref, ut_ref, hid_ref, h2_ref, x2_ref), rest = rest[:FIVE], rest[FIVE:]
     if first:
         (flat_ref, nw1, nw2, e1, e2), rest = rest[:FIVE], rest[FIVE:]
     (xf, hs, acts), rest = rest[:THREE], rest[THREE:]
     step = pl.program_id(ZERO)
     if first:
-        m1, m2, ed_sem, own_sem, *sems = rest
-
-        def pieces(d):
-            return matrix_moves(d, st1, st2, nw1, nw2, e1, e2)
-
-        job = Spread(pieces, *sems)
-
-        def keep_own(act):
-            def body(d, _):
-                for i, (a, b) in enumerate(pieces(d)):
-                    getattr(pltpu.make_async_copy(a, b, own_sem.at[i]), act)()
-            job.each((ZERO,), body)
+        m1, m2, ed_sem, *sems = rest
+
+        job = Spread(lambda d: [(there, there) for _, there in matrix_moves(d, nw1, nw2, nw1, nw2, e1, e2)], *sems)
 
         @pl.when(step == ZERO)
         def _():
             entry_barrier(job.me)
             job.start()
-            keep_own("start")
-
-        pl.when(step == ROWS // GR - ONE)(functools.partial(job.hand_on, ORDER[:THREE]))
+
+        pl.when(step == ROWS // GR // TWO)(functools.partial(job.hand_on, ORDER[:TWO]))
+        pl.when(step == ROWS // GR - ONE)(functools.partial(job.hand_on, RELS[TWO:]))
     load_group(x_ref, xf)
     if first:
         flat_ref[...] = xf[...].astype(BF16)
@@ -940,7 +937,6 @@
         def _():
             job.arrive()
             job.sent()
-            keep_own("wait")
             merge_edges(nw1, nw2, e1, e2, m1, m2, ed_sem)
 
 
@@ -952,7 +948,7 @@
     return pl.BlockSpec(shape, lambda g: (g,) + (ZERO,) * (len(shape) - ONE))
 
 
-def forward_layer(x, wt1t, wt2t, bt1, bt2, w1, w2, cv, b1, stage=()):
+def forward_layer(x, wt1t, wt2t, bt1, bt2, w1, w2, cv, b1, after=()):
     sds = jax.ShapeDtypeStruct
     first = x.ndim == THREE
     act = by_group((GR, CH))
@@ -960,23 +956,25 @@
     outs = [act, by_group((GROUP, TH, CH)), by_group((GR, HID)), act, act]
     shapes = [act_s, sds((24, TH, CH), F32), sds((ROWS, HID), F32), act_s, act_s]
     scratch = [pltpu.VMEM((GR, CH), F32), pltpu.VMEM((GR, CH), BF16), pltpu.VMEM((GR, HID), BF16)]
-    params = {}
+    params, alias = {}, {}
     if first:
         outs += [act] + [ANY] * FOUR
         shapes += [act_s, sds((CH, HID), BF16), sds((HID, CH), BF16), sds((len(EDGE1), SIXTEEN, HID), BF16), sds((len(EDGE2), SIXTEEN, CH), BF16)]
-        scratch += edge_scratch() + [pltpu.SemaphoreType.DMA((FOUR,))] + spread_sems(FOUR)
+        scratch += edge_scratch() + spread_sems(FOUR)
         params = {"collective_id": FOUR, "has_side_effects": True}
+        alias = {9 + i: SIX + i for i in range(FOUR)}
     return pl.pallas_call(
         functools.partial(forward_kernel, first),
         grid=(ROWS // GR,),
         in_specs=[by_group((GROUP, TOK, CH)) if first else act, once((GROUP, TH, WIN)), once((GROUP, WIN, TH)), once((TH, LANES)), once((GROUP, WIN, LANES)),
-                  once((CH, HID)), once((HID, CH)), once((EIGHT, CH)), once((EIGHT, HID))] + [ANY] * len(stage),
+                  once((CH, HID)), once((HID, CH)), once((EIGHT, CH)), once((EIGHT, HID))] + [ANY] * len(after),
         out_specs=outs,
         out_shape=shapes,
         scratch_shapes=scratch,
+        input_output_aliases=alias,
         compiler_params=pltpu.CompilerParams(vmem_limit_bytes=67000000, **params),
         name="forward_layer",
-    )(x, wt1t, wt2t, bt1, bt2, w1, w2, cv, b1, *stage)
+    )(x, wt1t, wt2t, bt1, bt2, w1, w2, cv, b1, *after)
 
 def fold_rows(a):
     return jnp.sum(a.reshape(a.shape[ZERO] // EIGHT, EIGHT, a.shape[ONE]), axis=ZERO)
@@ -999,33 +997,29 @@
 SUB = 112
 
 
-def backward_kernel(first, dh_ref, d2_ref, x1_ref, x_ref, ut_ref, w1_ref, wt1_ref, wt2_ref, cv_ref, gb1_ref, dw1, dw2, *rest):
-    if first:
-        tok1, vec1, *rest = rest
-        given = dw1, dw2, tok1, vec1
-    else:
+def backward_kernel(first, dh_ref, d2_ref, x1_ref, x_ref, ut_ref, w1_ref, wt1_ref, wt2_ref, cv_ref, gb1_ref, mine, theirs, *rest):
+    if not first:
         dx_ref, *rest = rest
-        given = dw1, dw2
-    tok_ref, vec_ref, red, gt1_ref, gt2_ref, gbt1_ref, gbt2_ref, gcv_ref, d1b, hs, dhf, acts, dus, *comm = rest
+    tok_ref, vec_ref, red, gt1_ref, gt2_ref, gbt1_ref, gbt2_ref, gcv_ref, d1b, hs, dhf, acts0, dus0, acts1, dus1, da0, da1, *comm = rest
+    pair = (acts0, dus0), (acts1, dus1)
+    das = da0, da1
     step = pl.program_id(ZERO)
-    job = Reduction(given, red, *comm)
+    job = Reduction(mine, theirs, red, *comm)
     pl.when(step == ZERO)(job.begin)
-    pl.when(step == TWO)(job.partner_done)
+    if not first:
+        pl.when(step == ONE)(job.combine)
 
     @pl.when(step == ZERO)
     def _():
         for r in (gt1_ref, gt2_ref, gbt1_ref, gbt2_ref, gcv_ref):
             r[...] = jnp.zeros(r.shape, F32)
 
-    def through_w1(c, carry):
-        cols = pl.ds(pl.multiple_of(c * TWO_TILES, TWO_TILES), TWO_TILES)
-        dhf[:, cols] = mm_t(dh_ref[...], w1_ref[cols, :])
-        return carry
-
-    lax.fori_loop(ZERO, CH // TWO_TILES, through_w1, ZERO)
-
-    def norm_two(i, carry):
-        rows = pl.ds(pl.multiple_of(i * SUB, SUB), SUB)
+    half = SUB * GROUP
+    for rows in (slice(ZERO, half), slice(half, GR)):
+        dhf[rows, :] = mm_t(dh_ref[rows, :], w1_ref[...])
+
+    for i in range(GR // SUB):
+        rows = slice(SUB * i, SUB * i + SUB)
         d_n2 = dhf[rows, :].astype(BF16).astype(F32)
         nrm2, rstd2 = norm_stats(x1_ref[rows, :].astype(F32))
         d2 = d2_ref[rows, :].astype(F32)
@@ -1037,24 +1031,38 @@
         nrm1, _ = norm_stats(x_ref[rows, :].astype(F32))
         hs[rows, :] = (nrm1 * cv_ref[ZERO:ONE, :] + cv_ref[ONE:TWO, :]).astype(BF16)
         dhf[rows, :] = jnp.zeros((SUB, CH), F32)
-        return carry
-
-    lax.fori_loop(ZERO, GR // SUB, norm_two, ZERO)
-    def one_image(i, carry):
-        win = pl.ds(pl.multiple_of(192 * i, 192), WIN)
+
+    def window(i):
+        return slice(192 * i, 192 * i + WIN)
+
+    def through_wt2(i):
+        das[i % TWO][...] = mm(wt2_ref[i], d1b[window(i), :]).astype(BF16)
+
+    def through_gelu(i):
+        acts, dus = pair[i % TWO]
         for j in range(ZERO, TH, LANES):
             part = slice(j, j + LANES)
-            d_act = mm(wt2_ref[i, part, :], d1b[win, :]).astype(BF16).astype(F32)
-            act, d_u = gelu_and_grad(ut_ref[i, part, :], d_act)
+            act, d_u = gelu_and_grad(ut_ref[i, part, :], das[i % TWO][part, :].astype(F32))
             gbt1_ref[part, :] += fold_lanes(d_u)
             acts[part, :] = act.astype(BF16)
             dus[part, :] = d_u.astype(BF16)
-        gt2_ref[i] += mm_t(d1b[win, :], acts[...])
-        gt1_ref[i] += mm_t(hs[win, :], dus[...])
-        dhf[win, :] += mm(wt1_ref[i], dus[...])
-        return carry
-
-    lax.fori_loop(ZERO, GROUP, one_image, ZERO)
+
+    def products(i):
+        acts, dus = pair[i % TWO]
+        gt2_ref[i] += mm_t(d1b[window(i), :], acts[...])
+        gt1_ref[i] += mm_t(hs[window(i), :], dus[...])
+        dhf[window(i), :] += mm(wt1_ref[i], dus[...])
+
+    if first:
+        pl.when(step == ZERO)(job.combine)
+        pl.when(step == ROWS // GR - TWO)(job.first_done)
+    for i in range(GROUP + ONE):
+        if i < GROUP:
+            through_wt2(i)
+        if i > ZERO:
+            products(i - ONE)
+        if i < GROUP:
+            through_gelu(i)
 
     def norm_one(i, carry):
         rows = pl.ds(pl.multiple_of(i * SUB, SUB), SUB)
@@ -1081,50 +1089,112 @@
         vec_ref[9:10, ZERO:TH] = jnp.sum(gbt1_ref[...].T, axis=ZERO, keepdims=True)
         per_tok = sum(gbt2_ref[TOK * i:TOK * i + TOK, :] for i in range(ONE, GROUP)) + gbt2_ref[ZERO:TOK, :]
         vec_ref[10:11, ZERO:TOK] = jnp.sum(per_tok.T, axis=ZERO, keepdims=True)
-        job.first_done()
-        job.finish()
-
-
-def backward_layer(dh, d2, x1, x, ut, w1, wt1s, wt2s, cv, gb1, dw1, dw2, extra):
+        if first:
+            job.finish()
+        else:
+            job.hand_over()
+
+
+def backward_layer(dh, d2, x1, x, ut, w1, wt1s, wt2s, cv, gb1, mine, theirs, first):
     sds = jax.ShapeDtypeStruct
-    first = len(extra) == TWO
     act = by_group((GR, CH))
     keep = lambda shape: pl.BlockSpec(shape, lambda g: (ZERO,) * len(shape))
     n = BLK
-    outs, shapes = [keep((TROWS, CH)), keep((VROWS, CH)), ANY], [sds((TROWS, CH), F32), sds((VROWS, CH), F32), sds((TWO, n, CH), F32)]
+    outs, shapes = [keep((TROWS, CH)), keep((VROWS, CH)), ANY], [sds((TROWS, CH), F32), sds((VROWS, CH), F32), sds((ONE if first else TWO, n, CH), F32)]
     if not first:
         outs, shapes = [act] + outs, [sds((ROWS, CH), BF16)] + shapes
     return pl.pallas_call(
         functools.partial(backward_kernel, first),
         grid=(ROWS // GR,),
-        in_specs=[by_group((GR, HID)), act, act, act, by_group((GROUP, TH, CH)), once((CH, HID)), once((GROUP, WIN, TH)), once((GROUP, TH, WIN)), once((EIGHT, CH)), once((EIGHT, HID))] + [ANY] * (TWO + len(extra)),
+        in_specs=[by_group((GR, HID)), act, act, act, by_group((GROUP, TH, CH)), once((CH, HID)), once((GROUP, WIN, TH)), once((GROUP, TH, WIN)), once((EIGHT, CH)), once((EIGHT, HID))] + [ANY] * TWO,
         out_specs=outs,
         out_shape=shapes,
         scratch_shapes=[pltpu.VMEM((GROUP, WIN, TH), F32), pltpu.VMEM((GROUP, WIN, TH), F32), pltpu.VMEM((TH, LANES), F32), pltpu.VMEM((GR, LANES), F32), pltpu.VMEM((FIVE, EIGHT, CH), F32),
-                        pltpu.VMEM((GR, CH), BF16), pltpu.VMEM((GR, CH), BF16), pltpu.VMEM((GR, CH), F32)] + [pltpu.VMEM((TH, CH), BF16)] * TWO + reduction_scratch(n),
+                        pltpu.VMEM((GR, CH), BF16), pltpu.VMEM((GR, CH), BF16), pltpu.VMEM((GR, CH), F32)] + [pltpu.VMEM((TH, CH), BF16)] * SIX + reduction_scratch(n),
         compiler_params=pltpu.CompilerParams(collective_id=ONE if first else TWO, has_side_effects=True, vmem_limit_bytes=67000000),
         name="backward_layer",
-    )(dh, d2, x1, x, ut, w1, wt1s, wt2s, cv, gb1, dw1, dw2, *extra)
+    )(dh, d2, x1, x, ut, w1, wt1s, wt2s, cv, gb1, mine, theirs)
 
 KP = 4864
-NJ = TWO_TILES
-NSUB = SIX
+NSUB = THREE
 STEPS = HID // NJ
 
 
 def channel_back_kernel(late, d2_ref, h2_ref, w2_ref, hid_ref, *rest):
-    give, dh_ref, dw1_ref, dw2_ref, db1_ref, take, st, even, odd, dbs, dwst, own_sem, send, recv = rest
+    if late:
+        tok, vec, red, dh_ref, mine, theirs, db1_ref, take, st, even, odd, dbs, dwst, ds1, ds2, ls, ss, rs, own_sem, send, recv = rest
+    else:
+        head, dh_ref, mine, theirs, db1_ref, heads, st, even, odd, dbs, dwst, ds1, ds2, ls, ss, rs, own_sem, send, recv = rest
     j = pl.program_id(ZERO)
-    sub, part = ROWS // NSUB, TWO * CH // NSUB
+    sub, part = ROWS // NSUB, CH // NSUB
     me = lax.axis_index("fsdp")
+    core, partner = lax.rem(me, TWO), peer(me, ONE)
+
+    def remote(src, dst, s, r, dev):
+        return pltpu.make_async_remote_copy(src_ref=src, dst_ref=dst, send_sem=s, recv_sem=r, device_id=(dev,), device_id_type=MESH)
+
+    def per_core(body):
+        for c in range(TWO):
+            pl.when(core == c)(functools.partial(body, c))
+
+    def kept(chunk, c):
+        p = chunk % TWO
+        return [pltpu.make_async_copy(a, b, ls.at[p, i]) for i, (a, b) in chunk_pieces(chunk, c, ds1.at[p], ds2.at[p], mine)]
+
+    def given(chunk, c):
+        p = chunk % TWO
+        return [remote(a, b, ss.at[p, i], rs.at[chunk, i], partner) for i, (a, b) in chunk_pieces(chunk, c, ds1.at[p], ds2.at[p], theirs)]
+
+    def drain(old, c):
+        for copy in kept(old, c):
+            copy.wait()
+        for copy in given(old, ONE - c):
+            copy.wait_send()
+
+    def leave():
+        for chunk in range(TWO, STEPS):
+            pl.when(j == chunk + ONE)(functools.partial(per_core, functools.partial(drain, chunk - TWO)))
+        slot = lax.rem(j + ONE, TWO)
+        ds1[slot] = dwst[ZERO:CH, :]
+        ds2[slot] = dwst[CH:TWO * CH, :].T
+
+        def start(chunk, c):
+            for copy in given(chunk, ONE - c) + kept(chunk, c):
+                copy.start()
+
+        for chunk in range(STEPS):
+            pl.when(j == chunk + ONE)(functools.partial(per_core, functools.partial(start, chunk)))
+
+        def settle(c):
+            drain(STEPS - TWO, c)
+            drain(STEPS - ONE, c)
+            for old in range(STEPS):
+                for copy in given(old, c):
+                    copy.wait_recv()
+
+        pl.when(j == STEPS)(functools.partial(per_core, settle))
+
+    def side(c, act):
+        if late:
+            (a, b), = extra_pieces(c, tok, vec, mine)
+            (a2, b2), = extra_pieces(ONE - c, tok, vec, theirs)
+            local, sent = pltpu.make_async_copy(a, b, own_sem), remote(a2, b2, send.at[TWO], recv.at[TWO], partner)
+            if act:
+                local.start()
+                sent.start()
+            else:
+                local.wait()
+                sent.wait_send()
+                remote(*extra_pieces(c, tok, vec, theirs)[ZERO], send.at[TWO], recv.at[TWO], partner).wait_recv()
+
+    others = [lax.rem(me + i, NDEV) for i in range(ONE, NDEV)]
     if late:
-        others = [peer(me, rel) for rel in (TWO, FOUR)]
-        hops = last_hops(give, take, send, recv, me)
+        others = [peer(me, rel) for rel in (ONE, TWO, FOUR)]
+        hops = last_hops(red, take, send, recv, me)
     else:
-        others = [lax.rem(me + i, NDEV) for i in range(ONE, NDEV)]
-        mine = lambda d: give.at[pl.ds(pl.multiple_of(HROWS * d, HROWS), HROWS)]
-        hops = [pltpu.make_async_remote_copy(src_ref=mine(d), dst_ref=take.at[me], send_sem=send.at[i], recv_sem=recv.at[i], device_id=(d,), device_id_type=MESH) for i, d in enumerate(others)]
-        own = pltpu.make_async_copy(mine(me), take.at[me], own_sem)
+        rows_for = lambda d: head.at[pl.ds(pl.multiple_of(HROWS * d, HROWS), HROWS)]
+        hops = [remote(rows_for(d), heads.at[me], send.at[i], recv.at[i], d) for i, d in enumerate(others)]
+        own = pltpu.make_async_copy(rows_for(me), heads.at[me], own_sem)
 
     @pl.when(j == ZERO)
     def _():
@@ -1134,7 +1204,9 @@
         pl.semaphore_wait(barrier, len(others))
         for copy in hops:
             copy.start()
-        if not late:
+        if late:
+            per_core(lambda c: side(c, True))
+        else:
             own.start()
 
     @pl.when(j == ZERO)
@@ -1159,13 +1231,9 @@
         return sums + fold_rows(dh)
 
     def weight_part(r, rhs):
-        rows = pl.ds(pl.multiple_of(r * part, part), part)
-        dwst[rows, :] = mm(st[rows, :], rhs[(r * part) // CH])
-
-    def emit():
-        db1_ref[...] = dbs[...]
-        dw1_ref[...] = dwst[ZERO:CH, :]
-        dw2_ref[...] = dwst[CH:TWO * CH, :].T
+        for kind in range(TWO):
+            rows = pl.ds(pl.multiple_of(CH * kind + r * part, part), part)
+            dwst[rows, :] = mm(st[rows, :], rhs[kind])
 
     zero = jnp.zeros((EIGHT, NJ), F32)
 
@@ -1182,7 +1250,7 @@
                 return through_gelu(r, d_act, sums, new)
 
             sums = lax.fori_loop(ZERO, NSUB, both, zero)
-            emit()
+            db1_ref[...] = dbs[...]
             dbs[...] = sums
 
     @pl.when(j == STEPS)
@@ -1192,54 +1260,62 @@
             return carry
 
         lax.fori_loop(ZERO, NSUB, only, ZERO)
-        emit()
+        db1_ref[...] = dbs[...]
+
+    pl.when(j > ZERO)(leave)
+
+    @pl.when(j == STEPS)
+    def _():
         for copy in hops:
             copy.wait()
-        if not late:
+        if late:
+            per_core(lambda c: side(c, False))
+        else:
             own.wait()
 
 
-def channel_back(d2, h2, w2, hid, give, late):
+def channel_back(d2, h2, w2, hid, give):
     sds = jax.ShapeDtypeStruct
+    dma = pltpu.SemaphoreType.DMA
+    late = len(give) > ONE
     cur = lambda j: jnp.minimum(j, STEPS - ONE)
     prev = lambda j: jnp.maximum(j - ONE, ZERO)
-    wide = CH // NJ
-    outs = [pl.BlockSpec((ROWS, NJ), lambda j: (ZERO, cur(j))), pl.BlockSpec((None, CH, NJ), lambda j: (prev(j) // wide, ZERO, lax.rem(prev(j), wide))),
-            pl.BlockSpec((NJ, CH), lambda j: (prev(j), ZERO)), pl.BlockSpec((EIGHT, NJ), lambda j: (ZERO, prev(j)))]
-    shapes = [sds((ROWS, HID), BF16), sds((QUART, CH, CH), F32), sds((HID, CH), F32), sds((EIGHT, HID), F32)]
-    scratch = [pltpu.VMEM((TWO * CH, KP), BF16), pltpu.VMEM((TWO, KP, NJ), BF16), pltpu.VMEM((TWO, KP, NJ), BF16), pltpu.VMEM((EIGHT, NJ), F32), pltpu.VMEM((TWO * CH, NJ), F32)]
+    blocks = sds((NDEV // TWO, BLK, CH), F32)
+    outs = [pl.BlockSpec((ROWS, NJ), lambda j: (ZERO, cur(j))), ANY, ANY, pl.BlockSpec((EIGHT, NJ), lambda j: (ZERO, prev(j)))]
+    shapes = [sds((ROWS, HID), BF16), blocks, blocks, sds((EIGHT, HID), F32)]
     outs.append(ANY)
-    shapes.append(sds(give.shape[ONE:] if late else (NDEV, HROWS, NCP), F32))
-    scratch += [pltpu.SemaphoreType.DMA] + [pltpu.SemaphoreType.DMA((NDEV,))] * TWO
+    shapes.append(sds(give[TWO].shape[ONE:] if late else (NDEV, HROWS, NCP), F32))
     return pl.pallas_call(
         functools.partial(channel_back_kernel, late),
         grid=(STEPS + ONE,),
-        in_specs=[once((ROWS, CH)), once((ROWS, CH)), pl.BlockSpec((NJ, CH), lambda j: (cur(j), ZERO)), pl.BlockSpec((ROWS, NJ), lambda j: (ZERO, cur(j)))] + [ANY],
+        in_specs=[once((ROWS, CH)), once((ROWS, CH)), pl.BlockSpec((NJ, CH), lambda j: (cur(j), ZERO)), pl.BlockSpec((ROWS, NJ), lambda j: (ZERO, cur(j)))] + [ANY] * len(give),
         out_specs=outs,
         out_shape=shapes,
-        scratch_shapes=scratch,
+        scratch_shapes=[pltpu.VMEM((TWO * CH, KP), BF16), pltpu.VMEM((TWO, KP, NJ), BF16), pltpu.VMEM((TWO, KP, NJ), BF16), pltpu.VMEM((EIGHT, NJ), F32), pltpu.VMEM((TWO * CH, NJ), F32),
+                        pltpu.VMEM((TWO, CH, NJ), F32), pltpu.VMEM((TWO, NJ, CH), F32), dma((TWO, EIGHT)), dma((TWO, EIGHT)), dma((STEPS, EIGHT)), dma, dma((NDEV,)), dma((NDEV,))],
         compiler_params=pltpu.CompilerParams(collective_id=FIVE + late, has_side_effects=True, vmem_limit_bytes=67000000),
         name="channel_back",
-    )(d2, h2, w2, hid, give)
+    )(d2, h2, w2, hid, *give)
 
 IMG_PAD = 32
 
 
-def head_kernel(x_ref, lab_ref, hw_ref, fv_ref, hb_ref, d2_ref, ghw_ref, ex_ref, pool, gfv_ref, dl):
+def head_kernel(x_ref, lab_ref, hw_ref, fv_ref, hb_ref, d2_ref, ghw_ref, ex_ref, pool, gfv_ref, dl, nrms, rstds):
     ngroup = ROWS // GR
 
     def image_of_row(shape, dim, g):
         row = lax.broadcasted_iota(jnp.int32, shape, dim)
         return GROUP * g + sum((row >= TOK * i).astype(jnp.int32) for i in range(ONE, GROUP))
 
-    def normed(g):
-        nrm, rstd = norm_stats(x_ref[pl.ds(pl.multiple_of(g * GR, GR), GR), :].astype(F32))
-        return nrm, rstd
+    def rows_of(g):
+        return pl.ds(pl.multiple_of(g * GR, GR), GR)
 
     pool[...] = jnp.zeros(pool.shape, F32)
 
     def pool_one(g, carry):
-        nrm, _ = normed(g)
+        nrm, rstd = norm_stats(x_ref[rows_of(g), :].astype(F32))
+        nrms[rows_of(g), :] = nrm
+        rstds[rows_of(g), :] = rstd
         pick = image_of_row((IMG_PAD, GR), ONE, g) == lax.broadcasted_iota(jnp.int32, (IMG_PAD, GR), ZERO)
         pool[...] += mm(pick.astype(F32).astype(BF16), (nrm * fv_ref[ZERO:ONE, :] + fv_ref[ONE:TWO, :]).astype(BF16))
         return carry
@@ -1263,12 +1339,12 @@
     gfv_ref[...] = jnp.zeros(gfv_ref.shape, F32)
 
     def back_one(g, carry):
-        nrm, rstd = normed(g)
+        nrm, rstd = nrms[rows_of(g), :], rstds[rows_of(g), :]
         pick = image_of_row((GR, IMG_PAD), ZERO, g) == lax.broadcasted_iota(jnp.int32, (GR, IMG_PAD), ONE)
         d_n = mm(pick.astype(F32).astype(BF16), pool[...].astype(BF16))
         gfv_ref[ZERO] += fold_rows(d_n * nrm)
         gfv_ref[ONE] += fold_rows(d_n)
-        d2_ref[pl.ds(pl.multiple_of(g * GR, GR), GR), :] = norm_back(nrm, rstd, fv_ref[ZERO:ONE, :], d_n).astype(BF16)
+        d2_ref[rows_of(g), :] = norm_back(nrm, rstd, fv_ref[ZERO:ONE, :], d_n).astype(BF16)
         return carry
 
     lax.fori_loop(ZERO, ngroup, back_one, ZERO)
@@ -1289,7 +1365,7 @@
         in_specs=[VMEM] * FIVE,
         out_specs=[VMEM] * THREE,
         out_shape=[sds((ROWS, CH), BF16), sds((CH, NCP), F32), sds((EXR, LANES), F32)],
-        scratch_shapes=[pltpu.VMEM((IMG_PAD, CH), F32), pltpu.VMEM((TWO, EIGHT, CH), F32), pltpu.VMEM((IMG_PAD, NCP), F32)],
+        scratch_shapes=[pltpu.VMEM((IMG_PAD, CH), F32), pltpu.VMEM((TWO, EIGHT, CH), F32), pltpu.VMEM((IMG_PAD, NCP), F32), pltpu.VMEM((ROWS, CH), F32), pltpu.VMEM((ROWS, ONE), F32)],
         compiler_params=pltpu.CompilerParams(vmem_limit_bytes=60000000),
         name="head_loss",
     )(x2, lab, head_full, fv, head_b)
@@ -1311,25 +1387,24 @@
 
     def device_step(act_in, labels, layer_p, head_w, small_p, layer_m, head_m, small_m, layer_v, head_v, small_v):
         small8 = jnp.pad(small_p.reshape(THREE, LANES), ((ZERO, FIVE), (ZERO, ZERO)))
-        (w1, w2, st1, st2, head_full), *vectors, (fv, hb) = gather_all(view(layer_p), head_w, small8)
-        x, stage, saved = act_in, (st1, st2), []
+        (w1, w2, nw1, nw2, head_full), edges_, *vectors, (fv, hb) = gather_all(view(layer_p), head_w, small8)
+        x, after, saved = act_in, (nw1, nw2, *edges_), []
         for wt1s, wt2s, wt1t, wt2t, bt1, bt2, cv, b1 in vectors:
-            x1, ut, hid, h2, x2, *more = forward_layer(x, wt1t, wt2t, bt1, bt2, w1, w2, cv, b1, stage)
+            x1, ut, hid, h2, x2, *more = forward_layer(x, wt1t, wt2t, bt1, bt2, w1, w2, cv, b1, after)
             saved.append((more[ZERO] if more else x, x1, ut, hid, h2, w1, w2, wt1s, wt2s, cv))
             if more:
                 w1, w2 = more[ONE:THREE]
-            x, stage = x2, ()
+            x, after = x2, ()
         d2, g_head, ex = head_layer(x, labels, head_full, fv, hb)
-        give, extra, arrived, reds = g_head, (), [], []
-        for x, x1, ut, hid, h2, w1, w2, wt1s, wt2s, cv in reversed(saved):
-            dh, dw1, dw2, gb1, got = channel_back(d2, h2, w2, hid, give, len(arrived) > ZERO)
-            *d_in, g_tok, g_vec, give = backward_layer(dh, d2, x1, x, ut, w1, wt1s, wt2s, cv, gb1, dw1, dw2, extra)
-            arrived.append(got)
-            reds.append(give)
-            extra = g_tok, g_vec
+        give, arrived = (g_head,), []
+        for l, (x, x1, ut, hid, h2, w1, w2, wt1s, wt2s, cv) in reversed(list(enumerate(saved))):
+            dh, mine, theirs, gb1, got = channel_back(d2, h2, w2, hid, give)
+            *d_in, g_tok, g_vec, red = backward_layer(dh, d2, x1, x, ut, w1, wt1s, wt2s, cv, gb1, mine, theirs, l == ZERO)
+            give = g_tok, g_vec, red
+            arrived += [got, red]
             d2 = d_in[ZERO] if d_in else None
-        heads, late = arrived
-        g, g_head, g_small, scalars = finish(reds[ONE], reds[ZERO], late, heads, g_tok, g_vec, ex)
+        heads, red1, late, red0 = arrived
+        g, g_head, g_small, scalars = finish(red0, red1, late, heads, g_tok, g_vec, ex)
         smalls = [a.reshape(THREE, LANES) for a in (small_p, small_m, small_v)]
         outs = update(view(layer_p), view(layer_m), view(layer_v), g, g_head, g_small, scalars, (head_w, head_m, head_v), smalls)
         new_lp, new_lm, new_lv = [unview(a) for a in outs[:THREE]]

time: 827 us -> 772 us (0.933)
  Pallas kernels: 808 us -> 753 us
    pallas_call x1, Pallas kernels: 52.2 us -> 24.3 us  [finish(): pl.pallas_call(finish_kernel, in_specs=[ANY] * FOUR + [VMEM] * THREE, out...]
    pallas_call x2, Pallas kernels: 228 us -> 206 us  [backward_layer(): pl.pallas_call(functools.partial(backward_kernel, first), grid=(ROWS // G...]
    pallas_call x1, Pallas kernels: 85.1 us -> 73.4 us  [gather_all(): pl.pallas_call(gather_kernel, in_specs=[ANY, VMEM, VMEM], out_specs=[ANY]...]
where the time goes in v3:
time: 772 us; the launch traced here: 767 us
  Pallas kernels  753 us (98%)
  local copies, waits for them, and re-layouts  11.3 us (1%)
    pallas_call x2, Pallas kernels, channel_back(): pl.pallas_call(functools.partial(channel_back_kernel, late), grid=(STEPS...  246 us
    pallas_call x2, Pallas kernels, backward_layer(): pl.pallas_call(functools.partial(backward_kernel, first), grid=(ROWS // G...  206 us
    pallas_call x2, Pallas kernels, forward_layer(): pl.pallas_call(functools.partial(forward_kernel, first), grid=(ROWS // GR...  165 us
    pallas_call x1, Pallas kernels, gather_all(): pl.pallas_call(gather_kernel, in_specs=[ANY, VMEM, VMEM], out_specs=[ANY]...  73.4 us
    pallas_call x1, Pallas kernels, finish(): pl.pallas_call(finish_kernel, in_specs=[ANY] * FOUR + [VMEM] * THREE, out...  24.3 us
    pallas_call x1, Pallas kernels, head_layer(): pl.pallas_call(head_kernel, in_specs=[VMEM] * FIVE, out_specs=[VMEM] * TH...  21 us
    pallas_call x1, Pallas kernels, update(): pl.pallas_call(update_kernel, in_specs=[ANY] * FOUR + [VMEM] * 9, out_spe...  16.4 us

profile of v3, /device:TPU:0, one launch (start us, length us, event | category | flops | bytes accessed | tf_op | source)
XLA Modules:
  0.0 766.8 jit_solution(10935635771911717344)
XLA Ops:
  0.6 0.7 pad.9
  1.3 1.3 pad.8.small_ref
  2.6 0.7 broadcast_in_dim.2.lab_ref
  3.3 7.5 copy.25.x_ref
  10.8 73.4 %gather_weights.1 = (bf16[768,3072]{1,0:T(8,128)(2,1)}, bf16[3072,768]{1,0:T(8,128)(2,1)}, bf16[768,3072]{1,0:T(8,128)(2,1)}, bf16[3072,768]{1,0:T(8,128)(2,1)},...) custom-call(f32[4763,2,128]{2,1,0:T(2,128)} %bitcast.25, ...), custom_call_target="tpu_custom_call" | custom-call | tf_op jit(solution)/shard_map/gather_weights/pallas_call | solution.py:379
  84.2 90.9 %forward_layer.2 = (bf16[4704,768]{1,0:T(8,128)(2,1)}, f32[24,384,768]{2,1,0:T(8,128)}, f32[4704,3072]{1,0:T(8,128)}, bf16[4704,768]{1,0:T(8,128)(2,1)}, bf16[47...) custom-call(bf16[24,196,768]{2,1,0:T(8,128)(2,1)} %copy.25.x_ref, ...), custom_call_target="tpu_custom_call", output_to_operand_aliasing={{6}: (9, {}), {7}: (10, {}), {8}: (11, {}), {9}: (12, {})} | custom-call | tf_op jit(solution)/shard_map/forward_layer/pallas_call | solution.py:966
  175.1 74.0 %forward_layer.3 = (bf16[4704,768]{1,0:T(8,128)(2,1)}, f32[24,384,768]{2,1,0:T(8,128)}, f32[4704,3072]{1,0:T(8,128)}, bf16[4704,768]{1,0:T(8,128)(2,1)}, bf16[4704,768]{1,0:T(8,128)(2,1)}) custom-call(bf16[4704,768]{1,0:T(8,128)(2,1)} %get-tuple-element.93.x_ref, bf16[4,384,208]{2,1,0:T(8,128)(2,1)} %get-tuple-element.94.wt1_ref, ...), custom_call_target="tpu_custom_call" | custom-call | tf_op jit(solution)/shard_map/forward_layer/pallas_call | solution.py:966
  249.1 21.0 %head_loss.1 = (bf16[4704,768]{1,0:T(8,128)(2,1)}, f32[768,1024]{1,0:T(8,128)}, f32[32,128]{1,0:T(8,128)}) custom-call(bf16[4704,768]{1,0:T(8,128)(2,1)} %get-tuple-element.102.x_ref, s32[32,128]{1,0:T(8,128)} %broadcast_in_dim.2.lab_ref, bf16[768,1000]{1,0:T(8,128)(2,1)} %get-tuple-element.103.hw_ref, f32[8,768]{1,0:T(8,128)} %get-tuple-element.104.fv_ref, ...), custom_call_target="tpu_custom_call" | custom-call | tf_op jit(solution)/shard_map/head_loss/pallas_call | solution.py:1363
  270.1 123.4 %channel_back.2 = (bf16[4704,3072]{1,0:T(8,128)(2,1)}, f32[4,832,768]{2,1,0:T(8,128)}, f32[4,832,768]{2,1,0:T(8,128)}, f32[8,3072]{1,0:T(8,128)}, f32[8,96,1024]{2,1,0:T(8,128)}) custom-call(bf16[4704,768]{1,0:T(8,128)(2,1)} %get-tuple-element.106.d2_ref, bf16[4704,768]{1,0:T(8,128)(2,1)} %get-tuple-element.107.h2_ref, ...), custom_call_target="tpu_custom_call" | custom-call | tf_op jit(solution)/shard_map/channel_back/pallas_call | solution.py:1288
  393.5 97.8 %backward_layer.2 = (bf16[4704,768]{1,0:T(8,128)(2,1)}, f32[200,768]{1,0:T(8,128)}, f32[16,768]{1,0:T(8,128)}, f32[2,832,768]{2,1,0:T(8,128)}) custom-call(bf16[4704,3072]{1,0:T(8,128)(2,1)} %get-tuple-element.110.dh_ref, bf16[4704,768]{1,0:T(8,128)(2,1)} %get-tuple-element.106.d2_ref, bf16[4704,768]{1,0:T(8,128)(2,1)} %get-tuple-element.111.x1_ref, ...), custom_call_target="tpu_custom_call" | custom-call | tf_op jit(solution)/shard_map/backward_layer/pallas_call | solution.py:1106
  491.3 122.9 %channel_back.3 = (bf16[4704,3072]{1,0:T(8,128)(2,1)}, f32[4,832,768]{2,1,0:T(8,128)}, f32[4,832,768]{2,1,0:T(8,128)}, f32[8,3072]{1,0:T(8,128)}, f32[832,768]{1,0:T(8,128)}) custom-call(bf16[4704,768]{1,0:T(8,128)(2,1)} %get-tuple-element.118.d2_ref, bf16[4704,768]{1,0:T(8,128)(2,1)} %get-tuple-element.119.h2_ref, ...), custom_call_target="tpu_custom_call" | custom-call | tf_op jit(solution)/shard_map/channel_back/pallas_call | solution.py:1288
  614.2 108.7 %backward_layer.3 = (f32[200,768]{1,0:T(8,128)}, f32[16,768]{1,0:T(8,128)}, f32[1,832,768]{2,1,0:T(8,128)}) custom-call(bf16[4704,3072]{1,0:T(8,128)(2,1)} %get-tuple-element.124.dh_ref, bf16[4704,768]{1,0:T(8,128)(2,1)} %get-tuple-element.118.d2_ref, bf16[4704,768]{1,0:T(8,128)(2,1)} %get-tuple-element.125.x1_ref, ...), custom_call_target="tpu_custom_call" | custom-call | tf_op jit(solution)/shard_map/backward_layer/pallas_call | solution.py:1106
  722.9 24.3 %finish.1 = (f32[2,4763,128]{2,1,0:T(8,128)}, f32[96,1000]{1,0:T(8,128)}, f32[3,128]{1,0:T(4,128)}, f32[8,128]{1,0:T(8,128)}) custom-call(f32[1,832,768]{2,1,0:T(8,128)} %get-tuple-element.133.red0, f32[2,832,768]{2,1,0:T(8,128)} %get-tuple-element.123.rest_2_.red1, f32[832,768]{1,0:T(8,128)} %get-tuple-element.134.late1, ...), custom_call_target="tpu_custom_call" | custom-call | tf_op jit(solution)/shard_map/finish/pallas_call | solution.py:775
  747.2 1.2 slice.3
  749.1 16.4 %update.1 = (f32[4763,2,128]{2,1,0:T(2,128)}, f32[4763,2,128]{2,1,0:T(2,128)}, f32[4763,2,128]{2,1,0:T(2,128)}, f32[96,1000]{1,0:T(8,128)}, f32[96,1000]{1,0:T(8...) custom-call(f32[4763,2,128]{2,1,0:T(2,128)} %bitcast.26, ...), custom_call_target="tpu_custom_call" | custom-call | tf_op jit(solution)/shard_map/update/pallas_call | solution.py:837

commit v4 on v3

--- a/solution.py
+++ b/solution.py
@@ -586,8 +586,8 @@
 
 
 NVIEW = 40
-CHUNK = 1200
-NCHUNK = FOUR
+CHUNK = 600
+NCHUNK = EIGHT
 GROWS = CHUNK * NCHUNK
 EXR = 32
 LOSS_ROW = 24

time: 772 us -> 771 us (level)
  no operation moved by 1% of the time
where the time goes in v4:
time: 771 us; the launch traced here: 766 us
  Pallas kernels  752 us (98%)
  local copies, waits for them, and re-layouts  11.3 us (1%)
    pallas_call x2, Pallas kernels, channel_back(): pl.pallas_call(functools.partial(channel_back_kernel, late), grid=(STEPS...  246 us
    pallas_call x2, Pallas kernels, backward_layer(): pl.pallas_call(functools.partial(backward_kernel, first), grid=(ROWS // G...  206 us
    pallas_call x2, Pallas kernels, forward_layer(): pl.pallas_call(functools.partial(forward_kernel, first), grid=(ROWS // GR...  165 us
    pallas_call x1, Pallas kernels, gather_all(): pl.pallas_call(gather_kernel, in_specs=[ANY, VMEM, VMEM], out_specs=[ANY]...  73.4 us
    pallas_call x1, Pallas kernels, finish(): pl.pallas_call(finish_kernel, in_specs=[ANY] * FOUR + [VMEM] * THREE, out...  24.3 us
    pallas_call x1, Pallas kernels, head_layer(): pl.pallas_call(head_kernel, in_specs=[VMEM] * FIVE, out_specs=[VMEM] * TH...  21 us
    pallas_call x1, Pallas kernels, update(): pl.pallas_call(update_kernel, in_specs=[ANY] * FOUR + [VMEM] * 9, out_spe...  15.8 us

profile of v4, /device:TPU:0, one launch (start us, length us, event | category | flops | bytes accessed | tf_op | source)
XLA Modules:
  0.0 766.1 jit_solution(2807576087396071644)
XLA Ops:
  0.6 0.7 pad.9
  1.3 1.3 pad.8.small_ref
  2.6 0.7 broadcast_in_dim.2.lab_ref
  3.3 7.5 copy.25.x_ref
  10.8 73.4 %gather_weights.1 = (bf16[768,3072]{1,0:T(8,128)(2,1)}, bf16[3072,768]{1,0:T(8,128)(2,1)}, bf16[768,3072]{1,0:T(8,128)(2,1)}, bf16[3072,768]{1,0:T(8,128)(2,1)},...) custom-call(f32[4763,2,128]{2,1,0:T(2,128)} %bitcast.25, ...), custom_call_target="tpu_custom_call" | custom-call | tf_op jit(solution)/shard_map/gather_weights/pallas_call | solution.py:379
  84.2 90.9 %forward_layer.2 = (bf16[4704,768]{1,0:T(8,128)(2,1)}, f32[24,384,768]{2,1,0:T(8,128)}, f32[4704,3072]{1,0:T(8,128)}, bf16[4704,768]{1,0:T(8,128)(2,1)}, bf16[47...) custom-call(bf16[24,196,768]{2,1,0:T(8,128)(2,1)} %copy.25.x_ref, ...), custom_call_target="tpu_custom_call", output_to_operand_aliasing={{6}: (9, {}), {7}: (10, {}), {8}: (11, {}), {9}: (12, {})} | custom-call | tf_op jit(solution)/shard_map/forward_layer/pallas_call | solution.py:966
  175.1 74.0 %forward_layer.3 = (bf16[4704,768]{1,0:T(8,128)(2,1)}, f32[24,384,768]{2,1,0:T(8,128)}, f32[4704,3072]{1,0:T(8,128)}, bf16[4704,768]{1,0:T(8,128)(2,1)}, bf16[4704,768]{1,0:T(8,128)(2,1)}) custom-call(bf16[4704,768]{1,0:T(8,128)(2,1)} %get-tuple-element.93.x_ref, bf16[4,384,208]{2,1,0:T(8,128)(2,1)} %get-tuple-element.94.wt1_ref, ...), custom_call_target="tpu_custom_call" | custom-call | tf_op jit(solution)/shard_map/forward_layer/pallas_call | solution.py:966
  249.1 21.0 %head_loss.1 = (bf16[4704,768]{1,0:T(8,128)(2,1)}, f32[768,1024]{1,0:T(8,128)}, f32[32,128]{1,0:T(8,128)}) custom-call(bf16[4704,768]{1,0:T(8,128)(2,1)} %get-tuple-element.102.x_ref, s32[32,128]{1,0:T(8,128)} %broadcast_in_dim.2.lab_ref, bf16[768,1000]{1,0:T(8,128)(2,1)} %get-tuple-element.103.hw_ref, f32[8,768]{1,0:T(8,128)} %get-tuple-element.104.fv_ref, ...), custom_call_target="tpu_custom_call" | custom-call | tf_op jit(solution)/shard_map/head_loss/pallas_call | solution.py:1363
  270.1 123.4 %channel_back.2 = (bf16[4704,3072]{1,0:T(8,128)(2,1)}, f32[4,832,768]{2,1,0:T(8,128)}, f32[4,832,768]{2,1,0:T(8,128)}, f32[8,3072]{1,0:T(8,128)}, f32[8,96,1024]{2,1,0:T(8,128)}) custom-call(bf16[4704,768]{1,0:T(8,128)(2,1)} %get-tuple-element.106.d2_ref, bf16[4704,768]{1,0:T(8,128)(2,1)} %get-tuple-element.107.h2_ref, ...), custom_call_target="tpu_custom_call" | custom-call | tf_op jit(solution)/shard_map/channel_back/pallas_call | solution.py:1288
  393.5 97.8 %backward_layer.2 = (bf16[4704,768]{1,0:T(8,128)(2,1)}, f32[200,768]{1,0:T(8,128)}, f32[16,768]{1,0:T(8,128)}, f32[2,832,768]{2,1,0:T(8,128)}) custom-call(bf16[4704,3072]{1,0:T(8,128)(2,1)} %get-tuple-element.110.dh_ref, bf16[4704,768]{1,0:T(8,128)(2,1)} %get-tuple-element.106.d2_ref, bf16[4704,768]{1,0:T(8,128)(2,1)} %get-tuple-element.111.x1_ref, ...), custom_call_target="tpu_custom_call" | custom-call | tf_op jit(solution)/shard_map/backward_layer/pallas_call | solution.py:1106
  491.3 122.9 %channel_back.3 = (bf16[4704,3072]{1,0:T(8,128)(2,1)}, f32[4,832,768]{2,1,0:T(8,128)}, f32[4,832,768]{2,1,0:T(8,128)}, f32[8,3072]{1,0:T(8,128)}, f32[832,768]{1,0:T(8,128)}) custom-call(bf16[4704,768]{1,0:T(8,128)(2,1)} %get-tuple-element.118.d2_ref, bf16[4704,768]{1,0:T(8,128)(2,1)} %get-tuple-element.119.h2_ref, ...), custom_call_target="tpu_custom_call" | custom-call | tf_op jit(solution)/shard_map/channel_back/pallas_call | solution.py:1288
  614.2 108.7 %backward_layer.3 = (f32[200,768]{1,0:T(8,128)}, f32[16,768]{1,0:T(8,128)}, f32[1,832,768]{2,1,0:T(8,128)}) custom-call(bf16[4704,3072]{1,0:T(8,128)(2,1)} %get-tuple-element.124.dh_ref, bf16[4704,768]{1,0:T(8,128)(2,1)} %get-tuple-element.118.d2_ref, bf16[4704,768]{1,0:T(8,128)(2,1)} %get-tuple-element.125.x1_ref, ...), custom_call_target="tpu_custom_call" | custom-call | tf_op jit(solution)/shard_map/backward_layer/pallas_call | solution.py:1106
  722.9 24.3 %finish.1 = (f32[2,4763,128]{2,1,0:T(8,128)}, f32[96,1000]{1,0:T(8,128)}, f32[3,128]{1,0:T(4,128)}, f32[8,128]{1,0:T(8,128)}) custom-call(f32[1,832,768]{2,1,0:T(8,128)} %get-tuple-element.133.red0, f32[2,832,768]{2,1,0:T(8,128)} %get-tuple-element.123.rest_2_.red1, f32[832,768]{1,0:T(8,128)} %get-tuple-element.134.late1, ...), custom_call_target="tpu_custom_call" | custom-call | tf_op jit(solution)/shard_map/finish/pallas_call | solution.py:775
  747.2 1.2 slice.3
  749.1 15.8 %update.1 = (f32[4763,2,128]{2,1,0:T(2,128)}, f32[4763,2,128]{2,1,0:T(2,128)}, f32[4763,2,128]{2,1,0:T(2,128)}, f32[96,1000]{1,0:T(8,128)}, f32[96,1000]{1,0:T(8...) custom-call(f32[4763,2,128]{2,1,0:T(2,128)} %bitcast.26, ...), custom_call_target="tpu_custom_call" | custom-call | tf_op jit(solution)/shard_map/update/pallas_call | solution.py:837
